TPU v7x, 256 devices: a whole 4x4x8 slice. The times are simulated.
256 devices in a mesh: dp: 64 (over z, y, core), mp: 4 (over x).
Axes of the slice: x: 4, y: 4, z: 8, core: 2. Of those that a mesh axis runs over, the one named last changes fastest.
Arguments:
- tokens: bfloat16 [393216, 512], P('dp'), may hold values from -6 to 6
- w_uvqk: bfloat16 [512, 2048], P(None, 'mp')
- w_out: bfloat16 [512, 512], replicated, may hold values from -0.25 to 0.25
- hist_len: int32 [64, 24], P('dp'), may hold values from 64 to 256, as said below
- owner: int32 [64, 24], P('dp'), may hold values from 0 to 63, as said below
- recv_offset: int32 [64, 24], P('dp'), may hold values from 0 to 47, as said below
- block_start: int32 [64, 24], P('dp'), may hold values from 0 to 47, as said below
Outputs:
- packed_out: bfloat16 [393216, 512], P('dp', 'mp')
- user_state: bfloat16 [1536, 512], P('dp', 'mp')
Inputs may be any that keep to these rules, and one draw needn't show every extreme that they name: User (d, u) has ceil(hist_len / 128) blocks, at most 2. owner[d, u] = (p(d) + r(u mod 64)) mod 64 for two permutations p, r of the indices of dp drawn from the seed: every owner receives exactly 24 users, and one device sends at most 1 users to one owner. On some owner every received user has 2 blocks. `recv_offset`: the users of one owner occupy disjoint runs of its 48 blocks, in the order of u; on some owner they fill all 48 blocks. `block_start`: the users of one device occupy disjoint runs of its 48 blocks, in the order of u.
All inputs are finite; a program needn't handle non-finite values.
Results may differ from a plain program's by a relative error of at most 0.0059.
Values may be sent and summed in bfloat16 or wider, within the bound.
No kernel may reach another device: no remote copies, remote signals or barrier semaphores. Data moves between devices by JAX's collectives and lax.ppermute only.
A program may use at most 128 MiB of HBM per device.

v0:
```python
import jax
import jax.numpy as jnp
from jax import lax
from jax.sharding import PartitionSpec as P

D = 512
HEADS = 4
BLOCK = 128
MAXB = 2
BLK_DEV = 48


EPS = 1e-05


def sent_to_all(shard, axis):
    count = lax.axis_size(axis)
    return lax.all_to_all(
        jnp.broadcast_to(shard[None], (count, *shard.shape)), axis, 0, 0, tiled=True
    )


def over_copies(shard, axis):
    everything = sent_to_all(shard, axis)
    return jnp.sum(everything, axis=0)


def together(arrays, axis):
    ends = [0]
    for a in arrays:
        ends.append(ends[-1] + a.size)
    subtotal = over_copies(jnp.concatenate([a.ravel() for a in arrays]), axis)
    return tuple((subtotal[b:e].reshape(a.shape) for a, b, e in zip(arrays, ends, ends[1:])))


def in_one_piece(arrays, axis, dim, along):
    widths = [a.shape[along] for a in arrays]
    both = jnp.concatenate(arrays, axis=along)
    result = lax.all_gather(both, axis, axis=dim, tiled=True)
    return tuple(jnp.split(result, [sum(widths[:k]) for k in range(1, len(widths))], axis=along))


def norm_rows(values):
    average = jnp.mean(values, axis=-1, keepdims=True)
    variance = jnp.mean(values * values, axis=-1, keepdims=True) - average * average
    return (values - average) * lax.rsqrt(variance + EPS)


def attend(query, keys, values, query_user, key_user):
    row_count, head_size = query.shape
    tile_rows = 4 * BLOCK
    back_rows = (MAXB - 1) * BLOCK
    scaling = (D // HEADS) ** (-0.5)
    keys_ext = jnp.concatenate([jnp.zeros((back_rows, head_size), keys.dtype), keys], 0)
    values_ext = jnp.concatenate([jnp.zeros((back_rows, head_size), values.dtype), values], 0)
    users_ext = jnp.concatenate([jnp.full((back_rows,), -2, jnp.int32), key_user], 0)
    query_pos = jnp.arange(tile_rows, dtype=jnp.int32)[:, None] + back_rows
    key_pos = jnp.arange(tile_rows + back_rows, dtype=jnp.int32)[None, :]

    def one_tile(start):
        query_tile = lax.dynamic_slice_in_dim(query, start, tile_rows, 0)
        key_tile = lax.dynamic_slice_in_dim(keys_ext, start, tile_rows + back_rows, 0)
        value_tile = lax.dynamic_slice_in_dim(values_ext, start, tile_rows + back_rows, 0)
        query_owner = lax.dynamic_slice_in_dim(query_user, start, tile_rows, 0)
        key_owner = lax.dynamic_slice_in_dim(users_ext, start, tile_rows + back_rows, 0)
        raw_scores = (
            lax.dot_general(
                query_tile, key_tile, (((1,), (1,)), ((), ())), preferred_element_type=jnp.float32
            )
            * scaling
        )
        allowed = (query_owner[:, None] == key_owner[None, :]) & (key_pos <= query_pos)
        weights = jnp.where(allowed, jax.nn.silu(raw_scores) / (MAXB * BLOCK), 0.0).astype(
            jnp.bfloat16
        )
        return jnp.dot(weights, value_tile, preferred_element_type=jnp.float32)

    tile_starts = jnp.arange(row_count // tile_rows, dtype=jnp.int32) * tile_rows
    return lax.map(one_tile, tile_starts).reshape(row_count, head_size)


def layer_rows(rows_in, query_user, key_user, w_uvqk, w_out):
    row_count = rows_in.shape[0]
    head_size = D // HEADS
    mp_size = lax.axis_size("mp")
    portion = lax.axis_index("mp")
    quarter = D // mp_size
    local_heads = w_uvqk.shape[1] // (4 * head_size)
    widened = rows_in.astype(jnp.float32)
    normed = norm_rows(widened).astype(jnp.bfloat16)
    projected = jax.nn.silu(jnp.dot(normed, w_uvqk, preferred_element_type=jnp.float32)).astype(
        jnp.bfloat16
    )
    pieces = projected.reshape(row_count, local_heads, 4, head_size)
    outputs = attend(pieces[:, 0, 2], pieces[:, 0, 3], pieces[:, 0, 1], query_user, key_user)
    totals = together((jnp.sum(outputs, 1), jnp.sum(outputs * outputs, 1)), "mp")
    average = totals[0] / D
    variance = totals[1] / D - average * average
    gates = pieces[:, :, 0].reshape(row_count, local_heads * head_size).astype(jnp.float32)
    gated_rows = ((outputs - average[:, None]) * lax.rsqrt(variance + EPS)[:, None] * gates).astype(
        jnp.bfloat16
    )
    every_head = lax.all_gather(gated_rows, "mp", axis=1, tiled=True)
    out_columns = lax.dynamic_slice_in_dim(w_out, portion * quarter, quarter, 1)
    mixed_rows = jnp.dot(every_head, out_columns, preferred_element_type=jnp.float32)
    residual = lax.dynamic_slice_in_dim(widened, portion * quarter, quarter, 1)
    return (mixed_rows + residual).astype(jnp.bfloat16)


def row_labels(block_user, block_fill):
    in_block = jnp.arange(BLOCK, dtype=jnp.int32)[None, :]
    row_live = (in_block < block_fill[:, None]).reshape(-1)
    row_user = jnp.broadcast_to(block_user[:, None], (block_user.shape[0], BLOCK)).reshape(-1)
    return (row_live, jnp.where(row_live, row_user, -3), jnp.where(row_live, row_user, -2))


def per_device(tokens, w_uvqk, w_out, hist_len, owner, recv_offset, block_start):
    dp_size = lax.axis_size("dp")
    mp_size = lax.axis_size("mp")
    myself = lax.axis_index("dp")
    user_count = hist_len.shape[1]
    per_pair = -(-user_count // dp_size)
    pair_cap = per_pair * MAXB
    quarter = D // mp_size
    lengths = hist_len[0]
    owners = owner[0]
    starts = block_start[0]
    counts = (lengths + BLOCK - 1) // BLOCK
    user_ids = jnp.arange(user_count, dtype=jnp.int32)
    earlier = user_ids[None, :] < user_ids[:, None]
    same_owner = (owners[:, None] == owners[None, :]) & earlier
    in_pair = jnp.sum(jnp.where(same_owner, counts[None, :], 0), axis=1)
    slot_ids = jnp.arange(pair_cap, dtype=jnp.int32)
    device_ids = jnp.arange(dp_size, dtype=jnp.int32)
    slot_step = slot_ids[None, :, None] - in_pair[None, None, :]
    sending = (
        (owners[None, None, :] == device_ids[:, None, None])
        & (slot_step >= 0)
        & (slot_step < counts[None, None, :])
    )
    send_block = jnp.sum(jnp.where(sending, starts[None, None, :] + slot_step, 0), axis=2)
    all_len, all_owner, all_offset = in_one_piece((hist_len, owner, recv_offset), "dp", 0, 1)
    all_counts = (all_len + BLOCK - 1) // BLOCK
    all_before = (all_owner[:, :, None] == all_owner[:, None, :]) & earlier[None]
    all_in_pair = jnp.sum(jnp.where(all_before, all_counts[:, None, :], 0), axis=2)
    owned = all_owner == myself
    flat_owned = owned.reshape(-1)
    flat_len = all_len.reshape(-1)
    flat_offset = all_offset.reshape(-1)
    flat_counts = all_counts.reshape(-1)
    flat_in_pair = all_in_pair.reshape(-1)
    candidate_ids = jnp.arange(dp_size * user_count, dtype=jnp.int32)
    source_ids = candidate_ids // user_count
    block_ids = jnp.arange(BLK_DEV, dtype=jnp.int32)
    land_step = block_ids[:, None] - flat_offset[None, :]
    landed = flat_owned[None, :] & (land_step >= 0) & (land_step < flat_counts[None, :])
    slot_index = jnp.sum(
        jnp.where(landed, source_ids[None, :] * pair_cap + flat_in_pair[None, :] + land_step, 0),
        axis=1,
    )
    owned_user = jnp.sum(jnp.where(landed, candidate_ids[None, :], 0), axis=1)
    owned_fill = jnp.sum(
        jnp.where(landed, jnp.clip(flat_len[None, :] - land_step * BLOCK, 0, BLOCK), 0), axis=1
    )
    owned_live, owned_query, owned_key = row_labels(owned_user, owned_fill)
    local_step = block_ids[:, None] - starts[None, :]
    within = (local_step >= 0) & (local_step < counts[None, :])
    local_user = jnp.sum(jnp.where(within, user_ids[None, :], 0), axis=1)
    local_fill = jnp.sum(
        jnp.where(within, jnp.clip(lengths[None, :] - local_step * BLOCK, 0, BLOCK), 0), axis=1
    )
    local_live, local_query, local_key = row_labels(local_user, local_fill)
    results = layer_rows(tokens, local_query, local_key, w_uvqk, w_out)
    state = jnp.take(results, starts * BLOCK + lengths - 1, axis=0)
    outgoing = jnp.take(results.reshape(BLK_DEV, BLOCK, quarter), send_block, axis=0)
    arrived = lax.all_to_all(outgoing, "dp", split_axis=0, concat_axis=0, tiled=True)
    gathered = jnp.take(
        arrived.reshape(dp_size * pair_cap, BLOCK, quarter), slot_index, axis=0
    ).reshape(BLK_DEV * BLOCK, quarter)
    packed = jnp.where(owned_live[:, None], gathered, jnp.zeros_like(gathered))
    return (packed, state)


def solution(mesh):
    in_specs = (
        P("dp", None),
        P(None, "mp"),
        P(),
        P("dp", None),
        P("dp", None),
        P("dp", None),
        P("dp", None),
    )
    out_specs = (P("dp", "mp"), P("dp", "mp"))
    return jax.shard_map(
        per_device, mesh=mesh, in_specs=in_specs, out_specs=out_specs, check_vma=False
    )
```

profile of v0, /device:TPU:1, one launch (start us, length us, event | category | flops | bytes accessed | tf_op | source)
XLA Modules:
  0.0 370.8 jit_solution(17628559279992237693)
XLA Ops:
  7.2 4.8 %convert_reduce_fusion = (f32[6144]{0:T(1024)S(1)}, f32[6144]{0:T(1024)S(1)}) fusion(bf16[6144,512]{1,0:T(8,128)(2,1)} %param.9), kind=kLoop, calls=%fused_computation.31 | loop fusion | flops 12570624 | bytes 6340608 | tf_op jit(solution)/shard_map/reduce_sum | solution.py:44
  12.0 8.0 %multiply_convert_fusion = bf16[6144,512]{0,1:T(8,128)(2,1)S(1)} fusion(bf16[512,512]{1,0:T(8,128)(2,1)S(1)} %copy-done, bf16[6144,512]{1,0:T(8,128)(2,1)S(1)} %copy-done.2, f32[6144]{0:T(1024)S(1)} %get-tuple-element.108, f32[6144]{0:T(1024)S(1)} %get-tuple-element.107), kind=kOutput, calls=%fused_computation.28 | convolution fusion | flops 3249537024 | bytes 13156352 | tf_op jit(solution)/shard_map/dot_general | solution.py:91
  20.0 2.3 fusion.59
  22.3 1.3 copy-done.3
  23.7 2.6 copy.50
  26.3 2.6 copy.51
  28.9 2.8 concatenate.17
  31.7 1.3 concatenate.18
  33.0 1.6 copy.49
  34.7 78.6 %while.11 = (s32[]{:T(128)}, f32[12,512,128]{2,1,0:T(8,128)}, s32[12]{0:T(128)S(1)}, s32[6144]{0:T(1024)S(1)}, s32[6272]{0:T(1024)S(1)}, /*index=5*/bf16[6144,12...) while((s32[]{:T(128)}, f32[12,512,128]{2,1,0:T(8,128)}, ...), condition=%wide.region_10.11_spmd.clone, body=%wide.region_9.10_spmd.clone.sunk | while | flops 171377152 | bytes 741060 | solution.py:79
  34.8 0.6 dynamic_slice.53
  38.7 2.6 fusion.70
  41.3 0.6 dynamic_slice.53
  45.3 2.6 fusion.70
  47.9 0.6 dynamic_slice.53
  51.8 2.6 fusion.70
  54.4 0.6 dynamic_slice.53
  58.4 2.6 fusion.70
  61.0 0.6 dynamic_slice.53
  64.9 2.6 fusion.70
  67.5 0.6 dynamic_slice.53
  71.5 2.6 fusion.70
  74.1 0.6 dynamic_slice.53
  78.0 2.6 fusion.70
  80.6 0.6 dynamic_slice.53
  84.5 2.6 fusion.70
  87.2 0.6 dynamic_slice.53
  91.1 2.6 fusion.70
  93.7 0.6 dynamic_slice.53
  97.7 2.6 fusion.70
  104.2 2.6 fusion.70
  110.8 2.6 fusion.70
  113.4 3.6 fusion.58
  117.0 0.8 broadcast_in_dim.174
  117.8 4.8 %all-to-all-start = ((f32[4,1,12288]{2,1,0:T(1,128)}), f32[4,1,12288]{2,1,0:T(1,128)S(1)}, u32[]{:S(2)}, u32[]{:S(2)}) async-start(f32[4,1,12288]{2,1,0:T(1,128)} %broadcast_in_dim.174), calls=%async_computation | async-start | bytes 393216 | tf_op jit(solution)/shard_map/all_to_all | solution.py:18
  122.6 3.5 copy.46
  126.2 1.6 all-to-all-done
  128.0 4.0 %fusion.30 = bf16[6144,128]{0,1:T(8,128)(2,1)} fusion(f32[6144,128]{0,1:T(8,128)} %copy.46, bf16[6144,1,4,128]{0,3,2,1:T(8,128)(2,1)} %bitcast.68, f32[6144]{0:T(1024)S(1)} %get-tuple-element.102, f32[6144]{0:T(1024)S(1)} %get-tuple-element.101), kind=kLoop, calls=%fused_computation.39 | loop fusion | flops 3932160 | bytes 6340608 | tf_op jit(solution)/shard_map/convert_element_type | solution.py:100
  132.0 9.2 %convert_element_type.24 = f32[6144,512]{1,0:T(8,128)} convert(bf16[6144,512]{1,0:T(8,128)(2,1)} %param.9) | non-fusion elementwise | flops 3145728 | bytes 18874368 | tf_op jit(solution)/shard_map/convert_element_type | solution.py:89
  142.0 60.7 %all-gather.3.cloned.1.call-done = bf16[6144,512]{0,1:T(8,128)(2,1)} async-done(((bf16[6144,128]{0,1:T(8,128)(2,1)}), bf16[6144,512]{0,1:T(8,128)(2,1)}) %all-gather.3.cloned.1.call-update) | async-done | bytes 6291472 | tf_op jit(solution)/shard_map/all_gather | solution.py:103
  202.7 5.6 %fusion.26 = bf16[6144,128]{1,0:T(8,128)(2,1)S(1)} fusion(bf16[6144,512]{0,1:T(8,128)(2,1)} %all-gather.3.cloned.1.call-done, f32[6144,512]{1,0:T(8,128)} %convert_element_type.24, s32[]{:T(128)S(6)} %select_n.164, bf16[512,512]{1,0:T(8,128)(2,1)} %param.11), kind=kOutput, calls=%fused_computation.33 | convolution fusion | flops 806879232 | bytes 11142144 | tf_op jit(solution)/shard_map/dot_general | solution.py:105
  208.4 3.1 gather_fusion
  211.4 4.6 %broadcast_select_fusion = bf16[64,2,128,128]{3,2,1,0:T(8,128)(2,1)} fusion(bf16[64,2,128,128]{3,2,1,0:T(8,128)(2,1)} %bitcast.65, pred[64,2]{1,0:T(8,128)(4,1)S(1)} %copy.41), kind=kLoop, calls=%fused_computation.37 | loop fusion | flops 2097152 | bytes 8388736 | tf_op jit(solution)/shard_map/jit(_take)/select_n | solution.py:175
  216.0 11.2 %all-to-all-start.1 = ((bf16[64,2,128,128]{3,2,1,0:T(8,128)(2,1)}), bf16[64,2,128,128]{3,2,1,0:T(8,128)(2,1)}, u32[]{:S(2)}, u32[]{:S(2)}) async-start(bf16[64,2,128,128]{3,2,1,0:T(8,128)(2,1)} %broadcast_select_fusion), calls=%async_computation.1 | async-start | bytes 8388608 | tf_op jit(solution)/shard_map/all_to_all | solution.py:176
  227.3 125.6 %all-gather = s32[64,1,72]{2,1,0:T(1,128)S(1)} all-gather(s32[1,1,72]{2,1,0:T(1,128)S(1)} %add_bitcast_fusion), channel_id=1, replica_groups=mesh['dp'=64,'mp'=4] {'dp'}, dimensions={0}, use_global_device_ids=true | all-gather | bytes 18720 | tf_op jit(solution)/shard_map/all_gather | solution.py:39
  355.0 0.7 broadcast_select_fusion.1
  355.6 3.1 gather_fusion.1
  358.7 5.2 %fusion.31 = bf16[6144,128]{1,0:T(8,128)(2,1)} fusion(bf16[48,128,128]{2,1,0:T(8,128)(2,1)S(1)} %gather_fusion.1, pred[6144]{0:T(1024)(128)(4,1)S(1)} %get-tuple-element.114, pred[6144]{0:T(1024)(128)(4,1)S(1)} %get-tuple-element.113), kind=kLoop, calls=%fused_computation.43 | loop fusion | flops 1572864 | bytes 3158016 | tf_op jit(solution)/shard_map/jit(_where)/select_n | solution.py:180
  (105 shorter events, 6.5 us)
Async XLA Ops:
  7.2 4.8 %copy-start = (bf16[512,512]{1,0:T(8,128)(2,1)S(1)}, bf16[512,512]{1,0:T(8,128)(2,1)}, u32[]{:S(2)}) copy-start(bf16[512,512]{1,0:T(8,128)(2,1)} %param.10) | copy-start | bytes 1572868
  7.2 4.8 %copy-start.2 = (bf16[6144,512]{1,0:T(8,128)(2,1)S(1)}, bf16[6144,512]{1,0:T(8,128)(2,1)}, u32[]{:S(2)}) copy-start(bf16[6144,512]{1,0:T(8,128)(2,1)} %param.9) | copy-start | bytes 18874372
  20.0 3.7 copy-start.3
  28.9 2.8 copy-start.4
  31.7 2.8 copy-start.6
  31.7 2.8 copy-start.7
  117.8 10.0 %all-to-all-start = ((f32[4,1,12288]{2,1,0:T(1,128)}), f32[4,1,12288]{2,1,0:T(1,128)S(1)}, u32[]{:S(2)}, u32[]{:S(2)}) async-start(f32[4,1,12288]{2,1,0:T(1,128)} %broadcast_in_dim.174), calls=%async_computation | async-start | bytes 393216 | tf_op jit(solution)/shard_map/all_to_all | solution.py:18
  122.6 80.1 %all-gather.3.cloned.1.call-start = ((), (), s32[]{:S(2)}) async-start(), calls=%async_computation.2 | async-start | bytes 7864320 | tf_op jit(solution)/shard_map/all_gather | solution.py:103
  132.0 9.2 %copy-start.5 = (s32[1,24]{1,0:T(1,128)S(1)}, s32[1,24]{1,0:T(1,128)}, u32[]{:S(2)}) copy-start(s32[1,24]{1,0:T(1,128)} %param.13) | copy-start | bytes 292
  216.0 11.2 %copy-start.8 = (s32[1,24]{1,0:T(1,128)S(1)}, s32[1,24]{1,0:T(1,128)}, u32[]{:S(2)}) copy-start(s32[1,24]{1,0:T(1,128)} %param.14) | copy-start | bytes 292
  216.0 139.6 %all-to-all-start.1 = ((bf16[64,2,128,128]{3,2,1,0:T(8,128)(2,1)}), bf16[64,2,128,128]{3,2,1,0:T(8,128)(2,1)}, u32[]{:S(2)}, u32[]{:S(2)}) async-start(bf16[64,2,128,128]{3,2,1,0:T(8,128)(2,1)} %broadcast_select_fusion), calls=%async_computation.1 | async-start | bytes 8388608 | tf_op jit(solution)/shard_map/all_to_all | solution.py:176
  355.6 8.3 %copy-start.1 = (bf16[512,512]{1,0:T(8,128)(2,1)S(1)}, bf16[512,512]{1,0:T(8,128)(2,1)}, u32[]{:S(2)}) copy-start(bf16[512,512]{1,0:T(8,128)(2,1)} %param.10) | copy-start | bytes 1572868
Sparse Core Ops, SparseCore 0:
  132.1 70.5 all-gather.2
where the time goes:
time: 372 us; the launch traced here: 371 us
  blocking collectives  126 us (34%)
  waiting for transfers between devices  62.4 us (17%)
  matrix products  45 us (12%)
  loops' own time  37.9 us (10%)
  local copies, waits for them, and re-layouts  35.9 us (10%)
  other arithmetic  33.7 us (9%)
  starting transfers between devices  16 us (4%)
  between operations  14.3 us (4%)
    all_gather x1, blocking collectives, in_one_piece(): result = lax.all_gather(both, axis, axis=dim, tiled=True)  126 us
    all_gather x1, waiting for transfers between devices, layer_rows(): every_head = lax.all_gather(gated_rows, 'mp', axis=1, tiled=True)  60.7 us
    another operation x1, loops' own time, attend(): return lax.map(one_tile, tile_starts).reshape(row_count, head_size)  37.9 us
    dot_general x12, matrix products, one_tile(): return jnp.dot(weights, value_tile, preferred_element_type=jnp.float32)  31.4 us
    all_to_all x1, starting transfers between devices, per_device(): lax.all_to_all(outgoing, 'dp', split_axis=0, concat_axis=0, tiled=True)  11.2 us
    convert_element_type x1, other arithmetic, layer_rows(): widened = rows_in.astype(jnp.float32)  9.17 us
    unnamed x21, local copies, waits for them, and re-layouts  8.13 us
    dot_general x1, matrix products, layer_rows(): jnp.dot(normed, w_uvqk, preferred_element_type=jnp.float32)  7.98 us
  transfers between devices with their start and end apart: 3, of which 2 were waited for; matrix products, arithmetic and copies ran while one was open for 4% of the time, Pallas kernels for 0%

commit v1 on v0

v1 whole, which is shorter than its diff:
```python
import jax
import jax.numpy as jnp
from jax import lax
from jax.experimental import pallas as pl
from jax.experimental.pallas import tpu as pltpu
from jax.sharding import PartitionSpec as P

D = 512
HEADS = 4
HEAD = D // HEADS
BLOCK = 128
MAXB = 2
BLK_DEV = 48
USERS = 24
N_DP = 64
N_MP = 4
WIN = MAXB * BLOCK
MINE = USERS // N_MP
TILE = 8
GROUPS = WIN // TILE
HALVES = N_DP // GROUPS
PER_HALF = MINE // HALVES
EPS = 1e-05
BF16 = jnp.bfloat16
F32 = jnp.float32


def silu(v):
    half = v * 0.5
    return half + half * jnp.tanh(half)


def norm_stats(total, squares):
    mean = total * (1.0 / D)
    var = squares * (1.0 / D) - mean * mean
    return mean, lax.rsqrt(var + EPS)


def user_rows(x_bf, length, w_in, w_out):
    x = x_bf.astype(F32)
    mean, inv = norm_stats(
        jnp.sum(x, axis=1, keepdims=True), jnp.sum(x * x, axis=1, keepdims=True)
    )
    normed = ((x - mean) * inv).astype(BF16)
    row = lax.broadcasted_iota(jnp.int32, (BLOCK, BLOCK), 0)
    col = lax.broadcasted_iota(jnp.int32, (BLOCK, BLOCK), 1)
    causal = col <= row
    scale = HEAD ** (-0.5)
    contract_last = (((1,), (1,)), ((), ()))
    heads, gates = [], []
    for h in range(HEADS):
        proj = silu(jnp.dot(normed, w_in[h], preferred_element_type=F32)).astype(BF16)
        gates.append(proj[:, :HEAD])
        v = proj[:, HEAD : 2 * HEAD]
        q = proj[:, 2 * HEAD : 3 * HEAD]
        k = proj[:, 3 * HEAD :]
        s0 = lax.dot_general(q[:BLOCK], k[:BLOCK], contract_last, preferred_element_type=F32)
        s1 = lax.dot_general(q[BLOCK:], k, contract_last, preferred_element_type=F32)
        a0 = jnp.where(causal, silu(s0 * scale) * (1.0 / WIN), 0.0).astype(BF16)
        b = silu(s1 * scale) * (1.0 / WIN)
        a1 = jnp.concatenate(
            [b[:, :BLOCK].astype(BF16), jnp.where(causal, b[:, BLOCK:], 0.0).astype(BF16)], axis=1
        )
        heads.append(
            jnp.concatenate(
                [
                    jnp.dot(a0, v[:BLOCK], preferred_element_type=F32),
                    jnp.dot(a1, v, preferred_element_type=F32),
                ],
                axis=0,
            )
        )
    total = sum(jnp.sum(a, axis=1, keepdims=True) for a in heads)
    squares = sum(jnp.sum(a * a, axis=1, keepdims=True) for a in heads)
    mean, inv = norm_stats(total, squares)
    gated = jnp.concatenate(
        [((a - mean) * inv * g.astype(F32)).astype(BF16) for a, g in zip(heads, gates)], axis=1
    )
    mixed = jnp.dot(gated, w_out, preferred_element_type=F32) + x
    at = lax.broadcasted_iota(jnp.int32, (WIN, 1), 0)
    return jnp.where(at < length, mixed, 0.0)


def layer_kernel(start_ref, len_ref, x0_ref, x1_ref, w_ref, w_out_ref, out_ref, state_ref):
    i = pl.program_id(0)
    length = len_ref[i]
    x = jnp.concatenate([x0_ref[...], x1_ref[...]], axis=0)
    mixed = user_rows(x, length, w_ref, w_out_ref[...])
    out_ref[...] = mixed.astype(BF16).reshape(1, GROUPS, 1, TILE, D)
    at = lax.broadcasted_iota(jnp.int32, (WIN, 1), 0)
    last = jnp.sum(jnp.where(at == length - 1, mixed, 0.0), axis=0, keepdims=True)
    state_ref[...] = last.astype(BF16).reshape(1, 1, D)


def layer(tokens, starts, lengths, w_in, w_out):
    return pl.pallas_call(
        layer_kernel,
        grid_spec=pltpu.PrefetchScalarGridSpec(
            num_scalar_prefetch=2,
            grid=(MINE,),
            in_specs=[
                pl.BlockSpec((BLOCK, D), lambda i, s, n: (s[i], 0)),
                pl.BlockSpec((BLOCK, D), lambda i, s, n: (jnp.minimum(s[i] + 1, BLK_DEV - 1), 0)),
                pl.BlockSpec((HEADS, D, D), lambda i, s, n: (0, 0, 0)),
                pl.BlockSpec((D, D), lambda i, s, n: (0, 0)),
            ],
            out_specs=[
                pl.BlockSpec(
                    (1, GROUPS, 1, TILE, D),
                    lambda i, s, n: (i // PER_HALF, 0, i % PER_HALF, 0, 0),
                ),
                pl.BlockSpec((1, 1, D), lambda i, s, n: (i, 0, 0)),
            ],
        ),
        out_shape=[
            jax.ShapeDtypeStruct((HALVES, GROUPS, PER_HALF, TILE, D), BF16),
            jax.ShapeDtypeStruct((MINE, 1, D), BF16),
        ],
        name="layer",
    )(starts, lengths, tokens, tokens, w_in, w_out)


def regroup_kernel(src_ref, in_ref, out_ref):
    for k in range(PER_HALF):

        def one(o, carry):
            rows = in_ref[src_ref[k * N_DP + o], k]
            for q in range(N_MP):
                out_ref[o, q, k] = rows[:, q * HEAD : (q + 1) * HEAD]
            return carry

        lax.fori_loop(0, N_DP, one, 0, unroll=8)


def regroup(spread, src):
    return pl.pallas_call(
        regroup_kernel,
        grid_spec=pltpu.PrefetchScalarGridSpec(
            num_scalar_prefetch=1,
            grid=(1,),
            in_specs=[pl.BlockSpec((N_DP, PER_HALF, TILE, D), lambda i, s: (0, 0, 0, 0))],
            out_specs=pl.BlockSpec(
                (N_DP, N_MP, PER_HALF, TILE, HEAD), lambda i, s: (0, 0, 0, 0, 0)
            ),
        ),
        out_shape=jax.ShapeDtypeStruct((N_DP, N_MP, PER_HALF, TILE, HEAD), BF16),
        name="regroup",
    )(src, spread)


def place_kernel(len_ref, off_ref, in_ref, out_ref):
    zeros = jnp.zeros((BLOCK, HEAD), BF16)

    def clear(b, carry):
        out_ref[pl.ds(pl.multiple_of(b * BLOCK, BLOCK), BLOCK), :] = zeros
        return carry

    lax.fori_loop(0, BLK_DEV, clear, 0)
    half_groups = BLOCK // TILE

    def one(u, carry):
        m = u // MINE
        half = (u % MINE) // PER_HALF
        k = u % PER_HALF
        base = off_ref[u] * BLOCK

        def block(first):
            for g in range(first, first + half_groups):
                at = pl.multiple_of(base + g * TILE, TILE)
                out_ref[pl.ds(at, TILE), :] = in_ref[half, g, m, k]

        block(0)

        @pl.when(len_ref[u] > BLOCK)
        def _():
            block(half_groups)

        return carry

    lax.fori_loop(0, USERS, one, 0)


def place(arrived, lengths, offsets):
    return pl.pallas_call(
        place_kernel,
        grid_spec=pltpu.PrefetchScalarGridSpec(
            num_scalar_prefetch=2,
            grid=(1,),
            in_specs=[
                pl.BlockSpec(
                    (HALVES, GROUPS, N_MP, PER_HALF, TILE, HEAD),
                    lambda i, a, b: (0, 0, 0, 0, 0, 0),
                )
            ],
            out_specs=pl.BlockSpec((BLK_DEV * BLOCK, HEAD), lambda i, a, b: (0, 0)),
        ),
        out_shape=jax.ShapeDtypeStruct((BLK_DEV * BLOCK, HEAD), BF16),
        name="place",
    )(lengths, offsets, arrived)


def per_device(tokens, w_uvqk, w_out, hist_len, owner, recv_offset, block_start):
    me = lax.axis_index("dp")
    part = lax.axis_index("mp")
    first = part * MINE

    w_all = lax.all_to_all(
        jnp.broadcast_to(w_uvqk[None], (N_MP, D, D)), "mp", 0, 0, tiled=True
    )
    row = jnp.concatenate([owner, hist_len, recv_offset, jnp.zeros((1, 56), jnp.int32)], axis=1)
    table = lax.all_to_all(
        jnp.broadcast_to(row[None], (N_DP, 1, 128)), "dp", 0, 0, tiled=True
    ).reshape(N_DP, 128)

    starts = lax.dynamic_slice_in_dim(block_start[0], first, MINE, 0)
    lengths = lax.dynamic_slice_in_dim(hist_len[0], first, MINE, 0)
    mixed, last = layer(tokens, starts, lengths, w_all, w_out)

    spread = lax.all_to_all(mixed.reshape(N_DP, PER_HALF * TILE, D), "dp", 0, 0, tiled=True)

    owners = table[:, :USERS]
    ids = jnp.arange(N_DP, dtype=jnp.int32)
    held = lax.dynamic_slice_in_dim(owners, first + (me // GROUPS) * PER_HALF, PER_HALF, 1)
    src = jnp.sum(
        jnp.where(held.T[:, None, :] == ids[None, :, None], ids[None, None, :], 0), axis=2
    ).reshape(-1)
    sorted_rows = regroup(spread.reshape(N_DP, PER_HALF, TILE, D), src)
    arrived = lax.all_to_all(
        sorted_rows.reshape(N_DP * N_MP, PER_HALF * TILE, HEAD), ("dp", "mp"), 0, 0, tiled=True
    )
    mine = owners == me
    recv_len = jnp.sum(jnp.where(mine, table[:, USERS : 2 * USERS], 0), axis=0)
    recv_off = jnp.sum(jnp.where(mine, table[:, 2 * USERS : 3 * USERS], 0), axis=0)
    packed = place(
        arrived.reshape(HALVES, GROUPS, N_MP, PER_HALF, TILE, HEAD), recv_len, recv_off
    )

    columns = last.reshape(MINE, N_MP, HEAD)
    state = jnp.zeros((N_MP, MINE, HEAD), BF16)
    for s in range(N_MP):
        to = (part + s) % N_MP
        piece = lax.dynamic_slice_in_dim(columns, to, 1, 1)[:, 0]
        if s:
            piece = lax.ppermute(piece, "mp", [(i, (i + s) % N_MP) for i in range(N_MP)])
        state = lax.dynamic_update_slice_in_dim(state, piece[None], (part - s) % N_MP, 0)
    return packed, state.reshape(USERS, HEAD)


def solution(mesh):
    in_specs = (
        P("dp", None),
        P(None, "mp"),
        P(),
        P("dp", None),
        P("dp", None),
        P("dp", None),
        P("dp", None),
    )
    out_specs = (P("dp", "mp"), P("dp", "mp"))
    return jax.shard_map(
        per_device, mesh=mesh, in_specs=in_specs, out_specs=out_specs, check_vma=False
    )
```

time: 372 us -> 176 us (0.47)
  blocking collectives: 126 us -> 0 us
  matrix products: 45 us -> 0 us
  loops' own time: 37.9 us -> 0 us
  waiting for transfers between devices: 62.4 us -> 97.3 us
  other arithmetic: 33.7 us -> 0.92 us
  local copies, waits for them, and re-layouts: 35.9 us -> 8.23 us
  Pallas kernels: 0 us -> 26.5 us
  starting transfers between devices: 16 us -> 41.8 us
  between operations: 14.3 us -> 0.86 us
    all_gather x1 -> x0, blocking collectives: 126 us -> none  [in_one_piece(): result = lax.all_gather(both, axis, axis=dim, tiled=True)]
    all_to_all x2 -> x4, waiting for transfers between devices: 1.65 us -> 95.8 us  [the longest x1 37.4 us: per_device(): lax.all_to_all(mixed.reshape(N_DP, PER_HALF * TILE, D), 'dp', 0, 0, tiled...]
    all_gather x1 -> x0, waiting for transfers between devices: 60.7 us -> none  [layer_rows(): every_head = lax.all_gather(gated_rows, 'mp', axis=1, tiled=True)]
    dot_general x14 -> x0, matrix products: 45 us -> none  [the longest x12 31.4 us: one_tile(): return jnp.dot(weights, value_tile, preferred_element_type=jnp.float32)]
    another operation x1 -> x0, loops' own time: 37.9 us -> none  [attend(): return lax.map(one_tile, tile_starts).reshape(row_count, head_size)]
    pallas_call x0 -> x3, Pallas kernels: none -> 26.5 us  [the longest x1 18 us: layer(): pl.pallas_call(layer_kernel, grid_spec=pltpu.PrefetchScalarGridSpec(num_s...]
    all_to_all x2 -> x4, starting transfers between devices: 16 us -> 36.8 us  [the longest x1 14.5 us: per_device(): lax.all_to_all(jnp.broadcast_to(row[None], (N_DP, 1, 128)), 'dp', 0, 0, t...]
    convert_element_type x2 -> x0, other arithmetic: 13.1 us -> none  [the longest x1 9.17 us: layer_rows(): widened = rows_in.astype(jnp.float32)]
  transfers between devices with their start and end apart: 3 -> 7, of which waited for: 2 -> 5; matrix products, arithmetic and copies ran while one was open for 4% -> 2% of each run, Pallas kernels for 0% -> 10%
where the time goes in v1:
time: 176 us
  waiting for transfers between devices  97.3 us (55%)
  starting transfers between devices  41.8 us (24%)
  Pallas kernels  26.5 us (15%)
  local copies, waits for them, and re-layouts  8.23 us (5%)
    all_to_all x1, waiting for transfers between devices, per_device(): lax.all_to_all(mixed.reshape(N_DP, PER_HALF * TILE, D), 'dp', 0, 0, tiled...  37.4 us
    all_to_all x1, waiting for transfers between devices, per_device(): lax.all_to_all(sorted_rows.reshape(N_DP * N_MP, PER_HALF * TILE, HEAD), (...  34.6 us
    all_to_all x1, waiting for transfers between devices, per_device(): lax.all_to_all(jnp.broadcast_to(w_uvqk[None], (N_MP, D, D)), 'mp', 0, 0,...  23.8 us
    pallas_call x1, Pallas kernels, layer(): pl.pallas_call(layer_kernel, grid_spec=pltpu.PrefetchScalarGridSpec(num_s...  18 us
    all_to_all x1, starting transfers between devices, per_device(): lax.all_to_all(jnp.broadcast_to(row[None], (N_DP, 1, 128)), 'dp', 0, 0, t...  14.5 us
    all_to_all x1, starting transfers between devices, per_device(): lax.all_to_all(mixed.reshape(N_DP, PER_HALF * TILE, D), 'dp', 0, 0, tiled...  10.3 us
    all_to_all x1, starting transfers between devices, per_device(): lax.all_to_all(sorted_rows.reshape(N_DP * N_MP, PER_HALF * TILE, HEAD), (...  7.02 us
    ppermute x3, starting transfers between devices, per_device(): lax.ppermute(piece, 'mp', [(i, (i + s) % N_MP) for i in range(N_MP)])  5.01 us
  transfers between devices with their start and end apart: 7, of which 5 were waited for; matrix products, arithmetic and copies ran while one was open for 2% of the time, Pallas kernels for 10%

profile of v1, /device:TPU:1, one launch (start us, length us, event | category | flops | bytes accessed | tf_op | source)
XLA Modules:
  0.0 175.6 jit_solution(13689781032027639467)
XLA Ops:
  0.6 0.0 copy-start
  0.6 2.5 %broadcast_in_dim.55 = bf16[4,512,512]{2,1,0:T(8,128)(2,1)} broadcast(bf16[512,512]{1,0:T(8,128)(2,1)} %param.8), dimensions={1,2} | broadcast | bytes 2621440 | tf_op jit(solution)/shard_map/broadcast_in_dim | solution.py:208
  3.2 0.0 copy-start.6
  3.2 0.0 copy-start.5
  3.2 0.0 copy-start.7
  3.2 5.0 %all-to-all-start.1 = ((bf16[4,512,512]{2,1,0:T(8,128)(2,1)}), bf16[4,512,512]{2,1,0:T(8,128)(2,1)S(1)}, u32[]{:S(2)}, u32[]{:S(2)}) async-start(bf16[4,512,512]{2,1,0:T(8,128)(2,1)} %broadcast_in_dim.55), calls=%async_computation.1 | async-start | bytes 4194304 | tf_op jit(solution)/shard_map/all_to_all | solution.py:207
  8.2 0.0 copy-done.6
  8.2 0.6 fusion.3.len_ref
  8.8 0.0 copy-done.5
  8.8 0.0 copy-done.7
  8.8 0.1 fusion.4
  8.9 23.8 %all-to-all-done.1.w_ref = bf16[4,512,512]{2,1,0:T(8,128)(2,1)S(1)} async-done(((bf16[4,512,512]{2,1,0:T(8,128)(2,1)}), bf16[4,512,512]{2,1,0:T(8,128)(2,1)S(1)}, u32[]{:S(2)}, u32[]{:S(2)}) %all-to-all-start.1) | async-done | bytes 2097184 | tf_op jit(solution)/shard_map/all_to_all | solution.py:207
  32.6 0.0 copy-start.1
  32.6 0.7 broadcast_in_dim.51
  33.3 14.5 %all-to-all-start = ((s32[64,1,128]{2,1,0:T(1,128)}), s32[64,1,128]{2,1,0:T(1,128)S(1)}, u32[]{:S(2)}, u32[]{:S(2)}) async-start(s32[64,1,128]{2,1,0:T(1,128)} %broadcast_in_dim.51), calls=%async_computation | async-start | bytes 65536 | tf_op jit(solution)/shard_map/all_to_all | solution.py:211
  47.8 0.0 copy-done
  47.8 0.6 fusion.2.start_ref
  48.4 0.0 copy-done.1
  48.4 18.0 %layer.1 = (bf16[2,32,3,8,512]{4,3,2,1,0:T(8,128)(2,1)}, bf16[6,1,512]{2,1,0:T(2,128)(2,1)}) custom-call(s32[6]{0:T(128)} %fusion.2.start_ref, s32[6]{0:T(128)} %fusion.3.len_ref, bf16[6144,512]{1,0:T(8,128)(2,1)} %x1_ref.1, bf16[6144,512]{1,0:T(8,128)(2,1)} %x1_ref.1, bf16[4,512,512]{2,1,0:T(8,128)(2,1)} %copy-done.1, bf16[512,512]{1,0:T(8,128)(2,1)} %w_out_ref.1), custom_call_target="tpu_custom_call" | custom-call | tf_op jit(solution)/shard_map/layer/pallas_call | solution.py:96
  66.4 0.0 all-to-all-done
  66.4 10.3 %all-to-all-start.2 = ((bf16[64,24,512]{2,1,0:T(8,128)(2,1)}), bf16[64,24,512]{2,1,0:T(8,128)(2,1)S(1)}, u32[]{:S(2)}, u32[]{:S(2)}) async-start(bf16[64,24,512]{2,1,0:T(8,128)(2,1)} %bitcast.37), calls=%async_computation.2 | async-start | bytes 3145728 | tf_op jit(solution)/shard_map/all_to_all | solution.py:219
  76.8 0.6 fusion
  77.4 0.1 dynamic-slice_bitcast_fusion
  77.5 0.1 copy.13
  77.5 0.2 select_reduce_fusion
  77.7 0.7 reshape.36.src_ref
  78.4 37.4 %all-to-all-done.2 = bf16[64,24,512]{2,1,0:T(8,128)(2,1)S(1)} async-done(((bf16[64,24,512]{2,1,0:T(8,128)(2,1)}), bf16[64,24,512]{2,1,0:T(8,128)(2,1)S(1)}, u32[]{:S(2)}, u32[]{:S(2)}) %all-to-all-start.2) | async-done | bytes 1572896 | tf_op jit(solution)/shard_map/all_to_all | solution.py:219
  115.8 0.0 copy-start.3
  115.8 1.1 copy-done.3
  116.9 3.7 %regroup.1 = bf16[64,4,3,8,128]{4,3,2,1,0:T(8,128)(2,1)} custom-call(s32[192]{0:T(256)} %reshape.36.src_ref, bf16[64,3,8,512]{3,2,1,0:T(8,128)(2,1)} %bitcast.36), custom_call_target="tpu_custom_call" | custom-call | tf_op jit(solution)/shard_map/regroup/pallas_call | solution.py:136
  120.6 0.0 copy-start.4
  120.6 7.0 %all-to-all-start.3 = ((bf16[256,24,128]{2,1,0:T(8,128)(2,1)}), bf16[256,24,128]{2,1,0:T(8,128)(2,1)S(1)}, u32[]{:S(2)}, u32[]{:S(2)}) async-start(bf16[256,24,128]{2,1,0:T(8,128)(2,1)} %bitcast.35), calls=%async_computation.3 | async-start | bytes 3145728 | tf_op jit(solution)/shard_map/all_to_all | solution.py:228
  127.8 0.0 copy-done.4
  127.9 1.4 collective-permute-start
  129.3 2.4 %collective-permute-start.1 = (bf16[6,128]{1,0:T(8,128)(2,1)S(1)}, bf16[6,128]{1,0:T(8,128)(2,1)S(1)}, u32[]{:S(2)}, u32[]{:S(2)}) collective-permute-start(bf16[6,128]{1,0:T(8,128)(2,1)S(1)} %bitcast.40), channel_id=1, source_target_pairs={{0,2},{1,3},{2,0},{3,1},{4,6},{5,7},{6,4},{7,5},{8,10},{9,11},{10,... | collective-permute-start | bytes 4616 | tf_op jit(solution)/shard_map/ppermute | solution.py:244
  131.7 1.2 collective-permute-start.2
  132.9 0.0 collective-permute-done
  132.9 0.6 collective-permute-done.1
  133.6 0.9 collective-permute-done.2
  134.5 0.6 reshape.42
  135.1 34.6 %all-to-all-done.3 = bf16[256,24,128]{2,1,0:T(8,128)(2,1)S(1)} async-done(((bf16[256,24,128]{2,1,0:T(8,128)(2,1)}), bf16[256,24,128]{2,1,0:T(8,128)(2,1)S(1)}, u32[]{:S(2)}, u32[]{:S(2)}) %all-to-all-start.3) | async-done | bytes 1572896 | tf_op jit(solution)/shard_map/all_to_all | solution.py:228
  169.7 0.0 copy-start.2
  169.7 1.1 copy-done.2
  170.8 4.8 %place.1 = bf16[6144,128]{1,0:T(8,128)(2,1)} custom-call(s32[24]{0:T(128)} %get-tuple-element.7.len_ref, s32[24]{0:T(128)} %get-tuple-element.6.off_ref, bf16[2,32,4,3,8,128]{5,4,3,2,1,0:T(8,128)(2,1)} %bitcast.34), custom_call_target="tpu_custom_call" | custom-call | tf_op jit(solution)/shard_map/place/pallas_call | solution.py:184
  (12 shorter events, 0.1 us)
Async XLA Ops:
  0.6 47.2 %copy-start = (s32[1,24]{1,0:T(1,128)S(1)}, s32[1,24]{1,0:T(1,128)}, u32[]{:S(2)}) copy-start(s32[1,24]{1,0:T(1,128)} %param.13) | copy-start | bytes 292
  3.2 5.0 %copy-start.6 = (s32[1,24]{1,0:T(1,128)S(1)}, s32[1,24]{1,0:T(1,128)}, u32[]{:S(2)}) copy-start(s32[1,24]{1,0:T(1,128)} %param.10) | copy-start | bytes 292
  3.2 5.6 %copy-start.5 = (s32[1,24]{1,0:T(1,128)S(1)}, s32[1,24]{1,0:T(1,128)}, u32[]{:S(2)}) copy-start(s32[1,24]{1,0:T(1,128)} %param.12) | copy-start | bytes 292
  3.2 5.6 %copy-start.7 = (s32[1,24]{1,0:T(1,128)S(1)}, s32[1,24]{1,0:T(1,128)}, u32[]{:S(2)}) copy-start(s32[1,24]{1,0:T(1,128)} %param.11) | copy-start | bytes 292
  3.2 29.4 %all-to-all-start.1 = ((bf16[4,512,512]{2,1,0:T(8,128)(2,1)}), bf16[4,512,512]{2,1,0:T(8,128)(2,1)S(1)}, u32[]{:S(2)}, u32[]{:S(2)}) async-start(bf16[4,512,512]{2,1,0:T(8,128)(2,1)} %broadcast_in_dim.55), calls=%async_computation.1 | async-start | bytes 4194304 | tf_op jit(solution)/shard_map/all_to_all | solution.py:207
  32.6 15.7 %copy-start.1 = (bf16[4,512,512]{2,1,0:T(8,128)(2,1)}, bf16[4,512,512]{2,1,0:T(8,128)(2,1)S(1)}, u32[]{:S(2)}) copy-start(bf16[4,512,512]{2,1,0:T(8,128)(2,1)S(1)} %all-to-all-done.1.w_ref) | copy-start | bytes 6291460
  33.3 33.1 %all-to-all-start = ((s32[64,1,128]{2,1,0:T(1,128)}), s32[64,1,128]{2,1,0:T(1,128)S(1)}, u32[]{:S(2)}, u32[]{:S(2)}) async-start(s32[64,1,128]{2,1,0:T(1,128)} %broadcast_in_dim.51), calls=%async_computation | async-start | bytes 65536 | tf_op jit(solution)/shard_map/all_to_all | solution.py:211
  66.4 49.4 %all-to-all-start.2 = ((bf16[64,24,512]{2,1,0:T(8,128)(2,1)}), bf16[64,24,512]{2,1,0:T(8,128)(2,1)S(1)}, u32[]{:S(2)}, u32[]{:S(2)}) async-start(bf16[64,24,512]{2,1,0:T(8,128)(2,1)} %bitcast.37), calls=%async_computation.2 | async-start | bytes 3145728 | tf_op jit(solution)/shard_map/all_to_all | solution.py:219
  115.8 1.1 copy-start.3
  120.6 7.1 %copy-start.4 = (bf16[6,1,512]{2,1,0:T(2,128)(2,1)S(1)}, bf16[6,1,512]{2,1,0:T(2,128)(2,1)}, u32[]{:S(2)}) copy-start(bf16[6,1,512]{2,1,0:T(2,128)(2,1)} %get-tuple-element.5) | copy-start | bytes 18436
  120.6 49.0 %all-to-all-start.3 = ((bf16[256,24,128]{2,1,0:T(8,128)(2,1)}), bf16[256,24,128]{2,1,0:T(8,128)(2,1)S(1)}, u32[]{:S(2)}, u32[]{:S(2)}) async-start(bf16[256,24,128]{2,1,0:T(8,128)(2,1)} %bitcast.35), calls=%async_computation.3 | async-start | bytes 3145728 | tf_op jit(solution)/shard_map/all_to_all | solution.py:228
  127.9 5.0 %collective-permute-start = (bf16[6,128]{1,0:T(8,128)(2,1)S(1)}, bf16[6,128]{1,0:T(8,128)(2,1)S(1)}, u32[]{:S(2)}, u32[]{:S(2)}) collective-permute-start(bf16[6,128]{1,0:T(8,128)(2,1)S(1)} %bitcast.41), channel_id=1, source_target_pairs={{0,1},{1,2},{2,3},{3,0},{4,5},{5,6},{6,7},{7,4},{8,9},{9,10},{10,1... | collective-permute-start | bytes 4616 | tf_op jit(solution)/shard_map/ppermute | solution.py:244
  129.3 4.2 %collective-permute-start.1 = (bf16[6,128]{1,0:T(8,128)(2,1)S(1)}, bf16[6,128]{1,0:T(8,128)(2,1)S(1)}, u32[]{:S(2)}, u32[]{:S(2)}) collective-permute-start(bf16[6,128]{1,0:T(8,128)(2,1)S(1)} %bitcast.40), channel_id=1, source_target_pairs={{0,2},{1,3},{2,0},{3,1},{4,6},{5,7},{6,4},{7,5},{8,10},{9,11},{10,... | collective-permute-start | bytes 4616 | tf_op jit(solution)/shard_map/ppermute | solution.py:244
  131.7 2.7 %collective-permute-start.2 = (bf16[6,128]{1,0:T(8,128)(2,1)S(1)}, bf16[6,128]{1,0:T(8,128)(2,1)S(1)}, u32[]{:S(2)}, u32[]{:S(2)}) collective-permute-start(bf16[6,128]{1,0:T(8,128)(2,1)S(1)} %bitcast.39), channel_id=1, source_target_pairs={{0,3},{1,0},{2,1},{3,2},{4,7},{5,4},{6,5},{7,6},{8,11},{9,8},{10,9... | collective-permute-start | bytes 4616 | tf_op jit(solution)/shard_map/ppermute | solution.py:244
  169.7 1.2 copy-start.2

commit v2 on v1

--- a/solution.py
+++ b/solution.py
@@ -36,80 +36,140 @@
     return mean, lax.rsqrt(var + EPS)
 
 
-def user_rows(x_bf, length, w_in, w_out):
-    x = x_bf.astype(F32)
-    mean, inv = norm_stats(
-        jnp.sum(x, axis=1, keepdims=True), jnp.sum(x * x, axis=1, keepdims=True)
-    )
-    normed = ((x - mean) * inv).astype(BF16)
+def silu_gate(normed_parts, w_parts):
+    acc = jnp.dot(normed_parts[0], w_parts[0], preferred_element_type=F32)
+    for n, w in zip(normed_parts[1:], w_parts[1:]):
+        acc = acc + jnp.dot(n, w, preferred_element_type=F32)
+    proj = silu(acc).astype(BF16)
+    return [proj[:, j * HEAD : (j + 1) * HEAD] for j in range(4)]
+
+
+def attend(q, k, v):
     row = lax.broadcasted_iota(jnp.int32, (BLOCK, BLOCK), 0)
     col = lax.broadcasted_iota(jnp.int32, (BLOCK, BLOCK), 1)
     causal = col <= row
     scale = HEAD ** (-0.5)
     contract_last = (((1,), (1,)), ((), ()))
-    heads, gates = [], []
-    for h in range(HEADS):
-        proj = silu(jnp.dot(normed, w_in[h], preferred_element_type=F32)).astype(BF16)
-        gates.append(proj[:, :HEAD])
-        v = proj[:, HEAD : 2 * HEAD]
-        q = proj[:, 2 * HEAD : 3 * HEAD]
-        k = proj[:, 3 * HEAD :]
-        s0 = lax.dot_general(q[:BLOCK], k[:BLOCK], contract_last, preferred_element_type=F32)
-        s1 = lax.dot_general(q[BLOCK:], k, contract_last, preferred_element_type=F32)
-        a0 = jnp.where(causal, silu(s0 * scale) * (1.0 / WIN), 0.0).astype(BF16)
-        b = silu(s1 * scale) * (1.0 / WIN)
-        a1 = jnp.concatenate(
-            [b[:, :BLOCK].astype(BF16), jnp.where(causal, b[:, BLOCK:], 0.0).astype(BF16)], axis=1
-        )
-        heads.append(
-            jnp.concatenate(
-                [
-                    jnp.dot(a0, v[:BLOCK], preferred_element_type=F32),
-                    jnp.dot(a1, v, preferred_element_type=F32),
-                ],
-                axis=0,
-            )
-        )
+    s0 = lax.dot_general(q[:BLOCK], k[:BLOCK], contract_last, preferred_element_type=F32)
+    s1 = lax.dot_general(q[BLOCK:], k, contract_last, preferred_element_type=F32)
+    a0 = jnp.where(causal, silu(s0 * scale) * (1.0 / WIN), 0.0).astype(BF16)
+    b = silu(s1 * scale) * (1.0 / WIN)
+    a1 = jnp.concatenate(
+        [b[:, :BLOCK].astype(BF16), jnp.where(causal, b[:, BLOCK:], 0.0).astype(BF16)], axis=1
+    )
+    return jnp.concatenate(
+        [
+            jnp.dot(a0, v[:BLOCK], preferred_element_type=F32),
+            jnp.dot(a1, v, preferred_element_type=F32),
+        ],
+        axis=0,
+    )
+
+
+def own_head_kernel(start_ref, x0_ref, x1_ref, w_ref, normed_ref, att_ref, gate_ref):
+    x = jnp.concatenate([x0_ref[...], x1_ref[...]], axis=0).astype(F32)
+    mean, inv = norm_stats(
+        jnp.sum(x, axis=1, keepdims=True), jnp.sum(x * x, axis=1, keepdims=True)
+    )
+    normed = ((x - mean) * inv).astype(BF16)
+    normed_ref[0] = normed
+    u, v, q, k = silu_gate([normed], [w_ref[...]])
+    gate_ref[0] = u
+    att_ref[0] = attend(q, k, v)
+
+
+def window_specs():
+    return [
+        pl.BlockSpec((BLOCK, D), lambda i, s, *_: (s[i], 0)),
+        pl.BlockSpec((BLOCK, D), lambda i, s, *_: (jnp.minimum(s[i] + 1, BLK_DEV - 1), 0)),
+    ]
+
+
+def own_head(tokens, starts, w_own):
+    def per_user(width):
+        return pl.BlockSpec((1, WIN, width), lambda i, s: (i, 0, 0))
+
+    return pl.pallas_call(
+        own_head_kernel,
+        grid_spec=pltpu.PrefetchScalarGridSpec(
+            num_scalar_prefetch=1,
+            grid=(MINE,),
+            in_specs=window_specs() + [pl.BlockSpec((D, D), lambda i, s: (0, 0))],
+            out_specs=[per_user(D), per_user(HEAD), per_user(HEAD)],
+        ),
+        out_shape=[
+            jax.ShapeDtypeStruct((MINE, WIN, D), BF16),
+            jax.ShapeDtypeStruct((MINE, WIN, HEAD), F32),
+            jax.ShapeDtypeStruct((MINE, WIN, HEAD), BF16),
+        ],
+        cost_estimate=pl.CostEstimate(
+            flops=MINE * WIN * D * D * 64, bytes_accessed=MINE * WIN * D * 8, transcendentals=0
+        ),
+        name="own_head",
+    )(starts, tokens, tokens, w_own)
+
+
+def layer_kernel(
+    start_ref, len_ref, pos_ref,
+    x0_ref, x1_ref, normed_ref, att_ref, gate_ref, near_ref, far_ref, w_out_ref,
+    out_ref, state_ref,
+):
+    i = pl.program_id(0)
+    length = len_ref[i]
+    part = pos_ref[0]
+    low_is_near = pos_ref[1] == 0
+    half = D // 2
+    low = normed_ref[0, :, :half]
+    high = normed_ref[0, :, half:]
+    parts = [jnp.where(low_is_near, low, high), jnp.where(low_is_near, high, low)]
+    order = [part] + [(part + s) % HEADS for s in range(1, HEADS)]
+    heads, gates = [att_ref[0]], [gate_ref[0]]
+    for h in order[1:]:
+        u, v, q, k = silu_gate(parts, [near_ref[h], far_ref[h]])
+        gates.append(u)
+        heads.append(attend(q, k, v))
     total = sum(jnp.sum(a, axis=1, keepdims=True) for a in heads)
     squares = sum(jnp.sum(a * a, axis=1, keepdims=True) for a in heads)
     mean, inv = norm_stats(total, squares)
-    gated = jnp.concatenate(
-        [((a - mean) * inv * g.astype(F32)).astype(BF16) for a, g in zip(heads, gates)], axis=1
-    )
-    mixed = jnp.dot(gated, w_out, preferred_element_type=F32) + x
+    x = jnp.concatenate([x0_ref[...], x1_ref[...]], axis=0).astype(F32)
+    mixed = x
+    for h, a, g in zip(order, heads, gates):
+        gated = ((a - mean) * inv * g.astype(F32)).astype(BF16)
+        rows = w_out_ref[pl.ds(pl.multiple_of(h * HEAD, HEAD), HEAD), :]
+        mixed = mixed + jnp.dot(gated, rows, preferred_element_type=F32)
     at = lax.broadcasted_iota(jnp.int32, (WIN, 1), 0)
-    return jnp.where(at < length, mixed, 0.0)
-
-
-def layer_kernel(start_ref, len_ref, x0_ref, x1_ref, w_ref, w_out_ref, out_ref, state_ref):
-    i = pl.program_id(0)
-    length = len_ref[i]
-    x = jnp.concatenate([x0_ref[...], x1_ref[...]], axis=0)
-    mixed = user_rows(x, length, w_ref, w_out_ref[...])
+    mixed = jnp.where(at < length, mixed, 0.0)
     out_ref[...] = mixed.astype(BF16).reshape(1, GROUPS, 1, TILE, D)
-    at = lax.broadcasted_iota(jnp.int32, (WIN, 1), 0)
     last = jnp.sum(jnp.where(at == length - 1, mixed, 0.0), axis=0, keepdims=True)
     state_ref[...] = last.astype(BF16).reshape(1, 1, D)
 
 
-def layer(tokens, starts, lengths, w_in, w_out):
+def layer(tokens, starts, lengths, position, normed, att, gate, near, far, w_out):
+    def per_user(width):
+        return pl.BlockSpec((1, WIN, width), lambda i, *_: (i, 0, 0))
+
+    weights = pl.BlockSpec(memory_space=pltpu.VMEM)
+    near, far = (pltpu.with_memory_space_constraint(w, pltpu.VMEM) for w in (near, far))
     return pl.pallas_call(
         layer_kernel,
         grid_spec=pltpu.PrefetchScalarGridSpec(
-            num_scalar_prefetch=2,
+            num_scalar_prefetch=3,
             grid=(MINE,),
-            in_specs=[
-                pl.BlockSpec((BLOCK, D), lambda i, s, n: (s[i], 0)),
-                pl.BlockSpec((BLOCK, D), lambda i, s, n: (jnp.minimum(s[i] + 1, BLK_DEV - 1), 0)),
-                pl.BlockSpec((HEADS, D, D), lambda i, s, n: (0, 0, 0)),
-                pl.BlockSpec((D, D), lambda i, s, n: (0, 0)),
+            in_specs=window_specs()
+            + [
+                per_user(D),
+                per_user(HEAD),
+                per_user(HEAD),
+                weights,
+                weights,
+                pl.BlockSpec((D, D), lambda i, *_: (0, 0)),
             ],
             out_specs=[
                 pl.BlockSpec(
                     (1, GROUPS, 1, TILE, D),
-                    lambda i, s, n: (i // PER_HALF, 0, i % PER_HALF, 0, 0),
+                    lambda i, *_: (i // PER_HALF, 0, i % PER_HALF, 0, 0),
                 ),
-                pl.BlockSpec((1, 1, D), lambda i, s, n: (i, 0, 0)),
+                pl.BlockSpec((1, 1, D), lambda i, *_: (i, 0, 0)),
             ],
         ),
         out_shape=[
@@ -117,7 +177,7 @@
             jax.ShapeDtypeStruct((MINE, 1, D), BF16),
         ],
         name="layer",
-    )(starts, lengths, tokens, tokens, w_in, w_out)
+    )(starts, lengths, position, tokens, tokens, normed, att, gate, near, far, w_out)
 
 
 def regroup_kernel(src_ref, in_ref, out_ref):
@@ -138,14 +198,14 @@
         grid_spec=pltpu.PrefetchScalarGridSpec(
             num_scalar_prefetch=1,
             grid=(1,),
-            in_specs=[pl.BlockSpec((N_DP, PER_HALF, TILE, D), lambda i, s: (0, 0, 0, 0))],
+            in_specs=[pl.BlockSpec(memory_space=pltpu.VMEM)],
             out_specs=pl.BlockSpec(
                 (N_DP, N_MP, PER_HALF, TILE, HEAD), lambda i, s: (0, 0, 0, 0, 0)
             ),
         ),
         out_shape=jax.ShapeDtypeStruct((N_DP, N_MP, PER_HALF, TILE, HEAD), BF16),
         name="regroup",
-    )(src, spread)
+    )(src, pltpu.with_memory_space_constraint(spread, pltpu.VMEM))
 
 
 def place_kernel(len_ref, off_ref, in_ref, out_ref):
@@ -186,17 +246,12 @@
         grid_spec=pltpu.PrefetchScalarGridSpec(
             num_scalar_prefetch=2,
             grid=(1,),
-            in_specs=[
-                pl.BlockSpec(
-                    (HALVES, GROUPS, N_MP, PER_HALF, TILE, HEAD),
-                    lambda i, a, b: (0, 0, 0, 0, 0, 0),
-                )
-            ],
+            in_specs=[pl.BlockSpec(memory_space=pltpu.VMEM)],
             out_specs=pl.BlockSpec((BLK_DEV * BLOCK, HEAD), lambda i, a, b: (0, 0)),
         ),
         out_shape=jax.ShapeDtypeStruct((BLK_DEV * BLOCK, HEAD), BF16),
         name="place",
-    )(lengths, offsets, arrived)
+    )(lengths, offsets, pltpu.with_memory_space_constraint(arrived, pltpu.VMEM))
 
 
 def per_device(tokens, w_uvqk, w_out, hist_len, owner, recv_offset, block_start):
@@ -204,17 +259,29 @@
     part = lax.axis_index("mp")
     first = part * MINE
 
-    w_all = lax.all_to_all(
-        jnp.broadcast_to(w_uvqk[None], (N_MP, D, D)), "mp", 0, 0, tiled=True
-    )
-    row = jnp.concatenate([owner, hist_len, recv_offset, jnp.zeros((1, 56), jnp.int32)], axis=1)
-    table = lax.all_to_all(
-        jnp.broadcast_to(row[None], (N_DP, 1, 128)), "dp", 0, 0, tiled=True
-    ).reshape(N_DP, 128)
+    core = me % 2
+    half = D // 2
+    mine_rows = lax.dynamic_slice_in_dim(w_uvqk, core * half, half, 0)
+    near = lax.all_to_all(
+        jnp.broadcast_to(mine_rows[None], (N_MP, half, D)), "mp", 0, 0, tiled=True
+    )
+    far = lax.ppermute(near, "dp", [(i, i ^ 1) for i in range(N_DP)])
+    table = jnp.concatenate([owner, hist_len, recv_offset, jnp.zeros((1, 56), jnp.int32)], axis=1)
+    step = 1
+    while step < N_DP:
+        other = lax.ppermute(table, "dp", [(i, i ^ step) for i in range(N_DP)])
+        ahead = (me // step) % 2 == 1
+        table = jnp.concatenate(
+            [jnp.where(ahead, other, table), jnp.where(ahead, table, other)], axis=0
+        )
+        step *= 2
 
     starts = lax.dynamic_slice_in_dim(block_start[0], first, MINE, 0)
     lengths = lax.dynamic_slice_in_dim(hist_len[0], first, MINE, 0)
-    mixed, last = layer(tokens, starts, lengths, w_all, w_out)
+    normed, att, gate = own_head(tokens, starts, w_uvqk)
+    mixed, last = layer(
+        tokens, starts, lengths, jnp.stack([part, core]), normed, att, gate, near, far, w_out
+    )
 
     spread = lax.all_to_all(mixed.reshape(N_DP, PER_HALF * TILE, D), "dp", 0, 0, tiled=True)
 

time: 176 us -> 168 us (0.955)
  waiting for transfers between devices: 97.3 us -> 82.2 us
  starting transfers between devices: 41.8 us -> 48.8 us
  local copies, waits for them, and re-layouts: 8.23 us -> 4.75 us
  Pallas kernels: 26.5 us -> 29.1 us
    all_to_all x1, waiting for transfers between devices: 37.4 us -> 0.01 us  [per_device(): lax.all_to_all(mixed.reshape(N_DP, PER_HALF * TILE, D), 'dp', 0, 0, tiled...]
    ppermute x0 -> x7, waiting for transfers between devices: none -> 34 us  [the longest x6 34 us: per_device(): other = lax.ppermute(table, 'dp', [(i, i ^ step) for i in range(N_DP)])]
    all_to_all x2 -> x1, starting transfers between devices: 19.4 us -> 4.83 us  [per_device(): lax.all_to_all(jnp.broadcast_to(mine_rows[None], (N_MP, half, D)), 'mp',...]
    ppermute x0 -> x7, starting transfers between devices: none -> 14.3 us  [the longest x6 11.6 us: per_device(): other = lax.ppermute(table, 'dp', [(i, i ^ step) for i in range(N_DP)])]
    all_to_all x2 -> x1, waiting for transfers between devices: 23.8 us -> 12.7 us  [per_device(): lax.all_to_all(jnp.broadcast_to(mine_rows[None], (N_MP, half, D)), 'mp',...]
    pallas_call x0 -> x1, Pallas kernels: none -> 7.58 us  [own_head(): pl.pallas_call(own_head_kernel, grid_spec=pltpu.PrefetchScalarGridSpec(nu...]
    all_to_all x1, starting transfers between devices: 7.02 us -> 12.7 us  [per_device(): lax.all_to_all(sorted_rows.reshape(N_DP * N_MP, PER_HALF * TILE, HEAD), (...]
    unnamed x19 -> x13, local copies, waits for them, and re-layouts: 2.33 us -> 0.04 us
  transfers between devices with their start and end apart: 7 -> 13, of which waited for: 5 -> 10; matrix products, arithmetic and copies ran while one was open for 2% -> 3% of each run, Pallas kernels for 10% -> 5%
where the time goes in v2:
time: 168 us; the launch traced here: 167 us
  waiting for transfers between devices  82.2 us (49%)
  starting transfers between devices  48.8 us (29%)
  Pallas kernels  29.1 us (17%)
  local copies, waits for them, and re-layouts  4.75 us (3%)
    ppermute x6, waiting for transfers between devices, per_device(): other = lax.ppermute(table, 'dp', [(i, i ^ step) for i in range(N_DP)])  34 us
    all_to_all x1, waiting for transfers between devices, per_device(): lax.all_to_all(sorted_rows.reshape(N_DP * N_MP, PER_HALF * TILE, HEAD), (...  34 us
    pallas_call x1, Pallas kernels, layer(): pl.pallas_call(layer_kernel, grid_spec=pltpu.PrefetchScalarGridSpec(num_s...  15.8 us
    all_to_all x1, starting transfers between devices, per_device(): lax.all_to_all(sorted_rows.reshape(N_DP * N_MP, PER_HALF * TILE, HEAD), (...  12.7 us
    all_to_all x1, waiting for transfers between devices, per_device(): lax.all_to_all(jnp.broadcast_to(mine_rows[None], (N_MP, half, D)), 'mp',...  12.7 us
    all_to_all x1, starting transfers between devices, per_device(): lax.all_to_all(mixed.reshape(N_DP, PER_HALF * TILE, D), 'dp', 0, 0, tiled...  11.9 us
    ppermute x6, starting transfers between devices, per_device(): other = lax.ppermute(table, 'dp', [(i, i ^ step) for i in range(N_DP)])  11.6 us
    pallas_call x1, Pallas kernels, own_head(): pl.pallas_call(own_head_kernel, grid_spec=pltpu.PrefetchScalarGridSpec(nu...  7.58 us
  transfers between devices with their start and end apart: 13, of which 10 were waited for; matrix products, arithmetic and copies ran while one was open for 3% of the time, Pallas kernels for 5%

profile of v2, /device:TPU:1, one launch (start us, length us, event | category | flops | bytes accessed | tf_op | source)
XLA Modules:
  0.0 167.4 jit_solution(14984882660692868575)
XLA Ops:
  0.6 0.0 copy-start
  0.7 1.0 constant_dynamic-slice_fusion.4
  1.6 1.1 broadcast_in_dim.45
  2.7 4.8 %all-to-all-start = ((bf16[4,256,512]{2,1,0:T(8,128)(2,1)}), bf16[4,256,512]{2,1,0:T(8,128)(2,1)S(1)}, u32[]{:S(2)}, u32[]{:S(2)}) async-start(bf16[4,256,512]{2,1,0:T(8,128)(2,1)} %broadcast_in_dim.45), calls=%async_computation | async-start | bytes 2097152 | tf_op jit(solution)/shard_map/all_to_all | solution.py:265
  7.5 0.0 copy-done
  7.5 0.7 fusion.6.start_ref
  8.2 12.7 %all-to-all-done.near_ref = bf16[4,256,512]{2,1,0:T(8,128)(2,1)S(1)} async-done(((bf16[4,256,512]{2,1,0:T(8,128)(2,1)}), bf16[4,256,512]{2,1,0:T(8,128)(2,1)S(1)}, u32[]{:S(2)}, u32[]{:S(2)}) %all-to-all-start) | async-done | bytes 1048608 | tf_op jit(solution)/shard_map/all_to_all | solution.py:265
  20.9 2.7 %collective-permute-start.6 = (bf16[4,256,512]{2,1,0:T(8,128)(2,1)S(1)}, bf16[4,256,512]{2,1,0:T(8,128)(2,1)S(1)}, u32[]{:S(2)}, u32[]{:S(2)}) collective-permute-start(bf16[4,256,512]{2,1,0:T(8,128)(2,1)S(1)} %all-to-all-done.near_ref), channel_id=1, source_target_pairs={{0,4},{4,0},{8,12},{12,8},{16,20},{20,16},{24,28},{28,24},{32,36},... | collective-permute-start | bytes 3145736 | tf_op jit(solution)/shard_map/ppermute | solution.py:268
  23.6 7.6 %own_head.1 = (bf16[6,256,512]{2,1,0:T(8,128)(2,1)}, f32[6,256,128]{2,1,0:T(8,128)}, bf16[6,256,128]{2,1,0:T(8,128)(2,1)}) custom-call(s32[6]{0:T(128)} %fusion.6.start_ref, bf16[6144,512]{1,0:T(8,128)(2,1)} %x1_ref.3, bf16[6144,512]{1,0:T(8,128)(2,1)} %x1_ref.3, bf16[512,512]{1,0:T(8,128)(2,1)} %w_ref.1), custom_call_target="tpu_custom_call" | custom-call | flops 25769803776 | bytes 6291456 | tf_op jit(solution)/shard_map/own_head/pallas_call | solution.py:92
  31.2 0.0 copy-done.3
  31.2 0.5 fusion.7.len_ref
  31.7 0.6 pad_add_fusion.6.pos_ref
  32.3 0.0 collective-permute-done.6.far_ref
  32.3 15.8 %layer.1 = (bf16[2,32,3,8,512]{4,3,2,1,0:T(8,128)(2,1)}, bf16[6,1,512]{2,1,0:T(2,128)(2,1)}) custom-call(s32[6]{0:T(128)} %fusion.6.start_ref, s32[6]{0:T(128)} %fusion.7.len_ref, s32[2]{0:T(128)} %pad_add_fusion.6.pos_ref, bf16[6144,512]{1,0:T(8,128)(2,1)} %x1_ref.3, bf16[6144,512]{1,0:T(8,128)(2,1)} %x1_ref.3, ...), custom_call_target="tpu_custom_call" | custom-call | tf_op jit(solution)/shard_map/layer/pallas_call | solution.py:153
  48.1 0.0 copy-start.4
  48.1 11.9 %all-to-all-start.1 = ((bf16[64,24,512]{2,1,0:T(8,128)(2,1)}), bf16[64,24,512]{2,1,0:T(8,128)(2,1)S(1)}, u32[]{:S(2)}, u32[]{:S(2)}) async-start(bf16[64,24,512]{2,1,0:T(8,128)(2,1)} %bitcast.36), calls=%async_computation.1 | async-start | bytes 3145728 | tf_op jit(solution)/shard_map/all_to_all | solution.py:286
  60.0 0.0 copy-done.2
  60.0 0.1 bitcast_add_fusion
  60.1 0.5 collective-permute-start
  60.6 0.8 collective-permute-done
  61.4 0.1 broadcast_select_fusion.7
  61.5 1.4 collective-permute-start.1
  62.9 1.4 collective-permute-done.1
  64.3 2.9 %collective-permute-start.2 = (s32[4,128]{1,0:T(4,128)S(1)}, s32[4,128]{1,0:T(4,128)S(1)}, u32[]{:S(2)}, u32[]{:S(2)}) collective-permute-start(s32[4,128]{1,0:T(4,128)S(1)} %pad_add_fusion.4), channel_id=1, source_target_pairs={{0,16},{4,20},{8,24},{12,28},{16,0},{20,4},{24,8},{28,12},{32,48},... | collective-permute-start | bytes 6152 | tf_op jit(solution)/shard_map/ppermute | solution.py:272
  67.2 1.5 collective-permute-done.2
  68.7 1.7 collective-permute-start.3
  70.4 25.0 %collective-permute-done.3 = s32[8,128]{1,0:T(8,128)S(1)} collective-permute-done((s32[8,128]{1,0:T(8,128)S(1)}, s32[8,128]{1,0:T(8,128)S(1)}, u32[]{:S(2)}, u32[]{:S(2)}) %collective-permute-start.3) | collective-permute-done | bytes 4128 | tf_op jit(solution)/shard_map/ppermute | solution.py:272
  95.4 0.6 collective-permute-start.4
  96.0 3.3 %collective-permute-done.4 = s32[16,128]{1,0:T(8,128)S(1)} collective-permute-done((s32[16,128]{1,0:T(8,128)S(1)}, s32[16,128]{1,0:T(8,128)S(1)}, u32[]{:S(2)}, u32[]{:S(2)}) %collective-permute-start.4) | collective-permute-done | bytes 8224 | tf_op jit(solution)/shard_map/ppermute | solution.py:272
  99.3 4.7 %collective-permute-start.5 = (s32[32,128]{1,0:T(8,128)S(1)}, s32[32,128]{1,0:T(8,128)S(1)}, u32[]{:S(2)}, u32[]{:S(2)}) collective-permute-start(s32[32,128]{1,0:T(8,128)S(1)} %pad_add_fusion.1), channel_id=1, source_target_pairs={{0,128},{4,132},{8,136},{12,140},{16,144},{20,148},{24,152},{28,15... | collective-permute-start | bytes 49160 | tf_op jit(solution)/shard_map/ppermute | solution.py:272
  104.0 1.9 %collective-permute-done.5 = s32[32,128]{1,0:T(8,128)S(1)} collective-permute-done((s32[32,128]{1,0:T(8,128)S(1)}, s32[32,128]{1,0:T(8,128)S(1)}, u32[]{:S(2)}, u32[]{:S(2)}) %collective-permute-start.5) | collective-permute-done | bytes 16416 | tf_op jit(solution)/shard_map/ppermute | solution.py:272
  105.9 0.1 dynamic-slice_bitcast_fusion
  106.0 0.1 copy.16
  106.1 0.2 select_reduce_fusion
  106.2 0.7 reshape.29.src_ref
  106.9 0.0 all-to-all-done.1
  106.9 2.3 %regroup.1 = bf16[64,4,3,8,128]{4,3,2,1,0:T(8,128)(2,1)} custom-call(s32[192]{0:T(256)} %reshape.29.src_ref, bf16[64,3,8,512]{3,2,1,0:T(8,128)(2,1)S(1)} %bitcast.33), custom_call_target="tpu_custom_call" | custom-call | tf_op jit(solution)/shard_map/regroup/pallas_call | solution.py:196
  109.2 12.7 %all-to-all-start.2 = ((bf16[256,24,128]{2,1,0:T(8,128)(2,1)}), bf16[256,24,128]{2,1,0:T(8,128)(2,1)S(1)}, u32[]{:S(2)}, u32[]{:S(2)}) async-start(bf16[256,24,128]{2,1,0:T(8,128)(2,1)} %bitcast.35), calls=%async_computation.2 | async-start | bytes 3145728 | tf_op jit(solution)/shard_map/all_to_all | solution.py:295
  122.0 0.6 fusion.5
  122.7 1.4 collective-permute-start.7
  124.1 2.4 %collective-permute-start.8 = (bf16[6,128]{1,0:T(8,128)(2,1)S(1)}, bf16[6,128]{1,0:T(8,128)(2,1)S(1)}, u32[]{:S(2)}, u32[]{:S(2)}) collective-permute-start(bf16[6,128]{1,0:T(8,128)(2,1)S(1)} %bitcast.38), channel_id=1, source_target_pairs={{0,2},{1,3},{2,0},{3,1},{4,6},{5,7},{6,4},{7,5},{8,10},{9,11},{10,... | collective-permute-start | bytes 4616 | tf_op jit(solution)/shard_map/ppermute | solution.py:311
  126.5 1.2 collective-permute-start.9
  127.7 0.0 collective-permute-done.7
  127.7 0.7 collective-permute-done.8
  128.4 0.8 collective-permute-done.9
  129.3 0.6 reshape.35
  129.9 34.0 %all-to-all-done.2 = bf16[256,24,128]{2,1,0:T(8,128)(2,1)S(1)} async-done(((bf16[256,24,128]{2,1,0:T(8,128)(2,1)}), bf16[256,24,128]{2,1,0:T(8,128)(2,1)S(1)}, u32[]{:S(2)}, u32[]{:S(2)}) %all-to-all-start.2) | async-done | bytes 1572896 | tf_op jit(solution)/shard_map/all_to_all | solution.py:295
  163.9 3.5 %place.1 = bf16[6144,128]{1,0:T(8,128)(2,1)} custom-call(s32[24]{0:T(128)} %get-tuple-element.13.len_ref, s32[24]{0:T(128)} %get-tuple-element.12.off_ref, bf16[2,32,4,3,8,128]{5,4,3,2,1,0:T(8,128)(2,1)S(1)} %bitcast.34), custom_call_target="tpu_custom_call" | custom-call | tf_op jit(solution)/shard_map/place/pallas_call | solution.py:244
  (28 shorter events, 0.2 us)
Async XLA Ops:
  0.6 6.9 %copy-start = (s32[1,24]{1,0:T(1,128)S(1)}, s32[1,24]{1,0:T(1,128)}, u32[]{:S(2)}) copy-start(s32[1,24]{1,0:T(1,128)} %param.13) | copy-start | bytes 292
  2.7 18.2 %all-to-all-start = ((bf16[4,256,512]{2,1,0:T(8,128)(2,1)}), bf16[4,256,512]{2,1,0:T(8,128)(2,1)S(1)}, u32[]{:S(2)}, u32[]{:S(2)}) async-start(bf16[4,256,512]{2,1,0:T(8,128)(2,1)} %broadcast_in_dim.45), calls=%async_computation | async-start | bytes 2097152 | tf_op jit(solution)/shard_map/all_to_all | solution.py:265
  8.2 23.0 %copy-start.3 = (s32[1,24]{1,0:T(1,128)S(1)}, s32[1,24]{1,0:T(1,128)}, u32[]{:S(2)}) copy-start(s32[1,24]{1,0:T(1,128)} %param.10) | copy-start | bytes 292
  20.9 11.4 %collective-permute-start.6 = (bf16[4,256,512]{2,1,0:T(8,128)(2,1)S(1)}, bf16[4,256,512]{2,1,0:T(8,128)(2,1)S(1)}, u32[]{:S(2)}, u32[]{:S(2)}) collective-permute-start(bf16[4,256,512]{2,1,0:T(8,128)(2,1)S(1)} %all-to-all-done.near_ref), channel_id=1, source_target_pairs={{0,4},{4,0},{8,12},{12,8},{16,20},{20,16},{24,28},{28,24},{32,36},... | collective-permute-start | bytes 3145736 | tf_op jit(solution)/shard_map/ppermute | solution.py:268
  48.1 11.9 %copy-start.2 = (s32[1,24]{1,0:T(1,128)S(1)}, s32[1,24]{1,0:T(1,128)}, u32[]{:S(2)}) copy-start(s32[1,24]{1,0:T(1,128)} %param.12) | copy-start | bytes 292
  48.1 12.0 %copy-start.4 = (s32[1,24]{1,0:T(1,128)S(1)}, s32[1,24]{1,0:T(1,128)}, u32[]{:S(2)}) copy-start(s32[1,24]{1,0:T(1,128)} %param.11) | copy-start | bytes 292
  48.1 58.8 %all-to-all-start.1 = ((bf16[64,24,512]{2,1,0:T(8,128)(2,1)}), bf16[64,24,512]{2,1,0:T(8,128)(2,1)S(1)}, u32[]{:S(2)}, u32[]{:S(2)}) async-start(bf16[64,24,512]{2,1,0:T(8,128)(2,1)} %bitcast.36), calls=%async_computation.1 | async-start | bytes 3145728 | tf_op jit(solution)/shard_map/all_to_all | solution.py:286
  60.1 1.3 collective-permute-start
  61.5 2.8 %collective-permute-start.1 = (s32[2,128]{1,0:T(2,128)S(1)}, s32[2,128]{1,0:T(2,128)S(1)}, u32[]{:S(2)}, u32[]{:S(2)}) collective-permute-start(s32[2,128]{1,0:T(2,128)S(1)} %pad_add_fusion.5), channel_id=1, source_target_pairs={{0,8},{4,12},{8,0},{12,4},{16,24},{20,28},{24,16},{28,20},{32,40},... | collective-permute-start | bytes 3080 | tf_op jit(solution)/shard_map/ppermute | solution.py:272
  64.3 4.4 %collective-permute-start.2 = (s32[4,128]{1,0:T(4,128)S(1)}, s32[4,128]{1,0:T(4,128)S(1)}, u32[]{:S(2)}, u32[]{:S(2)}) collective-permute-start(s32[4,128]{1,0:T(4,128)S(1)} %pad_add_fusion.4), channel_id=1, source_target_pairs={{0,16},{4,20},{8,24},{12,28},{16,0},{20,4},{24,8},{28,12},{32,48},... | collective-permute-start | bytes 6152 | tf_op jit(solution)/shard_map/ppermute | solution.py:272
  68.7 26.7 %collective-permute-start.3 = (s32[8,128]{1,0:T(8,128)S(1)}, s32[8,128]{1,0:T(8,128)S(1)}, u32[]{:S(2)}, u32[]{:S(2)}) collective-permute-start(s32[8,128]{1,0:T(8,128)S(1)} %pad_add_fusion.3), channel_id=1, source_target_pairs={{0,32},{4,36},{8,40},{12,44},{16,48},{20,52},{24,56},{28,60},{32,0... | collective-permute-start | bytes 12296 | tf_op jit(solution)/shard_map/ppermute | solution.py:272
  95.4 3.9 %collective-permute-start.4 = (s32[16,128]{1,0:T(8,128)S(1)}, s32[16,128]{1,0:T(8,128)S(1)}, u32[]{:S(2)}, u32[]{:S(2)}) collective-permute-start(s32[16,128]{1,0:T(8,128)S(1)} %pad_add_fusion.2), channel_id=1, source_target_pairs={{0,64},{4,68},{8,72},{12,76},{16,80},{20,84},{24,88},{28,92},{32,9... | collective-permute-start | bytes 24584 | tf_op jit(solution)/shard_map/ppermute | solution.py:272
  99.3 6.6 %collective-permute-start.5 = (s32[32,128]{1,0:T(8,128)S(1)}, s32[32,128]{1,0:T(8,128)S(1)}, u32[]{:S(2)}, u32[]{:S(2)}) collective-permute-start(s32[32,128]{1,0:T(8,128)S(1)} %pad_add_fusion.1), channel_id=1, source_target_pairs={{0,128},{4,132},{8,136},{12,140},{16,144},{20,148},{24,152},{28,15... | collective-permute-start | bytes 49160 | tf_op jit(solution)/shard_map/ppermute | solution.py:272
  109.2 13.4 %copy-start.1 = (bf16[6,1,512]{2,1,0:T(2,128)(2,1)S(1)}, bf16[6,1,512]{2,1,0:T(2,128)(2,1)}, u32[]{:S(2)}) copy-start(bf16[6,1,512]{2,1,0:T(2,128)(2,1)} %get-tuple-element.11) | copy-start | bytes 18436
  109.2 54.7 %all-to-all-start.2 = ((bf16[256,24,128]{2,1,0:T(8,128)(2,1)}), bf16[256,24,128]{2,1,0:T(8,128)(2,1)S(1)}, u32[]{:S(2)}, u32[]{:S(2)}) async-start(bf16[256,24,128]{2,1,0:T(8,128)(2,1)} %bitcast.35), calls=%async_computation.2 | async-start | bytes 3145728 | tf_op jit(solution)/shard_map/all_to_all | solution.py:295
  122.7 5.0 %collective-permute-start.7 = (bf16[6,128]{1,0:T(8,128)(2,1)S(1)}, bf16[6,128]{1,0:T(8,128)(2,1)S(1)}, u32[]{:S(2)}, u32[]{:S(2)}) collective-permute-start(bf16[6,128]{1,0:T(8,128)(2,1)S(1)} %bitcast.39), channel_id=1, source_target_pairs={{0,1},{1,2},{2,3},{3,0},{4,5},{5,6},{6,7},{7,4},{8,9},{9,10},{10,1... | collective-permute-start | bytes 4616 | tf_op jit(solution)/shard_map/ppermute | solution.py:311
  124.1 4.3 %collective-permute-start.8 = (bf16[6,128]{1,0:T(8,128)(2,1)S(1)}, bf16[6,128]{1,0:T(8,128)(2,1)S(1)}, u32[]{:S(2)}, u32[]{:S(2)}) collective-permute-start(bf16[6,128]{1,0:T(8,128)(2,1)S(1)} %bitcast.38), channel_id=1, source_target_pairs={{0,2},{1,3},{2,0},{3,1},{4,6},{5,7},{6,4},{7,5},{8,10},{9,11},{10,... | collective-permute-start | bytes 4616 | tf_op jit(solution)/shard_map/ppermute | solution.py:311
  126.5 2.7 %collective-permute-start.9 = (bf16[6,128]{1,0:T(8,128)(2,1)S(1)}, bf16[6,128]{1,0:T(8,128)(2,1)S(1)}, u32[]{:S(2)}, u32[]{:S(2)}) collective-permute-start(bf16[6,128]{1,0:T(8,128)(2,1)S(1)} %bitcast.37), channel_id=1, source_target_pairs={{0,3},{1,0},{2,1},{3,2},{4,7},{5,4},{6,5},{7,6},{8,11},{9,8},{10,9... | collective-permute-start | bytes 4616 | tf_op jit(solution)/shard_map/ppermute | solution.py:311

commit v3 on v2

--- a/solution.py
+++ b/solution.py
@@ -20,27 +20,21 @@
 GROUPS = WIN // TILE
 HALVES = N_DP // GROUPS
 PER_HALF = MINE // HALVES
+MSG = PER_HALF * N_MP + 1
 EPS = 1e-05
 BF16 = jnp.bfloat16
 F32 = jnp.float32
 
 
-def silu(v):
-    half = v * 0.5
-    return half + half * jnp.tanh(half)
-
-
-def norm_stats(total, squares):
-    mean = total * (1.0 / D)
-    var = squares * (1.0 / D) - mean * mean
-    return mean, lax.rsqrt(var + EPS)
-
-
-def silu_gate(normed_parts, w_parts):
-    acc = jnp.dot(normed_parts[0], w_parts[0], preferred_element_type=F32)
-    for n, w in zip(normed_parts[1:], w_parts[1:]):
+def silu_of_twice(h):
+    return h + h * jnp.tanh(h)
+
+
+def project(half_parts, w_parts):
+    acc = jnp.dot(half_parts[0], w_parts[0], preferred_element_type=F32)
+    for n, w in zip(half_parts[1:], w_parts[1:]):
         acc = acc + jnp.dot(n, w, preferred_element_type=F32)
-    proj = silu(acc).astype(BF16)
+    proj = silu_of_twice(acc).astype(BF16)
     return [proj[:, j * HEAD : (j + 1) * HEAD] for j in range(4)]
 
 
@@ -48,12 +42,12 @@
     row = lax.broadcasted_iota(jnp.int32, (BLOCK, BLOCK), 0)
     col = lax.broadcasted_iota(jnp.int32, (BLOCK, BLOCK), 1)
     causal = col <= row
-    scale = HEAD ** (-0.5)
+    scale = 0.5 * HEAD ** (-0.5)
     contract_last = (((1,), (1,)), ((), ()))
     s0 = lax.dot_general(q[:BLOCK], k[:BLOCK], contract_last, preferred_element_type=F32)
     s1 = lax.dot_general(q[BLOCK:], k, contract_last, preferred_element_type=F32)
-    a0 = jnp.where(causal, silu(s0 * scale) * (1.0 / WIN), 0.0).astype(BF16)
-    b = silu(s1 * scale) * (1.0 / WIN)
+    a0 = jnp.where(causal, silu_of_twice(s0 * scale), 0.0).astype(BF16)
+    b = silu_of_twice(s1 * scale)
     a1 = jnp.concatenate(
         [b[:, :BLOCK].astype(BF16), jnp.where(causal, b[:, BLOCK:], 0.0).astype(BF16)], axis=1
     )
@@ -66,14 +60,20 @@
     )
 
 
-def own_head_kernel(start_ref, x0_ref, x1_ref, w_ref, normed_ref, att_ref, gate_ref):
+def norm_stats(total, squares, unit=1.0):
+    mean = total * (1.0 / D)
+    var = squares * (1.0 / D) - mean * mean
+    return mean, lax.rsqrt(var * (unit * unit) + EPS) * unit
+
+
+def own_head_kernel(start_ref, x0_ref, x1_ref, w_ref, half_ref, att_ref, gate_ref):
     x = jnp.concatenate([x0_ref[...], x1_ref[...]], axis=0).astype(F32)
     mean, inv = norm_stats(
         jnp.sum(x, axis=1, keepdims=True), jnp.sum(x * x, axis=1, keepdims=True)
     )
-    normed = ((x - mean) * inv).astype(BF16)
-    normed_ref[0] = normed
-    u, v, q, k = silu_gate([normed], [w_ref[...]])
+    half = ((x - mean) * (inv * 0.5)).astype(BF16)
+    half_ref[0] = half
+    u, v, q, k = project([half], [w_ref[...]])
     gate_ref[0] = u
     att_ref[0] = attend(q, k, v)
 
@@ -111,40 +111,64 @@
 
 def layer_kernel(
     start_ref, len_ref, pos_ref,
-    x0_ref, x1_ref, normed_ref, att_ref, gate_ref, near_ref, far_ref, w_out_ref,
-    out_ref, state_ref,
+    x0_ref, x1_ref, half_ref, att_ref, gate_ref, near_ref, far_ref, w_out_ref, table_ref,
+    out_ref, state_ref, w_out_s,
 ):
     i = pl.program_id(0)
+    k_user = i % PER_HALF
     length = len_ref[i]
     part = pos_ref[0]
     low_is_near = pos_ref[1] == 0
-    half = D // 2
-    low = normed_ref[0, :, :half]
-    high = normed_ref[0, :, half:]
+    order = [part] + [(part + s) % HEADS for s in range(1, HEADS)]
+
+    @pl.when(i == 0)
+    def _():
+        for s, h in enumerate(order):
+            w_out_s[s * HEAD : (s + 1) * HEAD, :] = w_out_ref[
+                pl.ds(pl.multiple_of(h * HEAD, HEAD), HEAD), :
+            ]
+
+    @pl.when(k_user == 0)
+    def _():
+        tile = jnp.broadcast_to(table_ref[...], (TILE, 128)).astype(F32).astype(BF16)
+        out_ref[0, :, PER_HALF * N_MP] = jnp.broadcast_to(tile[None], (GROUPS, TILE, 128))
+
+    low = half_ref[0, :, : D // 2]
+    high = half_ref[0, :, D // 2 :]
     parts = [jnp.where(low_is_near, low, high), jnp.where(low_is_near, high, low)]
-    order = [part] + [(part + s) % HEADS for s in range(1, HEADS)]
     heads, gates = [att_ref[0]], [gate_ref[0]]
     for h in order[1:]:
-        u, v, q, k = silu_gate(parts, [near_ref[h], far_ref[h]])
+        u, v, q, k = project(parts, [near_ref[h], far_ref[h]])
         gates.append(u)
         heads.append(attend(q, k, v))
-    total = sum(jnp.sum(a, axis=1, keepdims=True) for a in heads)
-    squares = sum(jnp.sum(a * a, axis=1, keepdims=True) for a in heads)
-    mean, inv = norm_stats(total, squares)
+    total = jnp.sum(heads[0] + heads[1] + (heads[2] + heads[3]), axis=1, keepdims=True)
+    squares = jnp.sum(
+        heads[0] * heads[0] + heads[1] * heads[1] + (heads[2] * heads[2] + heads[3] * heads[3]),
+        axis=1,
+        keepdims=True,
+    )
+    mean, inv = norm_stats(total, squares, 1.0 / WIN)
+    gated = jnp.concatenate(
+        [((a - mean) * inv * g.astype(F32)).astype(BF16) for a, g in zip(heads, gates)], axis=1
+    )
     x = jnp.concatenate([x0_ref[...], x1_ref[...]], axis=0).astype(F32)
-    mixed = x
-    for h, a, g in zip(order, heads, gates):
-        gated = ((a - mean) * inv * g.astype(F32)).astype(BF16)
-        rows = w_out_ref[pl.ds(pl.multiple_of(h * HEAD, HEAD), HEAD), :]
-        mixed = mixed + jnp.dot(gated, rows, preferred_element_type=F32)
+    mixed = jnp.dot(gated, w_out_s[...], preferred_element_type=F32) + x
     at = lax.broadcasted_iota(jnp.int32, (WIN, 1), 0)
-    mixed = jnp.where(at < length, mixed, 0.0)
-    out_ref[...] = mixed.astype(BF16).reshape(1, GROUPS, 1, TILE, D)
-    last = jnp.sum(jnp.where(at == length - 1, mixed, 0.0), axis=0, keepdims=True)
-    state_ref[...] = last.astype(BF16).reshape(1, 1, D)
-
-
-def layer(tokens, starts, lengths, position, normed, att, gate, near, far, w_out):
+    mixed = jnp.where(at < length, mixed, 0.0).astype(BF16)
+    for q in range(N_MP):
+        out_ref[0, :, k_user * N_MP + q] = mixed[:, q * HEAD : (q + 1) * HEAD].reshape(
+            GROUPS, TILE, HEAD
+        )
+    last = length - 1
+    pick = lax.broadcasted_iota(jnp.int32, (TILE, HEAD), 0) == last % TILE
+    for q in range(N_MP):
+        tile = out_ref[0, last // TILE, k_user * N_MP + q].astype(F32)
+        state_ref[0, :, q * HEAD : (q + 1) * HEAD] = jnp.sum(
+            jnp.where(pick, tile, 0.0), axis=0, keepdims=True
+        ).astype(BF16)
+
+
+def layer(tokens, starts, lengths, position, half, att, gate, near, far, w_out, table):
     def per_user(width):
         return pl.BlockSpec((1, WIN, width), lambda i, *_: (i, 0, 0))
 
@@ -163,36 +187,43 @@
                 weights,
                 weights,
                 pl.BlockSpec((D, D), lambda i, *_: (0, 0)),
+                pl.BlockSpec((1, 128), lambda i, *_: (0, 0)),
             ],
             out_specs=[
                 pl.BlockSpec(
-                    (1, GROUPS, 1, TILE, D),
-                    lambda i, *_: (i // PER_HALF, 0, i % PER_HALF, 0, 0),
+                    (1, GROUPS, MSG, TILE, HEAD), lambda i, *_: (i // PER_HALF, 0, 0, 0, 0)
                 ),
                 pl.BlockSpec((1, 1, D), lambda i, *_: (i, 0, 0)),
             ],
+            scratch_shapes=[pltpu.VMEM((D, D), BF16)],
         ),
         out_shape=[
-            jax.ShapeDtypeStruct((HALVES, GROUPS, PER_HALF, TILE, D), BF16),
+            jax.ShapeDtypeStruct((HALVES, GROUPS, MSG, TILE, HEAD), BF16),
             jax.ShapeDtypeStruct((MINE, 1, D), BF16),
         ],
         name="layer",
-    )(starts, lengths, position, tokens, tokens, normed, att, gate, near, far, w_out)
-
-
-def regroup_kernel(src_ref, in_ref, out_ref):
-    for k in range(PER_HALF):
-
-        def one(o, carry):
-            rows = in_ref[src_ref[k * N_DP + o], k]
+    )(starts, lengths, position, tokens, tokens, half, att, gate, near, far, w_out, table)
+
+
+def regroup_kernel(first_ref, in_ref, out_ref, table_v, table_s, sem):
+    table = jnp.max(in_ref[:, PER_HALF * N_MP].astype(F32), axis=1)
+    table_v[...] = table.astype(jnp.int32)
+    copy = pltpu.make_async_copy(table_v, table_s, sem)
+    copy.start()
+    copy.wait()
+    first = first_ref[0]
+
+    def one(d, carry):
+        for k in range(PER_HALF):
+            o = table_s[d, first + k]
             for q in range(N_MP):
-                out_ref[o, q, k] = rows[:, q * HEAD : (q + 1) * HEAD]
-            return carry
-
-        lax.fori_loop(0, N_DP, one, 0, unroll=8)
-
-
-def regroup(spread, src):
+                out_ref[o, q, k] = in_ref[d, k * N_MP + q]
+        return carry
+
+    lax.fori_loop(0, N_DP, one, 0, unroll=8)
+
+
+def regroup(spread, first):
     return pl.pallas_call(
         regroup_kernel,
         grid_spec=pltpu.PrefetchScalarGridSpec(
@@ -202,10 +233,15 @@
             out_specs=pl.BlockSpec(
                 (N_DP, N_MP, PER_HALF, TILE, HEAD), lambda i, s: (0, 0, 0, 0, 0)
             ),
+            scratch_shapes=[
+                pltpu.VMEM((N_DP, 128), jnp.int32),
+                pltpu.SMEM((N_DP, 128), jnp.int32),
+                pltpu.SemaphoreType.DMA,
+            ],
         ),
         out_shape=jax.ShapeDtypeStruct((N_DP, N_MP, PER_HALF, TILE, HEAD), BF16),
         name="regroup",
-    )(src, pltpu.with_memory_space_constraint(spread, pltpu.VMEM))
+    )(first, pltpu.with_memory_space_constraint(spread, pltpu.VMEM))
 
 
 def place_kernel(len_ref, off_ref, in_ref, out_ref):
@@ -267,31 +303,20 @@
     )
     far = lax.ppermute(near, "dp", [(i, i ^ 1) for i in range(N_DP)])
     table = jnp.concatenate([owner, hist_len, recv_offset, jnp.zeros((1, 56), jnp.int32)], axis=1)
-    step = 1
-    while step < N_DP:
-        other = lax.ppermute(table, "dp", [(i, i ^ step) for i in range(N_DP)])
-        ahead = (me // step) % 2 == 1
-        table = jnp.concatenate(
-            [jnp.where(ahead, other, table), jnp.where(ahead, table, other)], axis=0
-        )
-        step *= 2
-
     starts = lax.dynamic_slice_in_dim(block_start[0], first, MINE, 0)
     lengths = lax.dynamic_slice_in_dim(hist_len[0], first, MINE, 0)
     normed, att, gate = own_head(tokens, starts, w_uvqk)
     mixed, last = layer(
-        tokens, starts, lengths, jnp.stack([part, core]), normed, att, gate, near, far, w_out
-    )
-
-    spread = lax.all_to_all(mixed.reshape(N_DP, PER_HALF * TILE, D), "dp", 0, 0, tiled=True)
-
+        tokens, starts, lengths, jnp.stack([part, core]), normed, att, gate, near, far, w_out, table
+    )
+
+    spread = lax.all_to_all(
+        mixed.reshape(N_DP, MSG * TILE, HEAD), "dp", 0, 0, tiled=True
+    ).reshape(N_DP, MSG, TILE, HEAD)
+    held = first + (me // GROUPS) * PER_HALF
+    sorted_rows = regroup(spread, held[None])
+    table = spread[:, MSG - 1, 0, :].astype(jnp.int32)
     owners = table[:, :USERS]
-    ids = jnp.arange(N_DP, dtype=jnp.int32)
-    held = lax.dynamic_slice_in_dim(owners, first + (me // GROUPS) * PER_HALF, PER_HALF, 1)
-    src = jnp.sum(
-        jnp.where(held.T[:, None, :] == ids[None, :, None], ids[None, None, :], 0), axis=2
-    ).reshape(-1)
-    sorted_rows = regroup(spread.reshape(N_DP, PER_HALF, TILE, D), src)
     arrived = lax.all_to_all(
         sorted_rows.reshape(N_DP * N_MP, PER_HALF * TILE, HEAD), ("dp", "mp"), 0, 0, tiled=True
     )

time: 168 us -> 157 us (0.935)
  starting transfers between devices: 48.8 us -> 31.5 us
  waiting for transfers between devices: 82.2 us -> 89.8 us
    all_to_all x1, waiting for transfers between devices: 0.01 us -> 41.7 us  [per_device(): lax.all_to_all(mixed.reshape(N_DP, MSG * TILE, HEAD), 'dp', 0, 0, tiled=T...]
    ppermute x6 -> x0, waiting for transfers between devices: 34 us -> none  [per_device(): other = lax.ppermute(table, 'dp', [(i, i ^ step) for i in range(N_DP)])]
    ppermute x6 -> x0, starting transfers between devices: 11.6 us -> none  [per_device(): other = lax.ppermute(table, 'dp', [(i, i ^ step) for i in range(N_DP)])]
    all_to_all x1, starting transfers between devices: 12.7 us -> 7.16 us  [per_device(): lax.all_to_all(sorted_rows.reshape(N_DP * N_MP, PER_HALF * TILE, HEAD), (...]
  transfers between devices with their start and end apart: 13 -> 7, of which waited for: 10 -> 5; matrix products, arithmetic and copies ran while one was open for 3% -> 2% of each run, Pallas kernels for 5% -> 5%
where the time goes in v3:
time: 157 us; the launch traced here: 156 us
  waiting for transfers between devices  89.8 us (57%)
  starting transfers between devices  31.5 us (20%)
  Pallas kernels  28.8 us (18%)
  local copies, waits for them, and re-layouts  3.4 us (2%)
  other arithmetic  1.96 us (1%)
    all_to_all x1, waiting for transfers between devices, per_device(): lax.all_to_all(mixed.reshape(N_DP, MSG * TILE, HEAD), 'dp', 0, 0, tiled=T...  41.7 us
    all_to_all x1, waiting for transfers between devices, per_device(): lax.all_to_all(sorted_rows.reshape(N_DP * N_MP, PER_HALF * TILE, HEAD), (...  33.9 us
    pallas_call x1, Pallas kernels, layer(): pl.pallas_call(layer_kernel, grid_spec=pltpu.PrefetchScalarGridSpec(num_s...  14.7 us
    all_to_all x1, waiting for transfers between devices, per_device(): lax.all_to_all(jnp.broadcast_to(mine_rows[None], (N_MP, half, D)), 'mp',...  12.7 us
    all_to_all x1, starting transfers between devices, per_device(): lax.all_to_all(mixed.reshape(N_DP, MSG * TILE, HEAD), 'dp', 0, 0, tiled=T...  11.8 us
    pallas_call x1, Pallas kernels, own_head(): pl.pallas_call(own_head_kernel, grid_spec=pltpu.PrefetchScalarGridSpec(nu...  7.66 us
    all_to_all x1, starting transfers between devices, per_device(): lax.all_to_all(sorted_rows.reshape(N_DP * N_MP, PER_HALF * TILE, HEAD), (...  7.16 us
    ppermute x3, starting transfers between devices, per_device(): lax.ppermute(piece, 'mp', [(i, (i + s) % N_MP) for i in range(N_MP)])  5.01 us
  transfers between devices with their start and end apart: 7, of which 5 were waited for; matrix products, arithmetic and copies ran while one was open for 2% of the time, Pallas kernels for 5%

profile of v3, /device:TPU:1, one launch (start us, length us, event | category | flops | bytes accessed | tf_op | source)
XLA Modules:
  0.0 156.3 jit_solution(5529113148094638453)
XLA Ops:
  0.6 1.0 constant_dynamic-slice_fusion.4
  1.6 0.0 copy-start.1
  1.6 0.0 copy-start.2
  1.6 1.1 broadcast_in_dim.29
  2.7 4.8 %all-to-all-start = ((bf16[4,256,512]{2,1,0:T(8,128)(2,1)}), bf16[4,256,512]{2,1,0:T(8,128)(2,1)S(1)}, u32[]{:S(2)}, u32[]{:S(2)}) async-start(bf16[4,256,512]{2,1,0:T(8,128)(2,1)} %broadcast_in_dim.29), calls=%async_computation | async-start | bytes 2097152 | tf_op jit(solution)/shard_map/all_to_all | solution.py:301
  7.5 0.0 copy-done.1
  7.5 0.0 copy-done.2
  7.5 0.7 fusion.2
  8.2 12.7 %all-to-all-done.near_ref = bf16[4,256,512]{2,1,0:T(8,128)(2,1)S(1)} async-done(((bf16[4,256,512]{2,1,0:T(8,128)(2,1)}), bf16[4,256,512]{2,1,0:T(8,128)(2,1)S(1)}, u32[]{:S(2)}, u32[]{:S(2)}) %all-to-all-start) | async-done | bytes 1048608 | tf_op jit(solution)/shard_map/all_to_all | solution.py:301
  20.9 2.7 %collective-permute-start = (bf16[4,256,512]{2,1,0:T(8,128)(2,1)S(1)}, bf16[4,256,512]{2,1,0:T(8,128)(2,1)S(1)}, u32[]{:S(2)}, u32[]{:S(2)}) collective-permute-start(bf16[4,256,512]{2,1,0:T(8,128)(2,1)S(1)} %all-to-all-done.near_ref), channel_id=1, source_target_pairs={{0,4},{4,0},{8,12},{12,8},{16,20},{20,16},{24,28},{28,24},{32,36},... | collective-permute-start | bytes 3145736 | tf_op jit(solution)/shard_map/ppermute | solution.py:304
  23.6 0.0 copy-start.3
  23.6 0.0 copy-start.4
  23.6 7.7 %own_head.1 = (bf16[6,256,512]{2,1,0:T(8,128)(2,1)}, f32[6,256,128]{2,1,0:T(8,128)}, bf16[6,256,128]{2,1,0:T(8,128)(2,1)}) custom-call(s32[6]{0:T(128)} %get-tuple-element.18.start_ref, bf16[6144,512]{1,0:T(8,128)(2,1)} %x1_ref.3, bf16[6144,512]{1,0:T(8,128)(2,1)} %x1_ref.3, bf16[512,512]{1,0:T(8,128)(2,1)} %w_ref.1), custom_call_target="tpu_custom_call" | custom-call | flops 25769803776 | bytes 6291456 | tf_op jit(solution)/shard_map/own_head/pallas_call | solution.py:92
  31.2 0.7 pad_add_fusion.pos_ref
  31.9 0.0 copy-done.3
  31.9 0.0 copy-done.4
  31.9 0.6 bitcast_add_fusion.table_ref
  32.5 0.0 collective-permute-done.far_ref
  32.5 14.7 %layer.1 = (bf16[2,32,13,8,128]{4,3,2,1,0:T(8,128)(2,1)}, bf16[6,1,512]{2,1,0:T(2,128)(2,1)}) custom-call(s32[6]{0:T(128)} %get-tuple-element.18.start_ref, s32[6]{0:T(128)} %get-tuple-element.19.len_ref, s32[2]{0:T(128)} %pad_add_fusion.pos_ref, bf16[6144,512]{1,0:T(8,128)(2,1)} %x1_ref.3, bf16[6144,512]{1,0:T(8,128)(2,1)} %x1_ref.3, ...), custom_call_target="tpu_custom_call" | custom-call | tf_op jit(solution)/shard_map/layer/pallas_call | solution.py:177
  47.2 11.8 %all-to-all-start.1 = ((bf16[64,104,128]{2,1,0:T(8,128)(2,1)}), bf16[64,104,128]{2,1,0:T(8,128)(2,1)S(1)}, u32[]{:S(2)}, u32[]{:S(2)}) async-start(bf16[64,104,128]{2,1,0:T(8,128)(2,1)} %bitcast.35), calls=%async_computation.1 | async-start | bytes 3407872 | tf_op jit(solution)/shard_map/all_to_all | solution.py:313
  59.0 41.7 %all-to-all-done.1 = bf16[64,104,128]{2,1,0:T(8,128)(2,1)S(1)} async-done(((bf16[64,104,128]{2,1,0:T(8,128)(2,1)}), bf16[64,104,128]{2,1,0:T(8,128)(2,1)S(1)}, u32[]{:S(2)}, u32[]{:S(2)}) %all-to-all-start.1) | async-done | bytes 1703968 | tf_op jit(solution)/shard_map/all_to_all | solution.py:313
  100.7 2.9 %regroup.1 = bf16[64,4,3,8,128]{4,3,2,1,0:T(8,128)(2,1)} custom-call(s32[1]{0:T(128)} %bitcast.7.first_ref, bf16[64,13,8,128]{3,2,1,0:T(8,128)(2,1)S(1)} %bitcast.31), custom_call_target="tpu_custom_call" | custom-call | tf_op jit(solution)/shard_map/regroup/pallas_call | solution.py:227
  103.6 0.0 copy-start
  103.6 7.2 %all-to-all-start.2 = ((bf16[256,24,128]{2,1,0:T(8,128)(2,1)}), bf16[256,24,128]{2,1,0:T(8,128)(2,1)S(1)}, u32[]{:S(2)}, u32[]{:S(2)}) async-start(bf16[256,24,128]{2,1,0:T(8,128)(2,1)} %bitcast.34), calls=%async_computation.2 | async-start | bytes 3145728 | tf_op jit(solution)/shard_map/all_to_all | solution.py:320
  110.9 0.0 copy-done
  111.0 1.4 collective-permute-start.1
  112.4 2.4 %collective-permute-start.2 = (bf16[6,128]{1,0:T(8,128)(2,1)S(1)}, bf16[6,128]{1,0:T(8,128)(2,1)S(1)}, u32[]{:S(2)}, u32[]{:S(2)}) collective-permute-start(bf16[6,128]{1,0:T(8,128)(2,1)S(1)} %bitcast.38), channel_id=1, source_target_pairs={{0,2},{1,3},{2,0},{3,1},{4,6},{5,7},{6,4},{7,5},{8,10},{9,11},{10,... | collective-permute-start | bytes 4616 | tf_op jit(solution)/shard_map/ppermute | solution.py:336
  114.8 1.2 collective-permute-start.3
  116.0 0.0 collective-permute-done.1
  116.1 0.6 collective-permute-done.2
  116.7 0.9 collective-permute-done.3
  117.6 0.6 reshape.32
  118.2 0.7 fusion
  118.9 33.9 %all-to-all-done.2 = bf16[256,24,128]{2,1,0:T(8,128)(2,1)S(1)} async-done(((bf16[256,24,128]{2,1,0:T(8,128)(2,1)}), bf16[256,24,128]{2,1,0:T(8,128)(2,1)S(1)}, u32[]{:S(2)}, u32[]{:S(2)}) %all-to-all-start.2) | async-done | bytes 1572896 | tf_op jit(solution)/shard_map/all_to_all | solution.py:320
  152.8 3.5 %place.1 = bf16[6144,128]{1,0:T(8,128)(2,1)} custom-call(s32[24]{0:T(128)} %get-tuple-element.13.len_ref, s32[24]{0:T(128)} %get-tuple-element.12.off_ref, bf16[2,32,4,3,8,128]{5,4,3,2,1,0:T(8,128)(2,1)S(1)} %bitcast.33), custom_call_target="tpu_custom_call" | custom-call | tf_op jit(solution)/shard_map/place/pallas_call | solution.py:280
  (13 shorter events, 0.2 us)
Async XLA Ops:
  1.6 5.9 %copy-start.1 = (s32[1,24]{1,0:T(1,128)S(1)}, s32[1,24]{1,0:T(1,128)}, u32[]{:S(2)}) copy-start(s32[1,24]{1,0:T(1,128)} %param.10) | copy-start | bytes 292
  1.6 5.9 %copy-start.2 = (s32[1,24]{1,0:T(1,128)S(1)}, s32[1,24]{1,0:T(1,128)}, u32[]{:S(2)}) copy-start(s32[1,24]{1,0:T(1,128)} %param.13) | copy-start | bytes 292
  2.7 18.2 %all-to-all-start = ((bf16[4,256,512]{2,1,0:T(8,128)(2,1)}), bf16[4,256,512]{2,1,0:T(8,128)(2,1)S(1)}, u32[]{:S(2)}, u32[]{:S(2)}) async-start(bf16[4,256,512]{2,1,0:T(8,128)(2,1)} %broadcast_in_dim.29), calls=%async_computation | async-start | bytes 2097152 | tf_op jit(solution)/shard_map/all_to_all | solution.py:301
  20.9 11.6 %collective-permute-start = (bf16[4,256,512]{2,1,0:T(8,128)(2,1)S(1)}, bf16[4,256,512]{2,1,0:T(8,128)(2,1)S(1)}, u32[]{:S(2)}, u32[]{:S(2)}) collective-permute-start(bf16[4,256,512]{2,1,0:T(8,128)(2,1)S(1)} %all-to-all-done.near_ref), channel_id=1, source_target_pairs={{0,4},{4,0},{8,12},{12,8},{16,20},{20,16},{24,28},{28,24},{32,36},... | collective-permute-start | bytes 3145736 | tf_op jit(solution)/shard_map/ppermute | solution.py:304
  23.6 8.3 %copy-start.3 = (s32[1,24]{1,0:T(1,128)S(1)}, s32[1,24]{1,0:T(1,128)}, u32[]{:S(2)}) copy-start(s32[1,24]{1,0:T(1,128)} %param.12) | copy-start | bytes 292
  23.6 8.3 %copy-start.4 = (s32[1,24]{1,0:T(1,128)S(1)}, s32[1,24]{1,0:T(1,128)}, u32[]{:S(2)}) copy-start(s32[1,24]{1,0:T(1,128)} %param.11) | copy-start | bytes 292
  47.2 53.5 %all-to-all-start.1 = ((bf16[64,104,128]{2,1,0:T(8,128)(2,1)}), bf16[64,104,128]{2,1,0:T(8,128)(2,1)S(1)}, u32[]{:S(2)}, u32[]{:S(2)}) async-start(bf16[64,104,128]{2,1,0:T(8,128)(2,1)} %bitcast.35), calls=%async_computation.1 | async-start | bytes 3407872 | tf_op jit(solution)/shard_map/all_to_all | solution.py:313
  103.6 7.3 %copy-start = (bf16[6,1,512]{2,1,0:T(2,128)(2,1)S(1)}, bf16[6,1,512]{2,1,0:T(2,128)(2,1)}, u32[]{:S(2)}) copy-start(bf16[6,1,512]{2,1,0:T(2,128)(2,1)} %get-tuple-element.11) | copy-start | bytes 18436
  103.6 49.2 %all-to-all-start.2 = ((bf16[256,24,128]{2,1,0:T(8,128)(2,1)}), bf16[256,24,128]{2,1,0:T(8,128)(2,1)S(1)}, u32[]{:S(2)}, u32[]{:S(2)}) async-start(bf16[256,24,128]{2,1,0:T(8,128)(2,1)} %bitcast.34), calls=%async_computation.2 | async-start | bytes 3145728 | tf_op jit(solution)/shard_map/all_to_all | solution.py:320
  111.0 5.0 %collective-permute-start.1 = (bf16[6,128]{1,0:T(8,128)(2,1)S(1)}, bf16[6,128]{1,0:T(8,128)(2,1)S(1)}, u32[]{:S(2)}, u32[]{:S(2)}) collective-permute-start(bf16[6,128]{1,0:T(8,128)(2,1)S(1)} %bitcast.39), channel_id=1, source_target_pairs={{0,1},{1,2},{2,3},{3,0},{4,5},{5,6},{6,7},{7,4},{8,9},{9,10},{10,1... | collective-permute-start | bytes 4616 | tf_op jit(solution)/shard_map/ppermute | solution.py:336
  112.4 4.2 %collective-permute-start.2 = (bf16[6,128]{1,0:T(8,128)(2,1)S(1)}, bf16[6,128]{1,0:T(8,128)(2,1)S(1)}, u32[]{:S(2)}, u32[]{:S(2)}) collective-permute-start(bf16[6,128]{1,0:T(8,128)(2,1)S(1)} %bitcast.38), channel_id=1, source_target_pairs={{0,2},{1,3},{2,0},{3,1},{4,6},{5,7},{6,4},{7,5},{8,10},{9,11},{10,... | collective-permute-start | bytes 4616 | tf_op jit(solution)/shard_map/ppermute | solution.py:336
  114.8 2.7 %collective-permute-start.3 = (bf16[6,128]{1,0:T(8,128)(2,1)S(1)}, bf16[6,128]{1,0:T(8,128)(2,1)S(1)}, u32[]{:S(2)}, u32[]{:S(2)}) collective-permute-start(bf16[6,128]{1,0:T(8,128)(2,1)S(1)} %bitcast.37), channel_id=1, source_target_pairs={{0,3},{1,0},{2,1},{3,2},{4,7},{5,4},{6,5},{7,6},{8,11},{9,8},{10,9... | collective-permute-start | bytes 4616 | tf_op jit(solution)/shard_map/ppermute | solution.py:336

commit v4 on v3

v4 whole, which is shorter than its diff:
```python
import jax
import jax.numpy as jnp
from jax import lax
from jax.experimental import pallas as pl
from jax.experimental.pallas import tpu as pltpu
from jax.sharding import PartitionSpec as P

D = 512
HEADS = 4
HEAD = D // HEADS
BLOCK = 128
MAXB = 2
BLK_DEV = 48
USERS = 24
N_DP = 64
N_MP = 4
WIN = MAXB * BLOCK
MINE = USERS // N_MP
TILE = 8
GROUPS = WIN // TILE
HALVES = N_DP // GROUPS
PER_HALF = MINE // HALVES
MSG = PER_HALF * N_MP + 1
EPS = 1e-05
BF16 = jnp.bfloat16
F32 = jnp.float32


def silu_of_twice(h):
    return h + h * jnp.tanh(h)


def project(half_parts, w_parts):
    acc = jnp.dot(half_parts[0], w_parts[0], preferred_element_type=F32)
    for n, w in zip(half_parts[1:], w_parts[1:]):
        acc = acc + jnp.dot(n, w, preferred_element_type=F32)
    proj = silu_of_twice(acc).astype(BF16)
    return [proj[:, j * HEAD : (j + 1) * HEAD] for j in range(4)]


def attend(q, k, v):
    row = lax.broadcasted_iota(jnp.int32, (BLOCK, BLOCK), 0)
    col = lax.broadcasted_iota(jnp.int32, (BLOCK, BLOCK), 1)
    causal = col <= row
    scale = 0.5 * HEAD ** (-0.5)
    contract_last = (((1,), (1,)), ((), ()))
    s0 = lax.dot_general(q[:BLOCK], k[:BLOCK], contract_last, preferred_element_type=F32)
    s1 = lax.dot_general(q[BLOCK:], k, contract_last, preferred_element_type=F32)
    a0 = jnp.where(causal, silu_of_twice(s0 * scale), 0.0).astype(BF16)
    b = silu_of_twice(s1 * scale)
    a1 = jnp.concatenate(
        [b[:, :BLOCK].astype(BF16), jnp.where(causal, b[:, BLOCK:], 0.0).astype(BF16)], axis=1
    )
    return jnp.concatenate(
        [
            jnp.dot(a0, v[:BLOCK], preferred_element_type=F32),
            jnp.dot(a1, v, preferred_element_type=F32),
        ],
        axis=0,
    )


def norm_stats(total, squares, unit=1.0):
    mean = total * (1.0 / D)
    var = squares * (1.0 / D) - mean * mean
    return mean, lax.rsqrt(var * (unit * unit) + EPS) * unit


def in_vmem():
    return pl.BlockSpec(memory_space=pltpu.VMEM)


def in_hbm():
    return pl.BlockSpec(memory_space=pl.ANY)


def keep(array):
    return pltpu.with_memory_space_constraint(array, pltpu.VMEM)


def own_head_kernel(start_ref, x0_ref, x1_ref, w_ref, half_ref, att_ref, gate_ref):
    x = jnp.concatenate([x0_ref[...], x1_ref[...]], axis=0).astype(F32)
    mean, inv = norm_stats(
        jnp.sum(x, axis=1, keepdims=True), jnp.sum(x * x, axis=1, keepdims=True)
    )
    half = ((x - mean) * (inv * 0.5)).astype(BF16)
    half_ref[0] = half
    u, v, q, k = project([half], [w_ref[...]])
    gate_ref[0] = u
    att_ref[0] = attend(q, k, v)


def own_head(tokens, starts, w_own):
    def per_user(width):
        return pl.BlockSpec((1, WIN, width), lambda i, s: (i, 0, 0))

    return pl.pallas_call(
        own_head_kernel,
        grid_spec=pltpu.PrefetchScalarGridSpec(
            num_scalar_prefetch=1,
            grid=(MINE,),
            in_specs=[
                pl.BlockSpec((BLOCK, D), lambda i, s: (s[i], 0)),
                pl.BlockSpec((BLOCK, D), lambda i, s: (jnp.minimum(s[i] + 1, BLK_DEV - 1), 0)),
                pl.BlockSpec((D, D), lambda i, s: (0, 0)),
            ],
            out_specs=[per_user(D), per_user(HEAD), per_user(HEAD)],
        ),
        out_shape=[
            jax.ShapeDtypeStruct((MINE, WIN, D), BF16),
            jax.ShapeDtypeStruct((MINE, WIN, HEAD), F32),
            jax.ShapeDtypeStruct((MINE, WIN, HEAD), BF16),
        ],
        cost_estimate=pl.CostEstimate(
            flops=MINE * WIN * D * D * 64, bytes_accessed=MINE * WIN * D * 8, transcendentals=0
        ),
        name="own_head",
    )(starts, tokens, tokens, w_own)


def layer_kernel(
    start_ref, len_ref, pos_ref,
    tokens_ref, half_hbm, att_hbm, gate_hbm, near_ref, far_ref, w_out_ref, table_ref,
    out_ref, state_ref,
    x_s, half_s, att_s, gate_s, w_out_s, out_s, sem_in, sem_w, sem_out,
):
    part = pos_ref[0]
    low_is_near = pos_ref[1] == 0
    order = [part] + [(part + s) % HEADS for s in range(1, HEADS)]

    def loads(i):
        first = start_ref[i]
        second = jnp.minimum(first + 1, BLK_DEV - 1)
        pairs = [
            (half_hbm.at[i], half_s.at[i]),
            (att_hbm.at[i], att_s.at[i]),
            (gate_hbm.at[i], gate_s.at[i]),
            (tokens_ref.at[pl.ds(first * BLOCK, BLOCK)], x_s.at[i, pl.ds(0, BLOCK)]),
            (tokens_ref.at[pl.ds(second * BLOCK, BLOCK)], x_s.at[i, pl.ds(BLOCK, BLOCK)]),
        ]
        return [pltpu.make_async_copy(a, b, sem_in.at[i, j]) for j, (a, b) in enumerate(pairs)]

    weights = [
        pltpu.make_async_copy(
            w_out_ref.at[pl.ds(h * HEAD, HEAD)], w_out_s.at[pl.ds(s * HEAD, HEAD)], sem_w.at[s]
        )
        for s, h in enumerate(order)
    ]

    def sends(i):
        at = (i // PER_HALF, slice(None), pl.ds((i % PER_HALF) * N_MP, N_MP))
        return pltpu.make_async_copy(out_s.at[at], out_ref.at[at], sem_out.at[i])

    def send_table(half):
        at = (half, slice(None), pl.ds(MSG - 1, 1))
        return pltpu.make_async_copy(out_s.at[at], out_ref.at[at], sem_out.at[MINE + half])

    for copy in loads(0):
        copy.start()
    for i in range(1, MINE):
        for copy in loads(i):
            copy.start()
        if i == 1:
            for copy in weights:
                copy.start()
    tile = jnp.broadcast_to(table_ref[...], (TILE, 128)).astype(F32).astype(BF16)
    for half in range(HALVES):
        out_s[half, :, MSG - 1] = jnp.broadcast_to(tile[None], (GROUPS, TILE, 128))
        send_table(half).start()

    def user(i, carry):
        length = len_ref[i]
        half_id = i // PER_HALF
        base = (i % PER_HALF) * N_MP
        for copy in loads(i):
            copy.wait()
        low = half_s[i, :, : D // 2]
        high = half_s[i, :, D // 2 :]
        parts = [jnp.where(low_is_near, low, high), jnp.where(low_is_near, high, low)]
        heads, gates = [att_s[i]], [gate_s[i]]
        for h in order[1:]:
            u, v, q, k = project(parts, [near_ref[h], far_ref[h]])
            gates.append(u)
            heads.append(attend(q, k, v))
        total = jnp.sum(heads[0] + heads[1] + (heads[2] + heads[3]), axis=1, keepdims=True)
        squares = jnp.sum(
            heads[0] * heads[0] + heads[1] * heads[1] + (heads[2] * heads[2] + heads[3] * heads[3]),
            axis=1,
            keepdims=True,
        )
        mean, inv = norm_stats(total, squares, 1.0 / WIN)
        gated = jnp.concatenate(
            [((a - mean) * inv * g.astype(F32)).astype(BF16) for a, g in zip(heads, gates)], axis=1
        )

        @pl.when(i == 0)
        def _():
            for copy in weights:
                copy.wait()

        mixed = jnp.dot(gated, w_out_s[...], preferred_element_type=F32) + x_s[i].astype(F32)
        at = lax.broadcasted_iota(jnp.int32, (WIN, 1), 0)
        mixed = jnp.where(at < length, mixed, 0.0).astype(BF16)
        for q in range(N_MP):
            out_s[half_id, :, base + q] = mixed[:, q * HEAD : (q + 1) * HEAD].reshape(
                GROUPS, TILE, HEAD
            )
        sends(i).start()
        last = length - 1
        pick = lax.broadcasted_iota(jnp.int32, (TILE, HEAD), 0) == last % TILE
        for q in range(N_MP):
            tile = out_s[half_id, last // TILE, base + q].astype(F32)
            state_ref[i, :, q * HEAD : (q + 1) * HEAD] = jnp.sum(
                jnp.where(pick, tile, 0.0), axis=0, keepdims=True
            ).astype(BF16)
        return carry

    lax.fori_loop(0, MINE, user, 0)
    for half in range(HALVES):
        send_table(half).wait()
    for i in range(MINE):
        sends(i).wait()


def layer(tokens, starts, lengths, position, kept, near, far, w_out, table):
    message = (HALVES, GROUPS, MSG, TILE, HEAD)
    return pl.pallas_call(
        layer_kernel,
        grid_spec=pltpu.PrefetchScalarGridSpec(
            num_scalar_prefetch=3,
            grid=(1,),
            in_specs=[in_hbm()] * 4 + [in_vmem()] * 2 + [in_hbm(), in_vmem()],
            out_specs=[in_hbm(), in_vmem()],
            scratch_shapes=[
                pltpu.VMEM((MINE, WIN, D), BF16),
                pltpu.VMEM((MINE, WIN, D), BF16),
                pltpu.VMEM((MINE, WIN, HEAD), F32),
                pltpu.VMEM((MINE, WIN, HEAD), BF16),
                pltpu.VMEM((D, D), BF16),
                pltpu.VMEM(message, BF16),
                pltpu.SemaphoreType.DMA((MINE, 5)),
                pltpu.SemaphoreType.DMA((HEADS,)),
                pltpu.SemaphoreType.DMA((MINE + HALVES,)),
            ],
        ),
        out_shape=[
            jax.ShapeDtypeStruct(message, BF16),
            jax.ShapeDtypeStruct((MINE, 1, D), BF16),
        ],
        name="layer",
    )(starts, lengths, position, tokens, *kept, keep(near), keep(far), w_out, table)


def regroup_kernel(first_ref, in_ref, out_ref, table_v, table_s, sem):
    table = jnp.max(in_ref[:, PER_HALF * N_MP].astype(F32), axis=1)
    table_v[...] = table.astype(jnp.int32)
    copy = pltpu.make_async_copy(table_v, table_s, sem)
    copy.start()
    copy.wait()
    first = first_ref[0]

    def one(d, carry):
        for k in range(PER_HALF):
            o = table_s[d, first + k]
            for q in range(N_MP):
                out_ref[o, q, k] = in_ref[d, k * N_MP + q]
        return carry

    lax.fori_loop(0, N_DP, one, 0, unroll=8)


def regroup(spread, first):
    return pl.pallas_call(
        regroup_kernel,
        grid_spec=pltpu.PrefetchScalarGridSpec(
            num_scalar_prefetch=1,
            grid=(1,),
            in_specs=[in_vmem()],
            out_specs=pl.BlockSpec(
                (N_DP, N_MP, PER_HALF, TILE, HEAD), lambda i, s: (0, 0, 0, 0, 0)
            ),
            scratch_shapes=[
                pltpu.VMEM((N_DP, 128), jnp.int32),
                pltpu.SMEM((N_DP, 128), jnp.int32),
                pltpu.SemaphoreType.DMA,
            ],
        ),
        out_shape=jax.ShapeDtypeStruct((N_DP, N_MP, PER_HALF, TILE, HEAD), BF16),
        name="regroup",
    )(first, keep(spread))


def place_kernel(len_ref, off_ref, in_ref, out_ref, zero_v, used_s, sem):
    per_block = BLOCK // TILE
    zero_v[...] = jnp.zeros_like(zero_v)

    def clear(b, carry):
        used_s[b] = 0
        return carry

    lax.fori_loop(0, BLK_DEV, clear, 0, unroll=8)

    def send(u, j):
        half = (u % MINE) // PER_HALF
        block = off_ref[u] + j
        used_s[block] = 1
        pltpu.make_async_copy(
            in_ref.at[half, pl.ds(j * per_block, per_block), u // MINE, u % PER_HALF],
            out_ref.at[pl.ds(block * per_block, per_block)],
            sem,
        ).start()

    def one(u, carry):
        send(u, 0)

        @pl.when(len_ref[u] > BLOCK)
        def _():
            send(u, 1)

        return carry

    lax.fori_loop(0, USERS, one, 0)

    def fill(b, carry):
        @pl.when(used_s[b] == 0)
        def _():
            pltpu.make_async_copy(zero_v, out_ref.at[pl.ds(b * per_block, per_block)], sem).start()

        return carry

    lax.fori_loop(0, BLK_DEV, fill, 0)
    pltpu.make_async_copy(out_ref, out_ref, sem).wait()


def place(arrived, lengths, offsets):
    rows = BLK_DEV * BLOCK
    return pl.pallas_call(
        place_kernel,
        grid_spec=pltpu.PrefetchScalarGridSpec(
            num_scalar_prefetch=2,
            grid=(1,),
            in_specs=[in_vmem()],
            out_specs=in_hbm(),
            scratch_shapes=[
                pltpu.VMEM((BLOCK // TILE, TILE, HEAD), BF16),
                pltpu.SMEM((BLK_DEV,), jnp.int32),
                pltpu.SemaphoreType.DMA,
            ],
        ),
        out_shape=jax.ShapeDtypeStruct((rows // TILE, TILE, HEAD), BF16),
        name="place",
    )(lengths, offsets, keep(arrived)).reshape(rows, HEAD)


def per_device(tokens, w_uvqk, w_out, hist_len, owner, recv_offset, block_start):
    me = lax.axis_index("dp")
    part = lax.axis_index("mp")
    first = part * MINE

    core = me % 2
    half = D // 2
    mine_rows = jnp.where(core == 0, w_uvqk[:half], w_uvqk[half:])
    near = lax.all_to_all(
        jnp.broadcast_to(mine_rows[None], (N_MP, half, D)), "mp", 0, 0, tiled=True
    )
    far = lax.ppermute(near, "dp", [(i, i ^ 1) for i in range(N_DP)])
    table = jnp.concatenate([owner, hist_len, recv_offset, jnp.zeros((1, 56), jnp.int32)], axis=1)
    starts = lax.dynamic_slice_in_dim(block_start[0], first, MINE, 0)
    lengths = lax.dynamic_slice_in_dim(hist_len[0], first, MINE, 0)
    kept = own_head(tokens, starts, w_uvqk)
    mixed, last = layer(
        tokens, starts, lengths, jnp.stack([part, core]), kept, near, far, w_out, table
    )

    spread = lax.all_to_all(
        mixed.reshape(N_DP, MSG * TILE, HEAD), "dp", 0, 0, tiled=True
    ).reshape(N_DP, MSG, TILE, HEAD)
    held = first + (me // GROUPS) * PER_HALF
    sorted_rows = regroup(spread, held[None])
    table = spread[:, MSG - 1, 0, :].astype(jnp.int32)
    owners = table[:, :USERS]
    arrived = lax.all_to_all(
        sorted_rows.reshape(N_DP * N_MP, PER_HALF * TILE, HEAD), ("dp", "mp"), 0, 0, tiled=True
    )
    mine = owners == me
    recv_len = jnp.sum(jnp.where(mine, table[:, USERS : 2 * USERS], 0), axis=0)
    recv_off = jnp.sum(jnp.where(mine, table[:, 2 * USERS : 3 * USERS], 0), axis=0)
    packed = place(
        arrived.reshape(HALVES, GROUPS, N_MP, PER_HALF, TILE, HEAD), recv_len, recv_off
    )

    columns = last.reshape(MINE, N_MP, HEAD)
    state = jnp.zeros((N_MP, MINE, HEAD), BF16)
    for s in range(N_MP):
        to = (part + s) % N_MP
        piece = lax.dynamic_slice_in_dim(columns, to, 1, 1)[:, 0]
        if s:
            piece = lax.ppermute(piece, "mp", [(i, (i + s) % N_MP) for i in range(N_MP)])
        state = lax.dynamic_update_slice_in_dim(state, piece[None], (part - s) % N_MP, 0)
    return packed, state.reshape(USERS, HEAD)


def solution(mesh):
    in_specs = (
        P("dp", None),
        P(None, "mp"),
        P(),
        P("dp", None),
        P("dp", None),
        P("dp", None),
        P("dp", None),
    )
    out_specs = (P("dp", "mp"), P("dp", "mp"))
    return jax.shard_map(
        per_device, mesh=mesh, in_specs=in_specs, out_specs=out_specs, check_vma=False
    )
```

time: 157 us -> 157 us (level)
  no operation moved by 1% of the time
where the time goes in v4:
time: 157 us; the launch traced here: 156 us
  waiting for transfers between devices  89.8 us (57%)
  starting transfers between devices  31.5 us (20%)
  Pallas kernels  28.5 us (18%)
  other arithmetic  3.02 us (2%)
  local copies, waits for them, and re-layouts  2.43 us (2%)
    all_to_all x1, waiting for transfers between devices, per_device(): lax.all_to_all(mixed.reshape(N_DP, MSG * TILE, HEAD), 'dp', 0, 0, tiled=T...  41.7 us
    all_to_all x1, waiting for transfers between devices, per_device(): lax.all_to_all(sorted_rows.reshape(N_DP * N_MP, PER_HALF * TILE, HEAD), (...  33.9 us
    pallas_call x1, Pallas kernels, layer(): pl.pallas_call(layer_kernel, grid_spec=pltpu.PrefetchScalarGridSpec(num_s...  15.9 us
    all_to_all x1, waiting for transfers between devices, per_device(): lax.all_to_all(jnp.broadcast_to(mine_rows[None], (N_MP, half, D)), 'mp',...  12.7 us
    all_to_all x1, starting transfers between devices, per_device(): lax.all_to_all(mixed.reshape(N_DP, MSG * TILE, HEAD), 'dp', 0, 0, tiled=T...  11.8 us
    pallas_call x1, Pallas kernels, own_head(): pl.pallas_call(own_head_kernel, grid_spec=pltpu.PrefetchScalarGridSpec(nu...  7.66 us
    all_to_all x1, starting transfers between devices, per_device(): lax.all_to_all(sorted_rows.reshape(N_DP * N_MP, PER_HALF * TILE, HEAD), (...  7.16 us
    ppermute x3, starting transfers between devices, per_device(): lax.ppermute(piece, 'mp', [(i, (i + s) % N_MP) for i in range(N_MP)])  5.01 us
  transfers between devices with their start and end apart: 7, of which 5 were waited for; matrix products, arithmetic and copies ran while one was open for 2% of the time, Pallas kernels for 5%

profile of v4, /device:TPU:1, one launch (start us, length us, event | category | flops | bytes accessed | tf_op | source)
XLA Modules:
  0.0 156.1 jit_solution(17136912826886670720)
XLA Ops:
  0.6 1.1 slice_select_fusion
  1.7 0.0 copy-start.1
  1.7 0.0 copy-start.2
  1.7 1.1 broadcast_in_dim.29
  2.8 4.8 %all-to-all-start = ((bf16[4,256,512]{2,1,0:T(8,128)(2,1)}), bf16[4,256,512]{2,1,0:T(8,128)(2,1)S(1)}, u32[]{:S(2)}, u32[]{:S(2)}) async-start(bf16[4,256,512]{2,1,0:T(8,128)(2,1)} %broadcast_in_dim.29), calls=%async_computation | async-start | bytes 2097152 | tf_op jit(solution)/shard_map/all_to_all | solution.py:363
  7.6 0.0 copy-done.1
  7.6 0.0 copy-done.2
  7.6 0.7 fusion.2
  8.3 12.7 %all-to-all-done.near_ref = bf16[4,256,512]{2,1,0:T(8,128)(2,1)S(1)} async-done(((bf16[4,256,512]{2,1,0:T(8,128)(2,1)}), bf16[4,256,512]{2,1,0:T(8,128)(2,1)S(1)}, u32[]{:S(2)}, u32[]{:S(2)}) %all-to-all-start) | async-done | bytes 1048608 | tf_op jit(solution)/shard_map/all_to_all | solution.py:363
  21.0 2.7 %collective-permute-start = (bf16[4,256,512]{2,1,0:T(8,128)(2,1)S(1)}, bf16[4,256,512]{2,1,0:T(8,128)(2,1)S(1)}, u32[]{:S(2)}, u32[]{:S(2)}) collective-permute-start(bf16[4,256,512]{2,1,0:T(8,128)(2,1)S(1)} %all-to-all-done.near_ref), channel_id=1, source_target_pairs={{0,4},{4,0},{8,12},{12,8},{16,20},{20,16},{24,28},{28,24},{32,36},... | collective-permute-start | bytes 3145736 | tf_op jit(solution)/shard_map/ppermute | solution.py:366
  23.7 0.0 copy-start.3
  23.7 0.0 copy-start.4
  23.7 7.7 %own_head.1 = (bf16[6,256,512]{2,1,0:T(8,128)(2,1)}, f32[6,256,128]{2,1,0:T(8,128)}, bf16[6,256,128]{2,1,0:T(8,128)(2,1)}) custom-call(s32[6]{0:T(128)} %get-tuple-element.18.start_ref, bf16[6144,512]{1,0:T(8,128)(2,1)} %tokens_ref.1, bf16[6144,512]{1,0:T(8,128)(2,1)} %tokens_ref.1, bf16[512,512]{1,0:T(8,128)(2,1)} %w_ref.1), custom_call_target="tpu_custom_call" | custom-call | flops 25769803776 | bytes 6291456 | tf_op jit(solution)/shard_map/own_head/pallas_call | solution.py:97
  31.3 0.7 pad_add_fusion.pos_ref
  32.0 0.0 copy-done.3
  32.0 0.0 copy-done.4
  32.0 0.6 bitcast_add_fusion.table_ref
  32.6 0.0 collective-permute-done.far_ref
  32.6 15.9 %layer.1 = (bf16[2,32,13,8,128]{4,3,2,1,0:T(8,128)(2,1)}, bf16[6,1,512]{2,1,0:T(2,128)(2,1)}) custom-call(s32[6]{0:T(128)} %get-tuple-element.18.start_ref, s32[6]{0:T(128)} %get-tuple-element.19.len_ref, s32[2]{0:T(128)} %pad_add_fusion.pos_ref, bf16[6144,512]{1,0:T(8,128)(2,1)} %tokens_ref.1, bf16[6,256,512]{2,1,0:T(8,128)(2,1)} %get-tuple-element.7.half_hbm, ...), custom_call_target="tpu_custom_call" | custom-call | tf_op jit(solution)/shard_map/layer/pallas_call | solution.py:227
  48.4 11.8 %all-to-all-start.1 = ((bf16[64,104,128]{2,1,0:T(8,128)(2,1)}), bf16[64,104,128]{2,1,0:T(8,128)(2,1)S(1)}, u32[]{:S(2)}, u32[]{:S(2)}) async-start(bf16[64,104,128]{2,1,0:T(8,128)(2,1)} %bitcast.36), calls=%async_computation.1 | async-start | bytes 3407872 | tf_op jit(solution)/shard_map/all_to_all | solution.py:375
  60.2 41.7 %all-to-all-done.1 = bf16[64,104,128]{2,1,0:T(8,128)(2,1)S(1)} async-done(((bf16[64,104,128]{2,1,0:T(8,128)(2,1)}), bf16[64,104,128]{2,1,0:T(8,128)(2,1)S(1)}, u32[]{:S(2)}, u32[]{:S(2)}) %all-to-all-start.1) | async-done | bytes 1703968 | tf_op jit(solution)/shard_map/all_to_all | solution.py:375
  101.9 2.9 %regroup.1 = bf16[64,4,3,8,128]{4,3,2,1,0:T(8,128)(2,1)} custom-call(s32[1]{0:T(128)} %bitcast.7.first_ref, bf16[64,13,8,128]{3,2,1,0:T(8,128)(2,1)S(1)} %bitcast.32), custom_call_target="tpu_custom_call" | custom-call | tf_op jit(solution)/shard_map/regroup/pallas_call | solution.py:273
  104.8 0.0 copy-start
  104.8 7.2 %all-to-all-start.2 = ((bf16[256,24,128]{2,1,0:T(8,128)(2,1)}), bf16[256,24,128]{2,1,0:T(8,128)(2,1)S(1)}, u32[]{:S(2)}, u32[]{:S(2)}) async-start(bf16[256,24,128]{2,1,0:T(8,128)(2,1)} %bitcast.35), calls=%async_computation.2 | async-start | bytes 3145728 | tf_op jit(solution)/shard_map/all_to_all | solution.py:382
  112.1 0.0 copy-done
  112.2 1.4 collective-permute-start.1
  113.7 2.4 %collective-permute-start.2 = (bf16[6,128]{1,0:T(8,128)(2,1)S(1)}, bf16[6,128]{1,0:T(8,128)(2,1)S(1)}, u32[]{:S(2)}, u32[]{:S(2)}) collective-permute-start(bf16[6,128]{1,0:T(8,128)(2,1)S(1)} %bitcast.40), channel_id=1, source_target_pairs={{0,2},{1,3},{2,0},{3,1},{4,6},{5,7},{6,4},{7,5},{8,10},{9,11},{10,... | collective-permute-start | bytes 4616 | tf_op jit(solution)/shard_map/ppermute | solution.py:398
  116.1 1.2 collective-permute-start.3
  117.3 0.0 collective-permute-done.1
  117.3 0.6 collective-permute-done.2
  117.9 0.9 collective-permute-done.3
  118.8 0.6 reshape.36
  119.4 0.7 fusion
  120.1 33.9 %all-to-all-done.2 = bf16[256,24,128]{2,1,0:T(8,128)(2,1)S(1)} async-done(((bf16[256,24,128]{2,1,0:T(8,128)(2,1)}), bf16[256,24,128]{2,1,0:T(8,128)(2,1)S(1)}, u32[]{:S(2)}, u32[]{:S(2)}) %all-to-all-start.2) | async-done | bytes 1572896 | tf_op jit(solution)/shard_map/all_to_all | solution.py:382
  154.0 2.1 %place.1 = bf16[768,8,128]{2,1,0:T(8,128)(2,1)} custom-call(s32[24]{0:T(128)} %get-tuple-element.13.len_ref, s32[24]{0:T(128)} %get-tuple-element.12.off_ref, bf16[2,32,4,3,8,128]{5,4,3,2,1,0:T(8,128)(2,1)S(1)} %bitcast.34), custom_call_target="tpu_custom_call" | custom-call | tf_op jit(solution)/shard_map/place/pallas_call | solution.py:337
  (13 shorter events, 0.2 us)
Async XLA Ops:
  1.7 5.9 %copy-start.1 = (s32[1,24]{1,0:T(1,128)S(1)}, s32[1,24]{1,0:T(1,128)}, u32[]{:S(2)}) copy-start(s32[1,24]{1,0:T(1,128)} %param.10) | copy-start | bytes 292
  1.7 5.9 %copy-start.2 = (s32[1,24]{1,0:T(1,128)S(1)}, s32[1,24]{1,0:T(1,128)}, u32[]{:S(2)}) copy-start(s32[1,24]{1,0:T(1,128)} %param.13) | copy-start | bytes 292
  2.8 18.2 %all-to-all-start = ((bf16[4,256,512]{2,1,0:T(8,128)(2,1)}), bf16[4,256,512]{2,1,0:T(8,128)(2,1)S(1)}, u32[]{:S(2)}, u32[]{:S(2)}) async-start(bf16[4,256,512]{2,1,0:T(8,128)(2,1)} %broadcast_in_dim.29), calls=%async_computation | async-start | bytes 2097152 | tf_op jit(solution)/shard_map/all_to_all | solution.py:363
  21.0 11.6 %collective-permute-start = (bf16[4,256,512]{2,1,0:T(8,128)(2,1)S(1)}, bf16[4,256,512]{2,1,0:T(8,128)(2,1)S(1)}, u32[]{:S(2)}, u32[]{:S(2)}) collective-permute-start(bf16[4,256,512]{2,1,0:T(8,128)(2,1)S(1)} %all-to-all-done.near_ref), channel_id=1, source_target_pairs={{0,4},{4,0},{8,12},{12,8},{16,20},{20,16},{24,28},{28,24},{32,36},... | collective-permute-start | bytes 3145736 | tf_op jit(solution)/shard_map/ppermute | solution.py:366
  23.7 8.3 %copy-start.3 = (s32[1,24]{1,0:T(1,128)S(1)}, s32[1,24]{1,0:T(1,128)}, u32[]{:S(2)}) copy-start(s32[1,24]{1,0:T(1,128)} %param.12) | copy-start | bytes 292
  23.7 8.3 %copy-start.4 = (s32[1,24]{1,0:T(1,128)S(1)}, s32[1,24]{1,0:T(1,128)}, u32[]{:S(2)}) copy-start(s32[1,24]{1,0:T(1,128)} %param.11) | copy-start | bytes 292
  48.4 53.5 %all-to-all-start.1 = ((bf16[64,104,128]{2,1,0:T(8,128)(2,1)}), bf16[64,104,128]{2,1,0:T(8,128)(2,1)S(1)}, u32[]{:S(2)}, u32[]{:S(2)}) async-start(bf16[64,104,128]{2,1,0:T(8,128)(2,1)} %bitcast.36), calls=%async_computation.1 | async-start | bytes 3407872 | tf_op jit(solution)/shard_map/all_to_all | solution.py:375
  104.8 7.3 %copy-start = (bf16[6,1,512]{2,1,0:T(2,128)(2,1)S(1)}, bf16[6,1,512]{2,1,0:T(2,128)(2,1)}, u32[]{:S(2)}) copy-start(bf16[6,1,512]{2,1,0:T(2,128)(2,1)} %get-tuple-element.11) | copy-start | bytes 18436
  104.8 49.2 %all-to-all-start.2 = ((bf16[256,24,128]{2,1,0:T(8,128)(2,1)}), bf16[256,24,128]{2,1,0:T(8,128)(2,1)S(1)}, u32[]{:S(2)}, u32[]{:S(2)}) async-start(bf16[256,24,128]{2,1,0:T(8,128)(2,1)} %bitcast.35), calls=%async_computation.2 | async-start | bytes 3145728 | tf_op jit(solution)/shard_map/all_to_all | solution.py:382
  112.2 5.0 %collective-permute-start.1 = (bf16[6,128]{1,0:T(8,128)(2,1)S(1)}, bf16[6,128]{1,0:T(8,128)(2,1)S(1)}, u32[]{:S(2)}, u32[]{:S(2)}) collective-permute-start(bf16[6,128]{1,0:T(8,128)(2,1)S(1)} %bitcast.41), channel_id=1, source_target_pairs={{0,1},{1,2},{2,3},{3,0},{4,5},{5,6},{6,7},{7,4},{8,9},{9,10},{10,1... | collective-permute-start | bytes 4616 | tf_op jit(solution)/shard_map/ppermute | solution.py:398
  113.7 4.2 %collective-permute-start.2 = (bf16[6,128]{1,0:T(8,128)(2,1)S(1)}, bf16[6,128]{1,0:T(8,128)(2,1)S(1)}, u32[]{:S(2)}, u32[]{:S(2)}) collective-permute-start(bf16[6,128]{1,0:T(8,128)(2,1)S(1)} %bitcast.40), channel_id=1, source_target_pairs={{0,2},{1,3},{2,0},{3,1},{4,6},{5,7},{6,4},{7,5},{8,10},{9,11},{10,... | collective-permute-start | bytes 4616 | tf_op jit(solution)/shard_map/ppermute | solution.py:398
  116.1 2.7 %collective-permute-start.3 = (bf16[6,128]{1,0:T(8,128)(2,1)S(1)}, bf16[6,128]{1,0:T(8,128)(2,1)S(1)}, u32[]{:S(2)}, u32[]{:S(2)}) collective-permute-start(bf16[6,128]{1,0:T(8,128)(2,1)S(1)} %bitcast.39), channel_id=1, source_target_pairs={{0,3},{1,0},{2,1},{3,2},{4,7},{5,4},{6,5},{7,6},{8,11},{9,8},{10,9... | collective-permute-start | bytes 4616 | tf_op jit(solution)/shard_map/ppermute | solution.py:398

commit v5 on v4

--- a/solution.py
+++ b/solution.py
@@ -21,6 +21,7 @@
 HALVES = N_DP // GROUPS
 PER_HALF = MINE // HALVES
 MSG = PER_HALF * N_MP + 1
+GROUP = 3
 EPS = 1e-05
 BF16 = jnp.bfloat16
 F32 = jnp.float32
@@ -118,6 +119,30 @@
     )(starts, tokens, tokens, w_own)
 
 
+def copies_kernel(core_ref, w_ref, out_ref, sem):
+    rows = w_ref.at[pl.ds(core_ref[0] * (D // 2), D // 2)]
+    copies = [pltpu.make_async_copy(rows, out_ref.at[j], sem.at[j]) for j in range(N_MP)]
+    for copy in copies:
+        copy.start()
+    for copy in copies:
+        copy.wait()
+
+
+def copies_of_half(w_own, core):
+    return pl.pallas_call(
+        copies_kernel,
+        grid_spec=pltpu.PrefetchScalarGridSpec(
+            num_scalar_prefetch=1,
+            grid=(1,),
+            in_specs=[in_hbm()],
+            out_specs=in_hbm(),
+            scratch_shapes=[pltpu.SemaphoreType.DMA((N_MP,))],
+        ),
+        out_shape=jax.ShapeDtypeStruct((N_MP, D // 2, D), BF16),
+        name="copies",
+    )(core, w_own)
+
+
 def layer_kernel(
     start_ref, len_ref, pos_ref,
     tokens_ref, half_hbm, att_hbm, gate_hbm, near_ref, far_ref, w_out_ref, table_ref,
@@ -132,11 +157,11 @@
         first = start_ref[i]
         second = jnp.minimum(first + 1, BLK_DEV - 1)
         pairs = [
-            (half_hbm.at[i], half_s.at[i]),
-            (att_hbm.at[i], att_s.at[i]),
-            (gate_hbm.at[i], gate_s.at[i]),
-            (tokens_ref.at[pl.ds(first * BLOCK, BLOCK)], x_s.at[i, pl.ds(0, BLOCK)]),
-            (tokens_ref.at[pl.ds(second * BLOCK, BLOCK)], x_s.at[i, pl.ds(BLOCK, BLOCK)]),
+            (half_hbm.at[i], half_s.at[pl.ds(i * WIN, WIN)]),
+            (att_hbm.at[i], att_s.at[pl.ds(i * WIN, WIN)]),
+            (gate_hbm.at[i], gate_s.at[pl.ds(i * WIN, WIN)]),
+            (tokens_ref.at[pl.ds(first * BLOCK, BLOCK)], x_s.at[pl.ds(i * WIN, BLOCK)]),
+            (tokens_ref.at[pl.ds(second * BLOCK, BLOCK)], x_s.at[pl.ds(i * WIN + BLOCK, BLOCK)]),
         ]
         return [pltpu.make_async_copy(a, b, sem_in.at[i, j]) for j, (a, b) in enumerate(pairs)]
 
@@ -168,20 +193,28 @@
         out_s[half, :, MSG - 1] = jnp.broadcast_to(tile[None], (GROUPS, TILE, 128))
         send_table(half).start()
 
-    def user(i, carry):
-        length = len_ref[i]
-        half_id = i // PER_HALF
-        base = (i % PER_HALF) * N_MP
-        for copy in loads(i):
-            copy.wait()
-        low = half_s[i, :, : D // 2]
-        high = half_s[i, :, D // 2 :]
+    def group(step, carry):
+        first_user = step * GROUP
+        for j in range(GROUP):
+            for copy in loads(first_user + j):
+                copy.wait()
+        rows = pl.ds(pl.multiple_of(first_user * WIN, WIN), GROUP * WIN)
+        low = half_s[rows, : D // 2]
+        high = half_s[rows, D // 2 :]
         parts = [jnp.where(low_is_near, low, high), jnp.where(low_is_near, high, low)]
-        heads, gates = [att_s[i]], [gate_s[i]]
+        heads, gates = [att_s[rows, :]], [gate_s[rows, :]]
         for h in order[1:]:
             u, v, q, k = project(parts, [near_ref[h], far_ref[h]])
             gates.append(u)
-            heads.append(attend(q, k, v))
+            heads.append(
+                jnp.concatenate(
+                    [
+                        attend(*(t[j * WIN : (j + 1) * WIN] for t in (q, k, v)))
+                        for j in range(GROUP)
+                    ],
+                    axis=0,
+                )
+            )
         total = jnp.sum(heads[0] + heads[1] + (heads[2] + heads[3]), axis=1, keepdims=True)
         squares = jnp.sum(
             heads[0] * heads[0] + heads[1] * heads[1] + (heads[2] * heads[2] + heads[3] * heads[3]),
@@ -193,29 +226,34 @@
             [((a - mean) * inv * g.astype(F32)).astype(BF16) for a, g in zip(heads, gates)], axis=1
         )
 
-        @pl.when(i == 0)
+        @pl.when(step == 0)
         def _():
             for copy in weights:
                 copy.wait()
 
-        mixed = jnp.dot(gated, w_out_s[...], preferred_element_type=F32) + x_s[i].astype(F32)
+        both = jnp.dot(gated, w_out_s[...], preferred_element_type=F32) + x_s[rows, :].astype(F32)
         at = lax.broadcasted_iota(jnp.int32, (WIN, 1), 0)
-        mixed = jnp.where(at < length, mixed, 0.0).astype(BF16)
-        for q in range(N_MP):
-            out_s[half_id, :, base + q] = mixed[:, q * HEAD : (q + 1) * HEAD].reshape(
-                GROUPS, TILE, HEAD
-            )
-        sends(i).start()
-        last = length - 1
-        pick = lax.broadcasted_iota(jnp.int32, (TILE, HEAD), 0) == last % TILE
-        for q in range(N_MP):
-            tile = out_s[half_id, last // TILE, base + q].astype(F32)
-            state_ref[i, :, q * HEAD : (q + 1) * HEAD] = jnp.sum(
-                jnp.where(pick, tile, 0.0), axis=0, keepdims=True
-            ).astype(BF16)
+        for j in range(GROUP):
+            i = first_user + j
+            length = len_ref[i]
+            half_id = i // PER_HALF
+            base = (i % PER_HALF) * N_MP
+            mixed = jnp.where(at < length, both[j * WIN : (j + 1) * WIN], 0.0).astype(BF16)
+            for q in range(N_MP):
+                out_s[half_id, :, base + q] = mixed[:, q * HEAD : (q + 1) * HEAD].reshape(
+                    GROUPS, TILE, HEAD
+                )
+            sends(i).start()
+            last = length - 1
+            pick = lax.broadcasted_iota(jnp.int32, (TILE, HEAD), 0) == last % TILE
+            for q in range(N_MP):
+                tile = out_s[half_id, last // TILE, base + q].astype(F32)
+                state_ref[i, :, q * HEAD : (q + 1) * HEAD] = jnp.sum(
+                    jnp.where(pick, tile, 0.0), axis=0, keepdims=True
+                ).astype(BF16)
         return carry
 
-    lax.fori_loop(0, MINE, user, 0)
+    lax.fori_loop(0, MINE // GROUP, group, 0)
     for half in range(HALVES):
         send_table(half).wait()
     for i in range(MINE):
@@ -232,10 +270,10 @@
             in_specs=[in_hbm()] * 4 + [in_vmem()] * 2 + [in_hbm(), in_vmem()],
             out_specs=[in_hbm(), in_vmem()],
             scratch_shapes=[
-                pltpu.VMEM((MINE, WIN, D), BF16),
-                pltpu.VMEM((MINE, WIN, D), BF16),
-                pltpu.VMEM((MINE, WIN, HEAD), F32),
-                pltpu.VMEM((MINE, WIN, HEAD), BF16),
+                pltpu.VMEM((MINE * WIN, D), BF16),
+                pltpu.VMEM((MINE * WIN, D), BF16),
+                pltpu.VMEM((MINE * WIN, HEAD), F32),
+                pltpu.VMEM((MINE * WIN, HEAD), BF16),
                 pltpu.VMEM((D, D), BF16),
                 pltpu.VMEM(message, BF16),
                 pltpu.SemaphoreType.DMA((MINE, 5)),
@@ -358,10 +396,8 @@
     first = part * MINE
 
     core = me % 2
-    half = D // 2
-    mine_rows = jnp.where(core == 0, w_uvqk[:half], w_uvqk[half:])
     near = lax.all_to_all(
-        jnp.broadcast_to(mine_rows[None], (N_MP, half, D)), "mp", 0, 0, tiled=True
+        copies_of_half(w_uvqk, core[None]), "mp", 0, 0, tiled=True
     )
     far = lax.ppermute(near, "dp", [(i, i ^ 1) for i in range(N_DP)])
     table = jnp.concatenate([owner, hist_len, recv_offset, jnp.zeros((1, 56), jnp.int32)], axis=1)

time: 157 us -> 184 us (1.17)
  Pallas kernels: 28.5 us -> 57.7 us
    pallas_call x0 -> x1, Pallas kernels: none -> 32.9 us  [copies_of_half(): pl.pallas_call(copies_kernel, grid_spec=pltpu.PrefetchScalarGridSpec(num_...]
    pallas_call x1, Pallas kernels: 15.9 us -> 12.2 us  [layer(): pl.pallas_call(layer_kernel, grid_spec=pltpu.PrefetchScalarGridSpec(num_s...]
  transfers between devices with their start and end apart: 7 -> 7, of which waited for: 5 -> 5; matrix products, arithmetic and copies ran while one was open for 2% -> 2% of each run, Pallas kernels for 5% -> 4%
where the time goes in v5:
time: 184 us; the launch traced here: 183 us
  waiting for transfers between devices  89.8 us (49%)
  Pallas kernels  57.7 us (31%)
  starting transfers between devices  31.6 us (17%)
  other arithmetic  1.96 us (1%)
    all_to_all x1, waiting for transfers between devices, per_device(): lax.all_to_all(mixed.reshape(N_DP, MSG * TILE, HEAD), 'dp', 0, 0, tiled=T...  41.7 us
    all_to_all x1, waiting for transfers between devices, per_device(): lax.all_to_all(sorted_rows.reshape(N_DP * N_MP, PER_HALF * TILE, HEAD), (...  33.9 us
    pallas_call x1, Pallas kernels, copies_of_half(): pl.pallas_call(copies_kernel, grid_spec=pltpu.PrefetchScalarGridSpec(num_...  32.9 us
    all_to_all x1, waiting for transfers between devices, per_device(): lax.all_to_all(copies_of_half(w_uvqk, core[None]), 'mp', 0, 0, tiled=True)  12.7 us
    pallas_call x1, Pallas kernels, layer(): pl.pallas_call(layer_kernel, grid_spec=pltpu.PrefetchScalarGridSpec(num_s...  12.2 us
    all_to_all x1, starting transfers between devices, per_device(): lax.all_to_all(mixed.reshape(N_DP, MSG * TILE, HEAD), 'dp', 0, 0, tiled=T...  11.8 us
    pallas_call x1, Pallas kernels, own_head(): pl.pallas_call(own_head_kernel, grid_spec=pltpu.PrefetchScalarGridSpec(nu...  7.66 us
    all_to_all x1, starting transfers between devices, per_device(): lax.all_to_all(sorted_rows.reshape(N_DP * N_MP, PER_HALF * TILE, HEAD), (...  7.29 us
  transfers between devices with their start and end apart: 7, of which 5 were waited for; matrix products, arithmetic and copies ran while one was open for 2% of the time, Pallas kernels for 4%

profile of v5, /device:TPU:1, one launch (start us, length us, event | category | flops | bytes accessed | tf_op | source)
XLA Modules:
  0.0 183.3 jit_solution(7784772180641820411)
XLA Ops:
  0.6 0.0 copy-start.1
  0.7 0.0 copy-start.2
  0.7 32.9 %copies.1 = bf16[4,256,512]{2,1,0:T(8,128)(2,1)} custom-call(s32[1]{0:T(128)} %bitcast.3.core_ref, bf16[512,512]{1,0:T(8,128)(2,1)} %w_ref.3), custom_call_target="tpu_custom_call" | custom-call | tf_op jit(solution)/shard_map/copies/pallas_call | solution.py:132
  33.6 4.8 %all-to-all-start = ((bf16[4,256,512]{2,1,0:T(8,128)(2,1)}), bf16[4,256,512]{2,1,0:T(8,128)(2,1)S(1)}, u32[]{:S(2)}, u32[]{:S(2)}) async-start(bf16[4,256,512]{2,1,0:T(8,128)(2,1)} %copies.1), calls=%async_computation | async-start | bytes 2097152 | tf_op jit(solution)/shard_map/all_to_all | solution.py:399
  38.4 0.0 copy-done.1
  38.4 0.0 copy-done.2
  38.4 0.7 fusion.2
  39.1 12.7 %all-to-all-done.near_ref = bf16[4,256,512]{2,1,0:T(8,128)(2,1)S(1)} async-done(((bf16[4,256,512]{2,1,0:T(8,128)(2,1)}), bf16[4,256,512]{2,1,0:T(8,128)(2,1)S(1)}, u32[]{:S(2)}, u32[]{:S(2)}) %all-to-all-start) | async-done | bytes 1048608 | tf_op jit(solution)/shard_map/all_to_all | solution.py:399
  51.8 2.7 %collective-permute-start = (bf16[4,256,512]{2,1,0:T(8,128)(2,1)S(1)}, bf16[4,256,512]{2,1,0:T(8,128)(2,1)S(1)}, u32[]{:S(2)}, u32[]{:S(2)}) collective-permute-start(bf16[4,256,512]{2,1,0:T(8,128)(2,1)S(1)} %all-to-all-done.near_ref), channel_id=1, source_target_pairs={{0,4},{4,0},{8,12},{12,8},{16,20},{20,16},{24,28},{28,24},{32,36},... | collective-permute-start | bytes 3145736 | tf_op jit(solution)/shard_map/ppermute | solution.py:402
  54.5 0.0 copy-start.3
  54.5 0.0 copy-start.4
  54.5 7.7 %own_head.1 = (bf16[6,256,512]{2,1,0:T(8,128)(2,1)}, f32[6,256,128]{2,1,0:T(8,128)}, bf16[6,256,128]{2,1,0:T(8,128)(2,1)}) custom-call(s32[6]{0:T(128)} %get-tuple-element.18.start_ref, bf16[6144,512]{1,0:T(8,128)(2,1)} %tokens_ref.1, bf16[6144,512]{1,0:T(8,128)(2,1)} %tokens_ref.1, bf16[512,512]{1,0:T(8,128)(2,1)} %w_ref.3), custom_call_target="tpu_custom_call" | custom-call | flops 25769803776 | bytes 6291456 | tf_op jit(solution)/shard_map/own_head/pallas_call | solution.py:98
  62.1 0.7 pad_add_fusion.pos_ref
  62.8 0.0 copy-done.3
  62.8 0.0 copy-done.4
  62.8 0.6 bitcast_add_fusion.table_ref
  63.4 0.0 collective-permute-done.far_ref
  63.4 12.2 %layer.1 = (bf16[2,32,13,8,128]{4,3,2,1,0:T(8,128)(2,1)}, bf16[6,1,512]{2,1,0:T(2,128)(2,1)}) custom-call(s32[6]{0:T(128)} %get-tuple-element.18.start_ref, s32[6]{0:T(128)} %get-tuple-element.19.len_ref, s32[2]{0:T(128)} %pad_add_fusion.pos_ref, bf16[6144,512]{1,0:T(8,128)(2,1)} %tokens_ref.1, bf16[6,256,512]{2,1,0:T(8,128)(2,1)} %get-tuple-element.7.half_hbm, ...), custom_call_target="tpu_custom_call" | custom-call | tf_op jit(solution)/shard_map/layer/pallas_call | solution.py:265
  75.5 11.8 %all-to-all-start.1 = ((bf16[64,104,128]{2,1,0:T(8,128)(2,1)}), bf16[64,104,128]{2,1,0:T(8,128)(2,1)S(1)}, u32[]{:S(2)}, u32[]{:S(2)}) async-start(bf16[64,104,128]{2,1,0:T(8,128)(2,1)} %bitcast.36), calls=%async_computation.1 | async-start | bytes 3407872 | tf_op jit(solution)/shard_map/all_to_all | solution.py:411
  87.3 41.7 %all-to-all-done.1 = bf16[64,104,128]{2,1,0:T(8,128)(2,1)S(1)} async-done(((bf16[64,104,128]{2,1,0:T(8,128)(2,1)}), bf16[64,104,128]{2,1,0:T(8,128)(2,1)S(1)}, u32[]{:S(2)}, u32[]{:S(2)}) %all-to-all-start.1) | async-done | bytes 1703968 | tf_op jit(solution)/shard_map/all_to_all | solution.py:411
  129.1 2.9 %regroup.1 = bf16[64,4,3,8,128]{4,3,2,1,0:T(8,128)(2,1)} custom-call(s32[1]{0:T(128)} %bitcast.7.first_ref, bf16[64,13,8,128]{3,2,1,0:T(8,128)(2,1)S(1)} %bitcast.32), custom_call_target="tpu_custom_call" | custom-call | tf_op jit(solution)/shard_map/regroup/pallas_call | solution.py:311
  131.9 0.0 copy-start
  132.0 7.3 %all-to-all-start.2 = ((bf16[256,24,128]{2,1,0:T(8,128)(2,1)}), bf16[256,24,128]{2,1,0:T(8,128)(2,1)S(1)}, u32[]{:S(2)}, u32[]{:S(2)}) async-start(bf16[256,24,128]{2,1,0:T(8,128)(2,1)} %bitcast.35), calls=%async_computation.2 | async-start | bytes 3145728 | tf_op jit(solution)/shard_map/all_to_all | solution.py:418
  139.4 0.0 copy-done
  139.5 1.4 collective-permute-start.1
  140.9 2.4 %collective-permute-start.2 = (bf16[6,128]{1,0:T(8,128)(2,1)S(1)}, bf16[6,128]{1,0:T(8,128)(2,1)S(1)}, u32[]{:S(2)}, u32[]{:S(2)}) collective-permute-start(bf16[6,128]{1,0:T(8,128)(2,1)S(1)} %bitcast.40), channel_id=1, source_target_pairs={{0,2},{1,3},{2,0},{3,1},{4,6},{5,7},{6,4},{7,5},{8,10},{9,11},{10,... | collective-permute-start | bytes 4616 | tf_op jit(solution)/shard_map/ppermute | solution.py:434
  143.3 1.2 collective-permute-start.3
  144.5 0.0 collective-permute-done.1
  144.5 0.6 collective-permute-done.2
  145.2 0.9 collective-permute-done.3
  146.1 0.6 reshape.35
  146.7 0.7 fusion
  147.4 33.9 %all-to-all-done.2 = bf16[256,24,128]{2,1,0:T(8,128)(2,1)S(1)} async-done(((bf16[256,24,128]{2,1,0:T(8,128)(2,1)}), bf16[256,24,128]{2,1,0:T(8,128)(2,1)S(1)}, u32[]{:S(2)}, u32[]{:S(2)}) %all-to-all-start.2) | async-done | bytes 1572896 | tf_op jit(solution)/shard_map/all_to_all | solution.py:418
  181.3 2.1 %place.1 = bf16[768,8,128]{2,1,0:T(8,128)(2,1)} custom-call(s32[24]{0:T(128)} %get-tuple-element.13.len_ref, s32[24]{0:T(128)} %get-tuple-element.12.off_ref, bf16[2,32,4,3,8,128]{5,4,3,2,1,0:T(8,128)(2,1)S(1)} %bitcast.34), custom_call_target="tpu_custom_call" | custom-call | tf_op jit(solution)/shard_map/place/pallas_call | solution.py:375
  (13 shorter events, 0.2 us)
Async XLA Ops:
  0.6 37.8 %copy-start.1 = (s32[1,24]{1,0:T(1,128)S(1)}, s32[1,24]{1,0:T(1,128)}, u32[]{:S(2)}) copy-start(s32[1,24]{1,0:T(1,128)} %param.10) | copy-start | bytes 292
  0.7 37.8 %copy-start.2 = (s32[1,24]{1,0:T(1,128)S(1)}, s32[1,24]{1,0:T(1,128)}, u32[]{:S(2)}) copy-start(s32[1,24]{1,0:T(1,128)} %param.13) | copy-start | bytes 292
  33.6 18.2 %all-to-all-start = ((bf16[4,256,512]{2,1,0:T(8,128)(2,1)}), bf16[4,256,512]{2,1,0:T(8,128)(2,1)S(1)}, u32[]{:S(2)}, u32[]{:S(2)}) async-start(bf16[4,256,512]{2,1,0:T(8,128)(2,1)} %copies.1), calls=%async_computation | async-start | bytes 2097152 | tf_op jit(solution)/shard_map/all_to_all | solution.py:399
  51.8 11.6 %collective-permute-start = (bf16[4,256,512]{2,1,0:T(8,128)(2,1)S(1)}, bf16[4,256,512]{2,1,0:T(8,128)(2,1)S(1)}, u32[]{:S(2)}, u32[]{:S(2)}) collective-permute-start(bf16[4,256,512]{2,1,0:T(8,128)(2,1)S(1)} %all-to-all-done.near_ref), channel_id=1, source_target_pairs={{0,4},{4,0},{8,12},{12,8},{16,20},{20,16},{24,28},{28,24},{32,36},... | collective-permute-start | bytes 3145736 | tf_op jit(solution)/shard_map/ppermute | solution.py:402
  54.5 8.3 %copy-start.3 = (s32[1,24]{1,0:T(1,128)S(1)}, s32[1,24]{1,0:T(1,128)}, u32[]{:S(2)}) copy-start(s32[1,24]{1,0:T(1,128)} %param.12) | copy-start | bytes 292
  54.5 8.3 %copy-start.4 = (s32[1,24]{1,0:T(1,128)S(1)}, s32[1,24]{1,0:T(1,128)}, u32[]{:S(2)}) copy-start(s32[1,24]{1,0:T(1,128)} %param.11) | copy-start | bytes 292
  75.5 53.5 %all-to-all-start.1 = ((bf16[64,104,128]{2,1,0:T(8,128)(2,1)}), bf16[64,104,128]{2,1,0:T(8,128)(2,1)S(1)}, u32[]{:S(2)}, u32[]{:S(2)}) async-start(bf16[64,104,128]{2,1,0:T(8,128)(2,1)} %bitcast.36), calls=%async_computation.1 | async-start | bytes 3407872 | tf_op jit(solution)/shard_map/all_to_all | solution.py:411
  131.9 7.4 %copy-start = (bf16[6,1,512]{2,1,0:T(2,128)(2,1)S(1)}, bf16[6,1,512]{2,1,0:T(2,128)(2,1)}, u32[]{:S(2)}) copy-start(bf16[6,1,512]{2,1,0:T(2,128)(2,1)} %get-tuple-element.11) | copy-start | bytes 18436
  132.0 49.3 %all-to-all-start.2 = ((bf16[256,24,128]{2,1,0:T(8,128)(2,1)}), bf16[256,24,128]{2,1,0:T(8,128)(2,1)S(1)}, u32[]{:S(2)}, u32[]{:S(2)}) async-start(bf16[256,24,128]{2,1,0:T(8,128)(2,1)} %bitcast.35), calls=%async_computation.2 | async-start | bytes 3145728 | tf_op jit(solution)/shard_map/all_to_all | solution.py:418
  139.5 5.0 %collective-permute-start.1 = (bf16[6,128]{1,0:T(8,128)(2,1)S(1)}, bf16[6,128]{1,0:T(8,128)(2,1)S(1)}, u32[]{:S(2)}, u32[]{:S(2)}) collective-permute-start(bf16[6,128]{1,0:T(8,128)(2,1)S(1)} %bitcast.41), channel_id=1, source_target_pairs={{0,1},{1,2},{2,3},{3,0},{4,5},{5,6},{6,7},{7,4},{8,9},{9,10},{10,1... | collective-permute-start | bytes 4616 | tf_op jit(solution)/shard_map/ppermute | solution.py:434
  140.9 4.2 %collective-permute-start.2 = (bf16[6,128]{1,0:T(8,128)(2,1)S(1)}, bf16[6,128]{1,0:T(8,128)(2,1)S(1)}, u32[]{:S(2)}, u32[]{:S(2)}) collective-permute-start(bf16[6,128]{1,0:T(8,128)(2,1)S(1)} %bitcast.40), channel_id=1, source_target_pairs={{0,2},{1,3},{2,0},{3,1},{4,6},{5,7},{6,4},{7,5},{8,10},{9,11},{10,... | collective-permute-start | bytes 4616 | tf_op jit(solution)/shard_map/ppermute | solution.py:434
  143.3 2.7 %collective-permute-start.3 = (bf16[6,128]{1,0:T(8,128)(2,1)S(1)}, bf16[6,128]{1,0:T(8,128)(2,1)S(1)}, u32[]{:S(2)}, u32[]{:S(2)}) collective-permute-start(bf16[6,128]{1,0:T(8,128)(2,1)S(1)} %bitcast.39), channel_id=1, source_target_pairs={{0,3},{1,0},{2,1},{3,2},{4,7},{5,4},{6,5},{7,6},{8,11},{9,8},{10,9... | collective-permute-start | bytes 4616 | tf_op jit(solution)/shard_map/ppermute | solution.py:434

commit v6 on v5

v6 whole, which is shorter than its diff:
```python
import jax
import jax.numpy as jnp
from jax import lax
from jax.experimental import pallas as pl
from jax.experimental.pallas import tpu as pltpu
from jax.sharding import PartitionSpec as P

D = 512
HEADS = 4
HEAD = D // HEADS
BLOCK = 128
MAXB = 2
BLK_DEV = 48
USERS = 24
N_DP = 64
N_MP = 4
WIN = MAXB * BLOCK
MINE = USERS // N_MP
RAW = 2
DONE = MINE - RAW
TILE = 8
GROUPS = WIN // TILE
HALVES = N_DP // GROUPS
GROUP = 2
RAW_MSG = N_MP + 1
ROUND = DONE // HALVES
MSG = (ROUND + 1) * N_MP
EPS = 1e-05
BF16 = jnp.bfloat16
F32 = jnp.float32


def silu_of_twice(h):
    return h + h * jnp.tanh(h)


def project(half_parts, w_parts):
    acc = jnp.dot(half_parts[0], w_parts[0], preferred_element_type=F32)
    for n, w in zip(half_parts[1:], w_parts[1:]):
        acc = acc + jnp.dot(n, w, preferred_element_type=F32)
    proj = silu_of_twice(acc).astype(BF16)
    return [proj[:, j * HEAD : (j + 1) * HEAD] for j in range(4)]


def attend(q, k, v):
    row = lax.broadcasted_iota(jnp.int32, (BLOCK, BLOCK), 0)
    col = lax.broadcasted_iota(jnp.int32, (BLOCK, BLOCK), 1)
    causal = col <= row
    scale = 0.5 * HEAD ** (-0.5)
    contract_last = (((1,), (1,)), ((), ()))
    s0 = lax.dot_general(q[:BLOCK], k[:BLOCK], contract_last, preferred_element_type=F32)
    s1 = lax.dot_general(q[BLOCK:], k, contract_last, preferred_element_type=F32)
    a0 = jnp.where(causal, silu_of_twice(s0 * scale), 0.0).astype(BF16)
    b = silu_of_twice(s1 * scale)
    a1 = jnp.concatenate(
        [b[:, :BLOCK].astype(BF16), jnp.where(causal, b[:, BLOCK:], 0.0).astype(BF16)], axis=1
    )
    return jnp.concatenate(
        [
            jnp.dot(a0, v[:BLOCK], preferred_element_type=F32),
            jnp.dot(a1, v, preferred_element_type=F32),
        ],
        axis=0,
    )


def norm_stats(total, squares, unit=1.0):
    mean = total * (1.0 / D)
    var = squares * (1.0 / D) - mean * mean
    return mean, lax.rsqrt(var * (unit * unit) + EPS) * unit


def in_vmem():
    return pl.BlockSpec(memory_space=pltpu.VMEM)


def in_hbm():
    return pl.BlockSpec(memory_space=pltpu.HBM)


def keep(array):
    return pltpu.with_memory_space_constraint(array, pltpu.VMEM)


def own_head_kernel(start_ref, x0_ref, x1_ref, w_ref, half_ref, att_ref, gate_ref):
    x = jnp.concatenate([x0_ref[...], x1_ref[...]], axis=0).astype(F32)
    mean, inv = norm_stats(
        jnp.sum(x, axis=1, keepdims=True), jnp.sum(x * x, axis=1, keepdims=True)
    )
    half = ((x - mean) * (inv * 0.5)).astype(BF16)
    half_ref[0] = half
    u, v, q, k = project([half], [w_ref[...]])
    gate_ref[0] = u
    att_ref[0] = attend(q, k, v)


def own_head(tokens, starts, w_own):
    def per_user(width):
        return pl.BlockSpec((1, WIN, width), lambda i, s: (i, 0, 0))

    return pl.pallas_call(
        own_head_kernel,
        grid_spec=pltpu.PrefetchScalarGridSpec(
            num_scalar_prefetch=1,
            grid=(DONE,),
            in_specs=[
                pl.BlockSpec((BLOCK, D), lambda i, s: (s[i], 0)),
                pl.BlockSpec((BLOCK, D), lambda i, s: (jnp.minimum(s[i] + 1, BLK_DEV - 1), 0)),
                pl.BlockSpec((D, D), lambda i, s: (0, 0)),
            ],
            out_specs=[per_user(D), per_user(HEAD), per_user(HEAD)],
        ),
        out_shape=[
            jax.ShapeDtypeStruct((DONE, WIN, D), BF16),
            jax.ShapeDtypeStruct((DONE, WIN, HEAD), F32),
            jax.ShapeDtypeStruct((DONE, WIN, HEAD), BF16),
        ],
        cost_estimate=pl.CostEstimate(
            flops=DONE * WIN * D * D * 64, bytes_accessed=DONE * WIN * D * 8, transcendentals=0
        ),
        name="own_head",
    )(starts, tokens, tokens, w_own)


def rows_of(tiles):
    return jnp.concatenate(
        [tiles[..., q, :, :].reshape(-1, HEAD) for q in range(N_MP)], axis=1
    )


def table_tile(table_ref):
    tile = jnp.broadcast_to(table_ref[...], (TILE, 128)).astype(F32).astype(BF16)
    return jnp.broadcast_to(tile[None], (GROUPS, TILE, 128))


def pack_kernel(start_ref, tokens_ref, table_ref, out_ref, x_s, sem):
    copies = []
    for k in range(RAW):
        first = start_ref[k]
        second = jnp.minimum(first + 1, BLK_DEV - 1)
        for j, block in enumerate((first, second)):
            copy = pltpu.make_async_copy(
                tokens_ref.at[pl.ds(block * BLOCK, BLOCK)],
                x_s.at[k, pl.ds(j * BLOCK, BLOCK)],
                sem.at[k, j],
            )
            copy.start()
            copies.append(copy)
    tile = table_tile(table_ref)
    for k in range(RAW):
        out_ref[k, :, N_MP] = tile
    for copy in copies:
        copy.wait()
    for k in range(RAW):
        for q in range(N_MP):
            out_ref[k, :, q] = x_s[k, :, q * HEAD : (q + 1) * HEAD].reshape(GROUPS, TILE, HEAD)


def pack(tokens, starts, table):
    shape = (RAW, GROUPS, RAW_MSG, TILE, HEAD)
    return pl.pallas_call(
        pack_kernel,
        grid_spec=pltpu.PrefetchScalarGridSpec(
            num_scalar_prefetch=1,
            grid=(1,),
            in_specs=[in_hbm(), in_vmem()],
            out_specs=pl.BlockSpec(shape, lambda i, s: (0, 0, 0, 0, 0)),
            scratch_shapes=[pltpu.VMEM((RAW, WIN, D), BF16), pltpu.SemaphoreType.DMA((RAW, MAXB))],
        ),
        out_shape=jax.ShapeDtypeStruct(shape, BF16),
        name="pack",
    )(starts, tokens, table)


def head_order(part):
    return [part] + [(part + HEADS - s) % HEADS for s in range(1, HEADS)]


def mix(low_is_near, half_rows, first, near, far, w_out_of, x_rows):
    low = half_rows[:, : D // 2]
    high = half_rows[:, D // 2 :]
    parts = [jnp.where(low_is_near, low, high), jnp.where(low_is_near, high, low)]
    users = half_rows.shape[0] // WIN
    heads, gates = [first[0]], [first[1]]
    for near_ref, far_ref in zip(near, far):
        u, v, q, k = project(parts, [near_ref[...], far_ref[...]])
        gates.append(u)
        heads.append(attend_users(users, q, k, v))
    total = jnp.sum(heads[0] + heads[1] + (heads[2] + heads[3]), axis=1, keepdims=True)
    squares = jnp.sum(
        heads[0] * heads[0] + heads[1] * heads[1] + (heads[2] * heads[2] + heads[3] * heads[3]),
        axis=1,
        keepdims=True,
    )
    mean, inv = norm_stats(total, squares, 1.0 / WIN)
    gated = jnp.concatenate(
        [((a - mean) * inv * g.astype(F32)).astype(BF16) for a, g in zip(heads, gates)], axis=1
    )
    return jnp.dot(gated, w_out_of(), preferred_element_type=F32) + x_rows().astype(F32)


def attend_users(users, q, k, v):
    return jnp.concatenate(
        [attend(*(t[j * WIN : (j + 1) * WIN] for t in (q, k, v))) for j in range(users)], axis=0
    )


def live_rows(mixed, length):
    at = lax.broadcasted_iota(jnp.int32, (WIN, 1), 0)
    return jnp.where(at < length, mixed, 0.0).astype(BF16)


def last_row(tile, length):
    pick = lax.broadcasted_iota(jnp.int32, (TILE, HEAD), 0) == (length - 1) % TILE
    return jnp.sum(jnp.where(pick, tile.astype(F32), 0.0), axis=0, keepdims=True).astype(BF16)


def w_out_copies(part, w_out_ref, w_out_s, sem):
    return [
        pltpu.make_async_copy(
            w_out_ref.at[pl.ds(h * HEAD, HEAD)], w_out_s.at[pl.ds(s * HEAD, HEAD)], sem.at[s]
        )
        for s, h in enumerate(head_order(part))
    ]


def layer_kernel(start_ref, len_ref, pos_ref, tokens_ref, half_hbm, att_hbm, gate_hbm, *rest):
    near, far = rest[: HEADS - 1], rest[HEADS - 1 : 2 * HEADS - 2]
    w_out_ref, out_ref, state_ref = rest[2 * HEADS - 2 : 2 * HEADS + 1]
    x_s, half_s, att_s, gate_s, w_out_s, out_s, sem_in, sem_w, sem_out = rest[2 * HEADS + 1 :]
    low_is_near = pos_ref[1] == 0

    def loads(i):
        first = start_ref[i]
        second = jnp.minimum(first + 1, BLK_DEV - 1)
        pairs = [
            (half_hbm.at[i], half_s.at[pl.ds(i * WIN, WIN)]),
            (att_hbm.at[i], att_s.at[pl.ds(i * WIN, WIN)]),
            (gate_hbm.at[i], gate_s.at[pl.ds(i * WIN, WIN)]),
            (tokens_ref.at[pl.ds(first * BLOCK, BLOCK)], x_s.at[pl.ds(i * WIN, BLOCK)]),
            (tokens_ref.at[pl.ds(second * BLOCK, BLOCK)], x_s.at[pl.ds(i * WIN + BLOCK, BLOCK)]),
        ]
        return [pltpu.make_async_copy(a, b, sem_in.at[i, j]) for j, (a, b) in enumerate(pairs)]

    weights = w_out_copies(pos_ref[0], w_out_ref, w_out_s, sem_w)

    def sends(i):
        at = (i % HALVES, slice(None), pl.ds((i // HALVES) * N_MP, N_MP))
        return pltpu.make_async_copy(out_s.at[at], out_ref.at[at], sem_out.at[i])

    for i in range(DONE):
        for copy in loads(i):
            copy.start()
        if i == GROUP - 1:
            for copy in weights:
                copy.start()

    def group(step, carry):
        first_user = step * GROUP
        for j in range(GROUP):
            for copy in loads(first_user + j):
                copy.wait()
        rows = pl.ds(pl.multiple_of(first_user * WIN, WIN), GROUP * WIN)

        def w_out_of():
            @pl.when(step == 0)
            def _():
                for copy in weights:
                    copy.wait()

            return w_out_s[...]

        both = mix(
            low_is_near,
            half_s[rows, :],
            (att_s[rows, :], gate_s[rows, :]),
            near,
            far,
            w_out_of,
            lambda: x_s[rows, :],
        )
        for j in range(GROUP):
            i = first_user + j
            length = len_ref[i]
            half_id = i % HALVES
            base = (i // HALVES) * N_MP
            mixed = live_rows(both[j * WIN : (j + 1) * WIN], length)
            for q in range(N_MP):
                out_s[half_id, :, base + q] = mixed[:, q * HEAD : (q + 1) * HEAD].reshape(
                    GROUPS, TILE, HEAD
                )
            sends(i).start()
            for q in range(N_MP):
                state_ref[i, :, q * HEAD : (q + 1) * HEAD] = last_row(
                    out_s[half_id, (length - 1) // TILE, base + q], length
                )
        return carry

    lax.fori_loop(0, DONE // GROUP, group, 0)
    for i in range(DONE):
        sends(i).wait()


def layer(tokens, starts, lengths, position, kept, near, far, w_out):
    message = (HALVES, GROUPS, MSG, TILE, HEAD)
    return pl.pallas_call(
        layer_kernel,
        grid_spec=pltpu.PrefetchScalarGridSpec(
            num_scalar_prefetch=3,
            grid=(1,),
            in_specs=[in_hbm()] * 4 + [in_vmem()] * (2 * HEADS - 2) + [in_hbm()],
            out_specs=[in_hbm(), in_vmem()],
            scratch_shapes=[
                pltpu.VMEM((DONE * WIN, D), BF16),
                pltpu.VMEM((DONE * WIN, D), BF16),
                pltpu.VMEM((DONE * WIN, HEAD), F32),
                pltpu.VMEM((DONE * WIN, HEAD), BF16),
                pltpu.VMEM((D, D), BF16),
                pltpu.VMEM((HALVES, GROUPS, ROUND * N_MP, TILE, HEAD), BF16),
                pltpu.SemaphoreType.DMA((DONE, 5)),
                pltpu.SemaphoreType.DMA((HEADS,)),
                pltpu.SemaphoreType.DMA((DONE,)),
            ],
        ),
        out_shape=[
            jax.ShapeDtypeStruct(message, BF16),
            jax.ShapeDtypeStruct((DONE, 1, D), BF16),
        ],
        name="layer",
    )(starts, lengths, position, tokens, *kept, *map(keep, near), *map(keep, far), w_out)


def raw_kernel(first_tile, len_ref, pos_ref, src_ref, w_own_ref, *rest):
    near, far = rest[: HEADS - 1], rest[HEADS - 1 : 2 * HEADS - 2]
    w_out_ref = rest[2 * HEADS - 2]
    pieces = rest[2 * HEADS - 1 : 2 * HEADS - 1 + N_MP]
    state_ref, x_s, w_out_s, mixed_s, sem_x, sem_w = rest[2 * HEADS - 1 + N_MP :]
    part = pos_ref[0]
    loads = [
        pltpu.make_async_copy(
            src_ref.at[pl.ds(k * GROUPS, GROUPS), pl.ds(first_tile, N_MP)], x_s.at[k], sem_x.at[k]
        )
        for k in range(RAW)
    ]
    weights = w_out_copies(part, w_out_ref, w_out_s, sem_w)
    for copy in loads + weights:
        copy.start()
    for copy in loads:
        copy.wait()

    def x_rows():
        return rows_of(x_s[...])

    x = x_rows().astype(F32)
    mean, inv = norm_stats(
        jnp.sum(x, axis=1, keepdims=True), jnp.sum(x * x, axis=1, keepdims=True)
    )
    half = ((x - mean) * (inv * 0.5)).astype(BF16)
    u, v, q, k = project([half], [w_own_ref[...]])

    def w_out_of():
        for copy in weights:
            copy.wait()
        return w_out_s[...]

    both = mix(
        pos_ref[1] == 0, half, (attend_users(RAW, q, k, v), u), near, far, w_out_of, x_rows
    )
    for k in range(RAW):
        mixed = live_rows(both[k * WIN : (k + 1) * WIN], len_ref[k])
        for q in range(N_MP):
            mixed_s[q, k] = mixed[:, q * HEAD : (q + 1) * HEAD].reshape(GROUPS, TILE, HEAD)
        for q in range(N_MP):
            state_ref[k, :, q * HEAD : (q + 1) * HEAD] = last_row(
                mixed_s[q, k, (len_ref[k] - 1) // TILE], len_ref[k]
            )
    for s in range(N_MP):
        pieces[s][...] = mixed_s[(part + s) % N_MP]


def raw_layer(source, first_tile, lengths, position, w_own, near, far, w_out):
    piece = jax.ShapeDtypeStruct((RAW, GROUPS, TILE, HEAD), BF16)
    outs = pl.pallas_call(
        lambda *refs: raw_kernel(first_tile, *refs),
        grid_spec=pltpu.PrefetchScalarGridSpec(
            num_scalar_prefetch=2,
            grid=(1,),
            in_specs=[in_hbm()] + [in_vmem()] * (2 * HEADS - 1) + [in_hbm()],
            out_specs=[in_vmem()] * (N_MP + 1),
            scratch_shapes=[
                pltpu.VMEM((RAW, GROUPS, N_MP, TILE, HEAD), BF16),
                pltpu.VMEM((D, D), BF16),
                pltpu.VMEM((N_MP, RAW, GROUPS, TILE, HEAD), BF16),
                pltpu.SemaphoreType.DMA((RAW,)),
                pltpu.SemaphoreType.DMA((HEADS,)),
            ],
        ),
        out_shape=[piece] * N_MP + [jax.ShapeDtypeStruct((RAW, 1, D), BF16)],
    )(lengths, position, source, w_own, *near, *far, w_out)
    return outs[:N_MP], outs[N_MP]


def merge_kernel(first_ref, in_ref, msg_ref, out_ref, sorted_s, table_v, table_s, sem):
    table = jnp.max(in_ref[:, N_MP].astype(F32), axis=1)
    table_v[...] = table.astype(jnp.int32)
    copy = pltpu.make_async_copy(table_v, table_s, sem.at[0])
    copy.start()
    copy.wait()
    first = first_ref[0]

    def one(d, carry):
        o = table_s[d, first]
        for q in range(N_MP):
            sorted_s[o, q] = in_ref[d, q]
        return carry

    lax.fori_loop(0, N_DP, one, 0, unroll=8)
    send = pltpu.make_async_copy(sorted_s, out_ref.at[:, pl.ds(ROUND * N_MP, N_MP)], sem.at[1])
    send.start()
    send.wait()


def merge(spread, first, message):
    return pl.pallas_call(
        merge_kernel,
        grid_spec=pltpu.PrefetchScalarGridSpec(
            num_scalar_prefetch=1,
            grid=(1,),
            in_specs=[in_vmem(), in_hbm()],
            out_specs=in_hbm(),
            scratch_shapes=[
                pltpu.VMEM((N_DP, N_MP, TILE, HEAD), BF16),
                pltpu.VMEM((N_DP, 128), jnp.int32),
                pltpu.SMEM((N_DP, 128), jnp.int32),
                pltpu.SemaphoreType.DMA((2,)),
            ],
        ),
        out_shape=jax.ShapeDtypeStruct((N_DP, MSG, TILE, HEAD), BF16),
        input_output_aliases={2: 0},
        name="merge",
    )(first, keep(spread), message)


def regroup_kernel(to_ref, in_ref, out_ref):
    def one(d, carry):
        for r in range(ROUND):
            o = to_ref[r * N_DP + d]
            for q in range(N_MP):
                out_ref[o, q, r] = in_ref[d, r * N_MP + q]
        return carry

    lax.fori_loop(0, N_DP, one, 0, unroll=8)


def regroup(spread, to):
    shape = (N_DP, N_MP, ROUND, TILE, HEAD)
    return pl.pallas_call(
        regroup_kernel,
        grid_spec=pltpu.PrefetchScalarGridSpec(
            num_scalar_prefetch=1,
            grid=(1,),
            in_specs=[in_vmem()],
            out_specs=pl.BlockSpec(shape, lambda i, s: (0, 0, 0, 0, 0)),
        ),
        out_shape=jax.ShapeDtypeStruct(shape, BF16),
        name="regroup",
    )(to, keep(spread))


def place_kernel(len_ref, off_ref, pos_ref, in_ref, *rest):
    pieces = rest[:N_MP]
    out_ref, zero_v, used_s, sem = rest[N_MP:]
    per_block = BLOCK // TILE
    zero_v[...] = jnp.zeros_like(zero_v)

    def clear(b, carry):
        used_s[b] = 0
        return carry

    lax.fori_loop(0, BLK_DEV, clear, 0, unroll=8)

    def send(u, source):
        def block(j):
            to = off_ref[u] + j
            used_s[to] = 1
            pltpu.make_async_copy(
                source(pl.ds(j * per_block, per_block)),
                out_ref.at[pl.ds(to * per_block, per_block)],
                sem,
            ).start()

        block(0)

        @pl.when(len_ref[u] > BLOCK)
        def _():
            block(1)

    for s in range(N_MP):
        m = (pos_ref[0] + N_MP - s) % N_MP
        for k in range(RAW):
            send(m * MINE + k, lambda rows: pieces[s].at[k, rows])

    def one(n, carry):
        m = n // DONE
        i = n % DONE
        send(m * MINE + RAW + i, lambda rows: in_ref.at[i % HALVES, rows, m, i // HALVES])
        return carry

    lax.fori_loop(0, N_MP * DONE, one, 0)

    def fill(b, carry):
        @pl.when(used_s[b] == 0)
        def _():
            pltpu.make_async_copy(zero_v, out_ref.at[pl.ds(b * per_block, per_block)], sem).start()

        return carry

    lax.fori_loop(0, BLK_DEV, fill, 0)
    pltpu.make_async_copy(out_ref, out_ref, sem).wait()


def place(arrived, pieces, lengths, offsets, position):
    rows = BLK_DEV * BLOCK
    return pl.pallas_call(
        place_kernel,
        grid_spec=pltpu.PrefetchScalarGridSpec(
            num_scalar_prefetch=3,
            grid=(1,),
            in_specs=[in_vmem()] * (1 + N_MP),
            out_specs=in_hbm(),
            scratch_shapes=[
                pltpu.VMEM((BLOCK // TILE, TILE, HEAD), BF16),
                pltpu.SMEM((BLK_DEV,), jnp.int32),
                pltpu.SemaphoreType.DMA,
            ],
        ),
        out_shape=jax.ShapeDtypeStruct((rows // TILE, TILE, HEAD), BF16),
        compiler_params=pltpu.CompilerParams(vmem_limit_bytes=32 * 1024 * 1024),
        name="place",
    )(lengths, offsets, position, keep(arrived), *map(keep, pieces)).reshape(rows, HEAD)


def along_mp(array, s):
    return lax.ppermute(array, "mp", [(i, (i + s) % N_MP) for i in range(N_MP)])


def per_device(tokens, w_uvqk, w_out, hist_len, owner, recv_offset, block_start):
    me = lax.axis_index("dp")
    part = lax.axis_index("mp")
    first = part * MINE
    core = me % 2
    half = me // GROUPS
    position = jnp.stack([part, core])

    starts = lax.dynamic_slice_in_dim(block_start[0], first, MINE, 0)
    lengths = lax.dynamic_slice_in_dim(hist_len[0], first, MINE, 0)
    table = jnp.concatenate([owner, hist_len, recv_offset, jnp.zeros((1, 56), jnp.int32)], axis=1)

    mine_rows = jnp.where(core == 0, w_uvqk[: D // 2], w_uvqk[D // 2 :])
    near, far = [], []
    for s in range(1, N_MP):
        near.append(along_mp(mine_rows, s))
    for s in range(1, N_MP):
        far.append(lax.ppermute(near[s - 1], "dp", [(i, i ^ 1) for i in range(N_DP)]))

    raw = pack(tokens, starts[:RAW], table)
    raw_in = lax.all_to_all(
        raw.reshape(N_DP, RAW_MSG * TILE, HEAD), "dp", 0, 0, tiled=True
    ).reshape(N_DP, RAW_MSG, TILE, HEAD)
    kept = own_head(tokens, starts[RAW:], w_uvqk)
    message, last = layer(
        tokens, starts[RAW:], lengths[RAW:], position, kept, near, far, w_out
    )
    message = merge(
        raw_in, (first + half)[None], message.reshape(N_DP, MSG, TILE, HEAD)
    )
    spread = lax.all_to_all(
        message.reshape(N_DP, MSG * TILE, HEAD), "dp", 0, 0, tiled=True
    ).reshape(N_DP, MSG, TILE, HEAD)
    _, raw_last = raw_layer(
        raw.reshape(N_DP, RAW_MSG, TILE, HEAD), 0, lengths[:RAW], position,
        w_uvqk, near, far, w_out,
    )

    table = raw_in[:, N_MP, 0, :].astype(jnp.int32)
    owners = table[:, :USERS]
    held = lax.dynamic_slice_in_dim(owners, first + RAW + half, HALVES * (ROUND - 1) + 1, 1)
    to = held[:, ::HALVES].T.reshape(-1)
    mine = owners == me
    recv_len = jnp.sum(jnp.where(mine, table[:, USERS : 2 * USERS], 0), axis=0)
    recv_off = jnp.sum(jnp.where(mine, table[:, 2 * USERS : 3 * USERS], 0), axis=0)

    sorted_rows = regroup(spread, to)
    arrived = lax.all_to_all(
        sorted_rows.reshape(N_DP * N_MP, ROUND * TILE, HEAD), ("dp", "mp"), 0, 0, tiled=True
    )
    pieces, _ = raw_layer(
        spread, ROUND * N_MP,
        lax.dynamic_slice_in_dim(recv_len, first, RAW, 0), position,
        w_uvqk, near, far, w_out,
    )
    pieces = [pieces[0]] + [along_mp(pieces[s], s) for s in range(1, N_MP)]
    packed = place(
        arrived.reshape(HALVES, GROUPS, N_MP, ROUND, TILE, HEAD),
        pieces, recv_len, recv_off, position,
    )

    columns = jnp.concatenate([raw_last, last], axis=0).reshape(MINE, N_MP, HEAD)
    state = jnp.zeros((N_MP, MINE, HEAD), BF16)
    for s in range(N_MP):
        to_part = (part + s) % N_MP
        piece = lax.dynamic_slice_in_dim(columns, to_part, 1, 1)[:, 0]
        if s:
            piece = along_mp(piece, s)
        state = lax.dynamic_update_slice_in_dim(state, piece[None], (part - s) % N_MP, 0)
    return packed, state.reshape(USERS, HEAD)


def solution(mesh):
    in_specs = (
        P("dp", None),
        P(None, "mp"),
        P(),
        P("dp", None),
        P("dp", None),
        P("dp", None),
        P("dp", None),
    )
    out_specs = (P("dp", "mp"), P("dp", "mp"))
    return jax.shard_map(
        per_device, mesh=mesh, in_specs=in_specs, out_specs=out_specs, check_vma=False
    )
```

time: 184 us -> 141 us (0.77); the launches traced: 183 us -> 138 us
  waiting for transfers between devices: 89.8 us -> 42.3 us
  Pallas kernels: 57.7 us -> 40 us
  starting transfers between devices: 31.6 us -> 44.4 us
  local copies, waits for them, and re-layouts: 1.38 us -> 5.76 us
  other arithmetic: 1.96 us -> 4.83 us
    all_to_all x3, waiting for transfers between devices: 88.3 us -> 39.1 us  [the longest x1 37.1 us: per_device(): lax.all_to_all(message.reshape(N_DP, MSG * TILE, HEAD), 'dp', 0, 0, tiled...]
    pallas_call x1 -> x4, Pallas kernels: 32.9 us -> 21.2 us  [the longest x2 15.8 us: raw_layer(): pl.pallas_call(lambda *refs: raw_kernel(first_tile, *refs), grid_spec=plt...]
    ppermute x4 -> x12, starting transfers between devices: 7.72 us -> 16.3 us  [the longest x9 15.3 us: along_mp(): return lax.ppermute(array, 'mp', [(i, (i + s) % N_MP) for i in range(N_MP)])]
    all_to_all x3, starting transfers between devices: 23.9 us -> 28.1 us  [the longest x1 13.2 us: per_device(): lax.all_to_all(raw.reshape(N_DP, RAW_MSG * TILE, HEAD), 'dp', 0, 0, tiled...]
    pallas_call x1, Pallas kernels: 12.2 us -> 9.25 us  [layer(): pl.pallas_call(layer_kernel, grid_spec=pltpu.PrefetchScalarGridSpec(num_s...]
    slice x0 -> x5, local copies, waits for them, and re-layouts: none -> 2.49 us  [the longest x1 0.67 us: per_device(): starts[RAW:]]
  transfers between devices with their start and end apart: 7 -> 15, of which waited for: 5 -> 6; matrix products, arithmetic and copies ran while one was open for 2% -> 6% of each run, Pallas kernels for 4% -> 25%
where the time goes in v6:
time: 141 us; the launch traced here: 138 us
  starting transfers between devices  44.4 us (31%)
  waiting for transfers between devices  42.3 us (30%)
  Pallas kernels  40 us (28%)
  local copies, waits for them, and re-layouts  5.76 us (4%)
  other arithmetic  4.83 us (3%)
    all_to_all x1, waiting for transfers between devices, per_device(): lax.all_to_all(message.reshape(N_DP, MSG * TILE, HEAD), 'dp', 0, 0, tiled...  37.1 us
    pallas_call x2, Pallas kernels, raw_layer(): pl.pallas_call(lambda *refs: raw_kernel(first_tile, *refs), grid_spec=plt...  15.8 us
    ppermute x9, starting transfers between devices, along_mp(): return lax.ppermute(array, 'mp', [(i, (i + s) % N_MP) for i in range(N_MP)])  15.3 us
    all_to_all x1, starting transfers between devices, per_device(): lax.all_to_all(raw.reshape(N_DP, RAW_MSG * TILE, HEAD), 'dp', 0, 0, tiled...  13.2 us
    pallas_call x1, Pallas kernels, layer(): pl.pallas_call(layer_kernel, grid_spec=pltpu.PrefetchScalarGridSpec(num_s...  9.25 us
    all_to_all x1, starting transfers between devices, per_device(): lax.all_to_all(message.reshape(N_DP, MSG * TILE, HEAD), 'dp', 0, 0, tiled...  8.26 us
    all_to_all x1, starting transfers between devices, per_device(): lax.all_to_all(sorted_rows.reshape(N_DP * N_MP, ROUND * TILE, HEAD), ('dp...  6.68 us
    pallas_call x1, Pallas kernels, own_head(): pl.pallas_call(own_head_kernel, grid_spec=pltpu.PrefetchScalarGridSpec(nu...  5.88 us
  transfers between devices with their start and end apart: 15, of which 6 were waited for; matrix products, arithmetic and copies ran while one was open for 6% of the time, Pallas kernels for 25%

profile of v6, /device:TPU:1, one launch (start us, length us, event | category | flops | bytes accessed | tf_op | source)
XLA Modules:
  0.0 138.5 jit_solution(2684277307405030611)
XLA Ops:
  0.7 1.1 slice_select_fusion
  1.7 2.1 %collective-permute-start = (bf16[256,512]{1,0:T(8,128)(2,1)S(1)}, bf16[256,512]{1,0:T(8,128)(2,1)S(1)}, u32[]{:S(2)}, u32[]{:S(2)}) collective-permute-start(bf16[256,512]{1,0:T(8,128)(2,1)S(1)} %slice_select_fusion), channel_id=1, source_target_pairs={{0,1},{1,2},{2,3},{3,0},{4,5},{5,6},{6,7},{7,4},{8,9},{9,10},{10,1... | collective-permute-start | bytes 786440 | tf_op jit(solution)/shard_map/ppermute | solution.py:544
  3.8 2.5 %collective-permute-start.1 = (bf16[256,512]{1,0:T(8,128)(2,1)S(1)}, bf16[256,512]{1,0:T(8,128)(2,1)S(1)}, u32[]{:S(2)}, u32[]{:S(2)}) collective-permute-start(bf16[256,512]{1,0:T(8,128)(2,1)S(1)} %slice_select_fusion), channel_id=1, source_target_pairs={{0,2},{1,3},{2,0},{3,1},{4,6},{5,7},{6,4},{7,5},{8,10},{9,11},{10,... | collective-permute-start | bytes 786440 | tf_op jit(solution)/shard_map/ppermute | solution.py:544
  6.3 1.2 collective-permute-start.2
  7.4 0.1 constant_dynamic-slice_fusion.6
  7.5 0.5 slice_bitcast_fusion.3.start_ref
  8.0 1.4 bitcast_add_fusion.table_ref
  9.4 3.3 %pack.1 = bf16[2,32,5,8,128]{4,3,2,1,0:T(8,128)(2,1)} custom-call(s32[2]{0:T(128)} %slice_bitcast_fusion.3.start_ref, bf16[6144,512]{1,0:T(8,128)(2,1)} %tokens_ref.3, s32[1,128]{1,0:T(1,128)} %bitcast_add_fusion.table_ref), custom_call_target="tpu_custom_call" | custom-call | tf_op jit(solution)/shard_map/pack/pallas_call | solution.py:161
  12.7 13.2 %all-to-all-start = ((bf16[64,40,128]{2,1,0:T(8,128)(2,1)}), bf16[64,40,128]{2,1,0:T(8,128)(2,1)S(1)}, u32[]{:S(2)}, u32[]{:S(2)}) async-start(bf16[64,40,128]{2,1,0:T(8,128)(2,1)} %bitcast.48), calls=%async_computation | async-start | bytes 1310720 | tf_op jit(solution)/shard_map/all_to_all | solution.py:567
  25.9 0.7 slice_bitcast_fusion.2.start_ref
  26.6 5.9 %own_head.1 = (bf16[4,256,512]{2,1,0:T(8,128)(2,1)}, f32[4,256,128]{2,1,0:T(8,128)}, bf16[4,256,128]{2,1,0:T(8,128)(2,1)}) custom-call(s32[4]{0:T(128)} %slice_bitcast_fusion.2.start_ref, bf16[6144,512]{1,0:T(8,128)(2,1)} %tokens_ref.3, bf16[6144,512]{1,0:T(8,128)(2,1)} %tokens_ref.3, bf16[512,512]{1,0:T(8,128)(2,1)} %refs_3_.3), custom_call_target="tpu_custom_call" | custom-call | flops 17179869184 | bytes 4194304 | tf_op jit(solution)/shard_map/own_head/pallas_call | solution.py:101
  32.5 0.1 constant_dynamic-slice_fusion.4
  32.5 0.5 collective-permute-start.3
  33.0 0.1 collective-permute-start.4
  33.2 0.4 collective-permute-start.5
  33.6 0.6 pad_add_fusion.pos_ref.refs_1_
  34.2 0.6 slice_bitcast_fusion.1.len_ref
  34.9 0.1 collective-permute-done.5.rest_5_.refs_9_
  35.0 9.2 %layer.1 = (bf16[2,32,12,8,128]{4,3,2,1,0:T(8,128)(2,1)}, bf16[4,1,512]{2,1,0:T(2,128)(2,1)}) custom-call(s32[4]{0:T(128)} %slice_bitcast_fusion.2.start_ref, s32[4]{0:T(128)} %slice_bitcast_fusion.1.len_ref, s32[2]{0:T(128)} %pad_add_fusion.pos_ref.refs_1_, bf16[6144,512]{1,0:T(8,128)(2,1)} %tokens_ref.3, bf16[4,256,512]{2,1,0:T(8,128)(2,1)} %get-tuple-element.12.half_hbm, ...), custom_call_target="tpu_custom_call" | custom-call | tf_op jit(solution)/shard_map/layer/pallas_call | solution.py:306
  44.3 2.0 %all-to-all-done = bf16[64,40,128]{2,1,0:T(8,128)(2,1)S(1)} async-done(((bf16[64,40,128]{2,1,0:T(8,128)(2,1)}), bf16[64,40,128]{2,1,0:T(8,128)(2,1)S(1)}, u32[]{:S(2)}, u32[]{:S(2)}) %all-to-all-start) | async-done | bytes 655392 | tf_op jit(solution)/shard_map/all_to_all | solution.py:567
  46.3 2.1 %merge.1 = bf16[64,12,8,128]{3,2,1,0:T(8,128)(2,1)} custom-call(s32[1]{0:T(128)} %bitcast.7.first_ref, bf16[64,5,8,128]{3,2,1,0:T(8,128)(2,1)S(1)} %bitcast.44, bf16[64,12,8,128]{3,2,1,0:T(8,128)(2,1)} %bitcast.46), custom_call_target="tpu_custom_call", output_to_operand_aliasing={{}: (2, {})} | custom-call | tf_op jit(solution)/shard_map/merge/pallas_call | solution.py:424
  48.4 8.3 %all-to-all-start.1 = ((bf16[64,96,128]{2,1,0:T(8,128)(2,1)}), bf16[64,96,128]{2,1,0:T(8,128)(2,1)S(1)}, u32[]{:S(2)}, u32[]{:S(2)}) async-start(bf16[64,96,128]{2,1,0:T(8,128)(2,1)} %bitcast.47), calls=%async_computation.1 | async-start | bytes 3145728 | tf_op jit(solution)/shard_map/all_to_all | solution.py:577
  56.7 0.9 slice_convert_fusion
  57.6 0.1 fusion
  57.7 0.1 constant_dynamic-slice_fusion.5
  57.8 0.1 slice.52
  57.9 0.1 copy.11
  58.0 0.7 reshape.50.to_ref
  58.6 37.1 %all-to-all-done.1 = bf16[64,96,128]{2,1,0:T(8,128)(2,1)S(1)} async-done(((bf16[64,96,128]{2,1,0:T(8,128)(2,1)}), bf16[64,96,128]{2,1,0:T(8,128)(2,1)S(1)}, u32[]{:S(2)}, u32[]{:S(2)}) %all-to-all-start.1) | async-done | bytes 1572896 | tf_op jit(solution)/shard_map/all_to_all | solution.py:577
  95.7 1.9 %regroup.1 = bf16[64,4,2,8,128]{4,3,2,1,0:T(8,128)(2,1)} custom-call(s32[128]{0:T(128)} %reshape.50.to_ref, bf16[64,12,8,128]{3,2,1,0:T(8,128)(2,1)S(1)} %bitcast.41), custom_call_target="tpu_custom_call" | custom-call | tf_op jit(solution)/shard_map/regroup/pallas_call | solution.py:457
  97.7 6.7 %all-to-all-start.2 = ((bf16[256,16,128]{2,1,0:T(8,128)(2,1)}), bf16[256,16,128]{2,1,0:T(8,128)(2,1)S(1)}, u32[]{:S(2)}, u32[]{:S(2)}) async-start(bf16[256,16,128]{2,1,0:T(8,128)(2,1)} %bitcast.50), calls=%async_computation.2 | async-start | bytes 2097152 | tf_op jit(solution)/shard_map/all_to_all | solution.py:594
  104.5 0.6 slice_bitcast_fusion.refs_0_
  105.0 7.9 %shard_map.87 = (bf16[2,32,8,128]{3,2,1,0:T(8,128)(2,1)}, bf16[2,32,8,128]{3,2,1,0:T(8,128)(2,1)}, bf16[2,32,8,128]{3,2,1,0:T(8,128)(2,1)}, bf16[2,32,8,128]{3,2,1,0:T(8,128)(2,1)}, bf16[2,1,512]{2,1,0:T(2,128)(2,1)}) custom-call(s32[2]{0:T(128)} %slice_bitcast_fusion.refs_0_, s32[2]{0:T(128)} %pad_add_fusion.pos_ref.refs_1_, ...), custom_call_target="tpu_custom_call" | custom-call | tf_op jit(solution)/shard_map/pallas_call | solution.py:383
  112.9 0.7 maximum_reduce_fusion
  113.7 1.4 %collective-permute-start.9 = (bf16[6,128]{1,0:T(8,128)(2,1)S(1)}, bf16[6,128]{1,0:T(8,128)(2,1)S(1)}, u32[]{:S(2)}, u32[]{:S(2)}) collective-permute-start(bf16[6,128]{1,0:T(8,128)(2,1)S(1)} %bitcast.56), channel_id=1, source_target_pairs={{0,1},{1,2},{2,3},{3,0},{4,5},{5,6},{6,7},{7,4},{8,9},{9,10},{10,1... | collective-permute-start | bytes 4616 | tf_op jit(solution)/shard_map/ppermute | solution.py:544
  115.2 2.4 %collective-permute-start.10 = (bf16[6,128]{1,0:T(8,128)(2,1)S(1)}, bf16[6,128]{1,0:T(8,128)(2,1)S(1)}, u32[]{:S(2)}, u32[]{:S(2)}) collective-permute-start(bf16[6,128]{1,0:T(8,128)(2,1)S(1)} %bitcast.55), channel_id=1, source_target_pairs={{0,2},{1,3},{2,0},{3,1},{4,6},{5,7},{6,4},{7,5},{8,10},{9,11},{10,... | collective-permute-start | bytes 4616 | tf_op jit(solution)/shard_map/ppermute | solution.py:544
  117.6 1.2 collective-permute-start.11
  118.8 0.6 collective-permute-done.10
  119.4 0.6 dynamic_slice.27.refs_0_
  120.1 7.9 %shard_map.86 = (bf16[2,32,8,128]{3,2,1,0:T(8,128)(2,1)}, bf16[2,32,8,128]{3,2,1,0:T(8,128)(2,1)}, bf16[2,32,8,128]{3,2,1,0:T(8,128)(2,1)}, bf16[2,32,8,128]{3,2,1,0:T(8,128)(2,1)}, bf16[2,1,512]{2,1,0:T(2,128)(2,1)}) custom-call(s32[2]{0:T(128)} %dynamic_slice.27.refs_0_, s32[2]{0:T(128)} %pad_add_fusion.pos_ref.refs_1_, bf16[64,12,8,128]{3,2,1,0:T(8,128)(2,1)} %bitcast.42, ...), custom_call_target="tpu_custom_call" | custom-call | tf_op jit(solution)/shard_map/pallas_call | solution.py:383
  128.0 1.3 collective-permute-start.6
  129.2 1.3 collective-permute-start.7
  130.6 2.0 %collective-permute-start.8 = (bf16[2,32,8,128]{3,2,1,0:T(8,128)(2,1)}, bf16[2,32,8,128]{3,2,1,0:T(8,128)(2,1)S(1)}, u32[]{:S(2)}, u32[]{:S(2)}) collective-permute-start(bf16[2,32,8,128]{3,2,1,0:T(8,128)(2,1)} %get-tuple-element.19), channel_id=1, source_target_pairs={{0,3},{1,0},{2,1},{3,2},{4,7},{5,4},{6,5},{7,6},{8,11},{9,8},{10,9... | collective-permute-start | bytes 393224 | tf_op jit(solution)/shard_map/ppermute | solution.py:544
  132.5 0.6 reshape.59
  133.1 2.2 %collective-permute-done.6.rest_1_ = bf16[2,32,8,128]{3,2,1,0:T(8,128)(2,1)S(1)} collective-permute-done((bf16[2,32,8,128]{3,2,1,0:T(8,128)(2,1)}, bf16[2,32,8,128]{3,2,1,0:T(8,128)(2,1)S(1)}, u32[]{:S(2)}, u32[]{:S(2)}) %collective-permute-start.6) | collective-permute-done | bytes 131104 | tf_op jit(solution)/shard_map/ppermute | solution.py:544
  135.4 0.3 collective-permute-done.8.rest_3_
  135.7 0.9 copy-done.9
  136.6 1.7 %place.1 = bf16[768,8,128]{2,1,0:T(8,128)(2,1)} custom-call(s32[24]{0:T(128)S(1)} %get-tuple-element.23.len_ref, s32[24]{0:T(128)S(1)} %get-tuple-element.22.off_ref, s32[2]{0:T(128)S(1)} %copy-done.10, bf16[2,32,4,2,8,128]{5,4,3,2,1,0:T(8,128)(2,1)S(1)} %bitcast.43, bf16[2,32,8,128]{3,2,1,0:T(8,128)(2,1)S(1)} %copy-done.9, ...), custom_call_target="tpu_custom_call" | custom-call | tf_op jit(solution)/shard_map/place/pallas_call | solution.py:524
  (45 shorter events, 0.2 us)
Async XLA Ops:
  0.6 6.8 %copy-start = (s32[1,24]{1,0:T(1,128)S(1)}, s32[1,24]{1,0:T(1,128)}, u32[]{:S(2)}) copy-start(s32[1,24]{1,0:T(1,128)} %param.13) | copy-start | bytes 292
  1.7 30.8 %collective-permute-start = (bf16[256,512]{1,0:T(8,128)(2,1)S(1)}, bf16[256,512]{1,0:T(8,128)(2,1)S(1)}, u32[]{:S(2)}, u32[]{:S(2)}) collective-permute-start(bf16[256,512]{1,0:T(8,128)(2,1)S(1)} %slice_select_fusion), channel_id=1, source_target_pairs={{0,1},{1,2},{2,3},{3,0},{4,5},{5,6},{6,7},{7,4},{8,9},{9,10},{10,1... | collective-permute-start | bytes 786440 | tf_op jit(solution)/shard_map/ppermute | solution.py:544
  3.8 29.2 %collective-permute-start.1 = (bf16[256,512]{1,0:T(8,128)(2,1)S(1)}, bf16[256,512]{1,0:T(8,128)(2,1)S(1)}, u32[]{:S(2)}, u32[]{:S(2)}) collective-permute-start(bf16[256,512]{1,0:T(8,128)(2,1)S(1)} %slice_select_fusion), channel_id=1, source_target_pairs={{0,2},{1,3},{2,0},{3,1},{4,6},{5,7},{6,4},{7,5},{8,10},{9,11},{10,... | collective-permute-start | bytes 786440 | tf_op jit(solution)/shard_map/ppermute | solution.py:544
  6.3 26.9 %collective-permute-start.2 = (bf16[256,512]{1,0:T(8,128)(2,1)S(1)}, bf16[256,512]{1,0:T(8,128)(2,1)S(1)}, u32[]{:S(2)}, u32[]{:S(2)}) collective-permute-start(bf16[256,512]{1,0:T(8,128)(2,1)S(1)} %slice_select_fusion), channel_id=1, source_target_pairs={{0,3},{1,0},{2,1},{3,2},{4,7},{5,4},{6,5},{7,6},{8,11},{9,8},{10,9... | collective-permute-start | bytes 786440 | tf_op jit(solution)/shard_map/ppermute | solution.py:544
  12.7 33.5 %all-to-all-start = ((bf16[64,40,128]{2,1,0:T(8,128)(2,1)}), bf16[64,40,128]{2,1,0:T(8,128)(2,1)S(1)}, u32[]{:S(2)}, u32[]{:S(2)}) async-start(bf16[64,40,128]{2,1,0:T(8,128)(2,1)} %bitcast.48), calls=%async_computation | async-start | bytes 1310720 | tf_op jit(solution)/shard_map/all_to_all | solution.py:567
  26.6 5.9 %copy-start.12 = (s32[1,24]{1,0:T(1,128)S(1)}, s32[1,24]{1,0:T(1,128)}, u32[]{:S(2)}) copy-start(s32[1,24]{1,0:T(1,128)} %param.10) | copy-start | bytes 292
  32.5 11.7 %copy-start.3 = (bf16[256,512]{1,0:T(8,128)(2,1)}, bf16[256,512]{1,0:T(8,128)(2,1)S(1)}, u32[]{:S(2)}) copy-start(bf16[256,512]{1,0:T(8,128)(2,1)S(1)} %collective-permute-done.rest_0_.refs_4_) | copy-start | bytes 786436
  32.5 2.3 %collective-permute-start.3 = (bf16[256,512]{1,0:T(8,128)(2,1)S(1)}, bf16[256,512]{1,0:T(8,128)(2,1)S(1)}, u32[]{:S(2)}, u32[]{:S(2)}) collective-permute-start(bf16[256,512]{1,0:T(8,128)(2,1)S(1)} %collective-permute-done.rest_0_.refs_4_), channel_id=1, source_target_pairs={{0,4},{4,0},{8,12},{12,8},{16,20},{20,16},{24,28},{28,24},{32,36},... | collective-permute-start | bytes 786440 | tf_op jit(solution)/shard_map/ppermute | solution.py:564
  33.0 11.2 %copy-start.4 = (bf16[256,512]{1,0:T(8,128)(2,1)}, bf16[256,512]{1,0:T(8,128)(2,1)S(1)}, u32[]{:S(2)}) copy-start(bf16[256,512]{1,0:T(8,128)(2,1)S(1)} %collective-permute-done.1.rest_1_.refs_5_) | copy-start | bytes 786436
  33.0 1.8 %collective-permute-start.4 = (bf16[256,512]{1,0:T(8,128)(2,1)S(1)}, bf16[256,512]{1,0:T(8,128)(2,1)S(1)}, u32[]{:S(2)}, u32[]{:S(2)}) collective-permute-start(bf16[256,512]{1,0:T(8,128)(2,1)S(1)} %collective-permute-done.1.rest_1_.refs_5_), channel_id=1, source_target_pairs={{0,4},{4,0},{8,12},{12,8},{16,20},{20,16},{24,28},{28,24},{32,36},... | collective-permute-start | bytes 786440 | tf_op jit(solution)/shard_map/ppermute | solution.py:564
  33.2 11.1 %copy-start.5 = (bf16[256,512]{1,0:T(8,128)(2,1)}, bf16[256,512]{1,0:T(8,128)(2,1)S(1)}, u32[]{:S(2)}) copy-start(bf16[256,512]{1,0:T(8,128)(2,1)S(1)} %collective-permute-done.2.rest_2_.refs_6_) | copy-start | bytes 786436
  33.2 1.8 %collective-permute-start.5 = (bf16[256,512]{1,0:T(8,128)(2,1)S(1)}, bf16[256,512]{1,0:T(8,128)(2,1)S(1)}, u32[]{:S(2)}, u32[]{:S(2)}) collective-permute-start(bf16[256,512]{1,0:T(8,128)(2,1)S(1)} %collective-permute-done.2.rest_2_.refs_6_), channel_id=1, source_target_pairs={{0,4},{4,0},{8,12},{12,8},{16,20},{20,16},{24,28},{28,24},{32,36},... | collective-permute-start | bytes 786440 | tf_op jit(solution)/shard_map/ppermute | solution.py:564
  34.9 9.4 %copy-start.6 = (bf16[256,512]{1,0:T(8,128)(2,1)}, bf16[256,512]{1,0:T(8,128)(2,1)S(1)}, u32[]{:S(2)}) copy-start(bf16[256,512]{1,0:T(8,128)(2,1)S(1)} %collective-permute-done.3.rest_3_.refs_7_) | copy-start | bytes 786436
  34.9 9.4 %copy-start.7 = (bf16[256,512]{1,0:T(8,128)(2,1)}, bf16[256,512]{1,0:T(8,128)(2,1)S(1)}, u32[]{:S(2)}) copy-start(bf16[256,512]{1,0:T(8,128)(2,1)S(1)} %collective-permute-done.4.rest_4_.refs_8_) | copy-start | bytes 786436
  35.0 9.3 %copy-start.8 = (bf16[256,512]{1,0:T(8,128)(2,1)}, bf16[256,512]{1,0:T(8,128)(2,1)S(1)}, u32[]{:S(2)}) copy-start(bf16[256,512]{1,0:T(8,128)(2,1)S(1)} %collective-permute-done.5.rest_5_.refs_9_) | copy-start | bytes 786436
  46.3 2.1 %copy-start.2 = (bf16[64,40,128]{2,1,0:T(8,128)(2,1)}, bf16[64,40,128]{2,1,0:T(8,128)(2,1)S(1)}, u32[]{:S(2)}) copy-start(bf16[64,40,128]{2,1,0:T(8,128)(2,1)S(1)} %all-to-all-done) | copy-start | bytes 1966084
  48.4 47.3 %all-to-all-start.1 = ((bf16[64,96,128]{2,1,0:T(8,128)(2,1)}), bf16[64,96,128]{2,1,0:T(8,128)(2,1)S(1)}, u32[]{:S(2)}, u32[]{:S(2)}) async-start(bf16[64,96,128]{2,1,0:T(8,128)(2,1)} %bitcast.47), calls=%async_computation.1 | async-start | bytes 3145728 | tf_op jit(solution)/shard_map/all_to_all | solution.py:577
  95.7 1.9 %copy-start.1 = (bf16[64,96,128]{2,1,0:T(8,128)(2,1)}, bf16[64,96,128]{2,1,0:T(8,128)(2,1)S(1)}, u32[]{:S(2)}) copy-start(bf16[64,96,128]{2,1,0:T(8,128)(2,1)S(1)} %all-to-all-done.1) | copy-start | bytes 4718596
  97.7 38.0 %all-to-all-start.2 = ((bf16[256,16,128]{2,1,0:T(8,128)(2,1)}), bf16[256,16,128]{2,1,0:T(8,128)(2,1)S(1)}, u32[]{:S(2)}, u32[]{:S(2)}) async-start(bf16[256,16,128]{2,1,0:T(8,128)(2,1)} %bitcast.50), calls=%async_computation.2 | async-start | bytes 2097152 | tf_op jit(solution)/shard_map/all_to_all | solution.py:594
  105.0 7.9 %copy-start.11 = (bf16[4,1,512]{2,1,0:T(2,128)(2,1)S(1)}, bf16[4,1,512]{2,1,0:T(2,128)(2,1)}, u32[]{:S(2)}) copy-start(bf16[4,1,512]{2,1,0:T(2,128)(2,1)} %get-tuple-element.21) | copy-start | bytes 12292
  113.7 5.0 %collective-permute-start.9 = (bf16[6,128]{1,0:T(8,128)(2,1)S(1)}, bf16[6,128]{1,0:T(8,128)(2,1)S(1)}, u32[]{:S(2)}, u32[]{:S(2)}) collective-permute-start(bf16[6,128]{1,0:T(8,128)(2,1)S(1)} %bitcast.56), channel_id=1, source_target_pairs={{0,1},{1,2},{2,3},{3,0},{4,5},{5,6},{6,7},{7,4},{8,9},{9,10},{10,1... | collective-permute-start | bytes 4616 | tf_op jit(solution)/shard_map/ppermute | solution.py:544
  115.2 4.3 %collective-permute-start.10 = (bf16[6,128]{1,0:T(8,128)(2,1)S(1)}, bf16[6,128]{1,0:T(8,128)(2,1)S(1)}, u32[]{:S(2)}, u32[]{:S(2)}) collective-permute-start(bf16[6,128]{1,0:T(8,128)(2,1)S(1)} %bitcast.55), channel_id=1, source_target_pairs={{0,2},{1,3},{2,0},{3,1},{4,6},{5,7},{6,4},{7,5},{8,10},{9,11},{10,... | collective-permute-start | bytes 4616 | tf_op jit(solution)/shard_map/ppermute | solution.py:544
  117.6 15.0 %collective-permute-start.11 = (bf16[6,128]{1,0:T(8,128)(2,1)S(1)}, bf16[6,128]{1,0:T(8,128)(2,1)S(1)}, u32[]{:S(2)}, u32[]{:S(2)}) collective-permute-start(bf16[6,128]{1,0:T(8,128)(2,1)S(1)} %bitcast.54), channel_id=1, source_target_pairs={{0,3},{1,0},{2,1},{3,2},{4,7},{5,4},{6,5},{7,6},{8,11},{9,8},{10,9... | collective-permute-start | bytes 4616 | tf_op jit(solution)/shard_map/ppermute | solution.py:544
  120.1 15.6 %copy-start.10 = (s32[2]{0:T(128)S(1)}, s32[2]{0:T(128)}, u32[]{:S(2)}) copy-start(s32[2]{0:T(128)} %pad_add_fusion.pos_ref.refs_1_) | copy-start | bytes 28
  128.0 7.4 %collective-permute-start.6 = (bf16[2,32,8,128]{3,2,1,0:T(8,128)(2,1)}, bf16[2,32,8,128]{3,2,1,0:T(8,128)(2,1)S(1)}, u32[]{:S(2)}, u32[]{:S(2)}) collective-permute-start(bf16[2,32,8,128]{3,2,1,0:T(8,128)(2,1)} %get-tuple-element.17), channel_id=1, source_target_pairs={{0,1},{1,2},{2,3},{3,0},{4,5},{5,6},{6,7},{7,4},{8,9},{9,10},{10,1... | collective-permute-start | bytes 393224 | tf_op jit(solution)/shard_map/ppermute | solution.py:544
  129.2 6.2 %collective-permute-start.7 = (bf16[2,32,8,128]{3,2,1,0:T(8,128)(2,1)}, bf16[2,32,8,128]{3,2,1,0:T(8,128)(2,1)S(1)}, u32[]{:S(2)}, u32[]{:S(2)}) collective-permute-start(bf16[2,32,8,128]{3,2,1,0:T(8,128)(2,1)} %get-tuple-element.18), channel_id=1, source_target_pairs={{0,2},{1,3},{2,0},{3,1},{4,6},{5,7},{6,4},{7,5},{8,10},{9,11},{10,... | collective-permute-start | bytes 393224 | tf_op jit(solution)/shard_map/ppermute | solution.py:544
  130.6 5.1 %collective-permute-start.8 = (bf16[2,32,8,128]{3,2,1,0:T(8,128)(2,1)}, bf16[2,32,8,128]{3,2,1,0:T(8,128)(2,1)S(1)}, u32[]{:S(2)}, u32[]{:S(2)}) collective-permute-start(bf16[2,32,8,128]{3,2,1,0:T(8,128)(2,1)} %get-tuple-element.19), channel_id=1, source_target_pairs={{0,3},{1,0},{2,1},{3,2},{4,7},{5,4},{6,5},{7,6},{8,11},{9,8},{10,9... | collective-permute-start | bytes 393224 | tf_op jit(solution)/shard_map/ppermute | solution.py:544
  135.6 0.9 copy-start.9

commit v7 on v6

--- a/solution.py
+++ b/solution.py
@@ -22,6 +22,7 @@
 GROUPS = WIN // TILE
 HALVES = N_DP // GROUPS
 GROUP = 2
+OWN_GROUP = 2
 RAW_MSG = N_MP + 1
 ROUND = DONE // HALVES
 MSG = (ROUND + 1) * N_MP
@@ -70,6 +71,65 @@
     return mean, lax.rsqrt(var * (unit * unit) + EPS) * unit
 
 
+def token_copies(tokens_ref, block, x_ref, row, sem):
+    second = jnp.minimum(block + 1, BLK_DEV - 1)
+    return [
+        pltpu.make_async_copy(
+            tokens_ref.at[pl.ds(b * BLOCK, BLOCK)],
+            x_ref.at[pl.ds(row + j * BLOCK, BLOCK)],
+            sem.at[j],
+        )
+        for j, b in enumerate((block, second))
+    ]
+
+
+def norm_half(x):
+    mean, inv = norm_stats(
+        jnp.sum(x, axis=1, keepdims=True), jnp.sum(x * x, axis=1, keepdims=True)
+    )
+    return ((x - mean) * (inv * 0.5)).astype(BF16)
+
+
+def own_head_kernel(
+    start_ref, part_ref, tokens_ref, w_ref, half_ref, att_ref, gate_ref,
+    x_s, half_s, att_s, gate_s, sem_in, sem_out,
+):
+    def loads(i):
+        block = start_ref[0, part_ref[0] * MINE + RAW + i]
+        return token_copies(tokens_ref, block, x_s, i * WIN, sem_in.at[i])
+
+    def sends(step):
+        rows = pl.ds(step * OWN_GROUP * WIN, OWN_GROUP * WIN)
+        pairs = ((half_s, half_ref), (att_s, att_ref), (gate_s, gate_ref))
+        return [
+            pltpu.make_async_copy(a.at[rows], b.at[rows], sem_out.at[step, j])
+            for j, (a, b) in enumerate(pairs)
+        ]
+
+    for i in range(DONE):
+        for copy in loads(i):
+            copy.start()
+
+    def group(step, carry):
+        for j in range(OWN_GROUP):
+            for copy in loads(step * OWN_GROUP + j):
+                copy.wait()
+        rows = pl.ds(pl.multiple_of(step * OWN_GROUP * WIN, WIN), OWN_GROUP * WIN)
+        half = norm_half(x_s[rows, :].astype(F32))
+        half_s[rows, :] = half
+        u, v, q, k = project([half], [w_ref[...]])
+        gate_s[rows, :] = u
+        att_s[rows, :] = attend_users(OWN_GROUP, q, k, v)
+        for copy in sends(step):
+            copy.start()
+        return carry
+
+    lax.fori_loop(0, DONE // OWN_GROUP, group, 0)
+    for step in range(DONE // OWN_GROUP):
+        for copy in sends(step):
+            copy.wait()
+
+
 def in_vmem():
     return pl.BlockSpec(memory_space=pltpu.VMEM)
 
@@ -82,44 +142,28 @@
     return pltpu.with_memory_space_constraint(array, pltpu.VMEM)
 
 
-def own_head_kernel(start_ref, x0_ref, x1_ref, w_ref, half_ref, att_ref, gate_ref):
-    x = jnp.concatenate([x0_ref[...], x1_ref[...]], axis=0).astype(F32)
-    mean, inv = norm_stats(
-        jnp.sum(x, axis=1, keepdims=True), jnp.sum(x * x, axis=1, keepdims=True)
-    )
-    half = ((x - mean) * (inv * 0.5)).astype(BF16)
-    half_ref[0] = half
-    u, v, q, k = project([half], [w_ref[...]])
-    gate_ref[0] = u
-    att_ref[0] = attend(q, k, v)
-
-
-def own_head(tokens, starts, w_own):
-    def per_user(width):
-        return pl.BlockSpec((1, WIN, width), lambda i, s: (i, 0, 0))
-
+def own_head(tokens, starts, part, w_own):
+    kept = [((DONE * WIN, D), BF16), ((DONE * WIN, HEAD), F32), ((DONE * WIN, HEAD), BF16)]
     return pl.pallas_call(
         own_head_kernel,
         grid_spec=pltpu.PrefetchScalarGridSpec(
-            num_scalar_prefetch=1,
-            grid=(DONE,),
-            in_specs=[
-                pl.BlockSpec((BLOCK, D), lambda i, s: (s[i], 0)),
-                pl.BlockSpec((BLOCK, D), lambda i, s: (jnp.minimum(s[i] + 1, BLK_DEV - 1), 0)),
-                pl.BlockSpec((D, D), lambda i, s: (0, 0)),
+            num_scalar_prefetch=2,
+            grid=(1,),
+            in_specs=[in_hbm(), in_vmem()],
+            out_specs=[in_hbm()] * 3,
+            scratch_shapes=[pltpu.VMEM((DONE * WIN, D), BF16)]
+            + [pltpu.VMEM(*k) for k in kept]
+            + [
+                pltpu.SemaphoreType.DMA((DONE, MAXB)),
+                pltpu.SemaphoreType.DMA((DONE // OWN_GROUP, 3)),
             ],
-            out_specs=[per_user(D), per_user(HEAD), per_user(HEAD)],
-        ),
-        out_shape=[
-            jax.ShapeDtypeStruct((DONE, WIN, D), BF16),
-            jax.ShapeDtypeStruct((DONE, WIN, HEAD), F32),
-            jax.ShapeDtypeStruct((DONE, WIN, HEAD), BF16),
-        ],
+        ),
+        out_shape=[jax.ShapeDtypeStruct(*k) for k in kept],
         cost_estimate=pl.CostEstimate(
             flops=DONE * WIN * D * D * 64, bytes_accessed=DONE * WIN * D * 8, transcendentals=0
         ),
         name="own_head",
-    )(starts, tokens, tokens, w_own)
+    )(starts, part, tokens, w_own)
 
 
 def rows_of(tiles):
@@ -128,48 +172,48 @@
     )
 
 
-def table_tile(table_ref):
-    tile = jnp.broadcast_to(table_ref[...], (TILE, 128)).astype(F32).astype(BF16)
-    return jnp.broadcast_to(tile[None], (GROUPS, TILE, 128))
-
-
-def pack_kernel(start_ref, tokens_ref, table_ref, out_ref, x_s, sem):
+def pack_kernel(
+    start_ref, part_ref, tokens_ref, owner_ref, len_ref, off_ref, out_ref, x_s, row_s, sem
+):
     copies = []
     for k in range(RAW):
-        first = start_ref[k]
-        second = jnp.minimum(first + 1, BLK_DEV - 1)
-        for j, block in enumerate((first, second)):
-            copy = pltpu.make_async_copy(
-                tokens_ref.at[pl.ds(block * BLOCK, BLOCK)],
-                x_s.at[k, pl.ds(j * BLOCK, BLOCK)],
-                sem.at[k, j],
-            )
-            copy.start()
-            copies.append(copy)
-    tile = table_tile(table_ref)
+        block = start_ref[0, part_ref[0] * MINE + k]
+        copies += token_copies(tokens_ref, block, x_s, k * WIN, sem.at[k])
+    for copy in copies:
+        copy.start()
+    row_s[...] = jnp.zeros_like(row_s)
+    for j, ref in enumerate((owner_ref, len_ref, off_ref)):
+        row_s[:, j * USERS : (j + 1) * USERS] = ref[...]
+    tile = jnp.broadcast_to(row_s[...], (TILE, 128)).astype(F32).astype(BF16)
     for k in range(RAW):
-        out_ref[k, :, N_MP] = tile
+        out_ref[k, :, N_MP] = jnp.broadcast_to(tile[None], (GROUPS, TILE, 128))
     for copy in copies:
         copy.wait()
     for k in range(RAW):
         for q in range(N_MP):
-            out_ref[k, :, q] = x_s[k, :, q * HEAD : (q + 1) * HEAD].reshape(GROUPS, TILE, HEAD)
-
-
-def pack(tokens, starts, table):
+            out_ref[k, :, q] = x_s[k * WIN : (k + 1) * WIN, q * HEAD : (q + 1) * HEAD].reshape(
+                GROUPS, TILE, HEAD
+            )
+
+
+def pack(tokens, starts, part, owner, hist_len, recv_offset):
     shape = (RAW, GROUPS, RAW_MSG, TILE, HEAD)
     return pl.pallas_call(
         pack_kernel,
         grid_spec=pltpu.PrefetchScalarGridSpec(
-            num_scalar_prefetch=1,
+            num_scalar_prefetch=2,
             grid=(1,),
-            in_specs=[in_hbm(), in_vmem()],
-            out_specs=pl.BlockSpec(shape, lambda i, s: (0, 0, 0, 0, 0)),
-            scratch_shapes=[pltpu.VMEM((RAW, WIN, D), BF16), pltpu.SemaphoreType.DMA((RAW, MAXB))],
+            in_specs=[in_hbm()] + [in_vmem()] * 3,
+            out_specs=pl.BlockSpec(shape, lambda i, *_: (0, 0, 0, 0, 0)),
+            scratch_shapes=[
+                pltpu.VMEM((RAW * WIN, D), BF16),
+                pltpu.VMEM((1, 128), jnp.int32),
+                pltpu.SemaphoreType.DMA((RAW, MAXB)),
+            ],
         ),
         out_shape=jax.ShapeDtypeStruct(shape, BF16),
         name="pack",
-    )(starts, tokens, table)
+    )(starts, part, tokens, owner, hist_len, recv_offset)
 
 
 def head_order(part):
@@ -224,25 +268,24 @@
     ]
 
 
-def layer_kernel(start_ref, len_ref, pos_ref, tokens_ref, half_hbm, att_hbm, gate_hbm, *rest):
+def layer_kernel(
+    start_ref, len_ref, part_ref, core_ref, tokens_ref, half_hbm, att_hbm, gate_hbm, *rest
+):
     near, far = rest[: HEADS - 1], rest[HEADS - 1 : 2 * HEADS - 2]
     w_out_ref, out_ref, state_ref = rest[2 * HEADS - 2 : 2 * HEADS + 1]
     x_s, half_s, att_s, gate_s, w_out_s, out_s, sem_in, sem_w, sem_out = rest[2 * HEADS + 1 :]
-    low_is_near = pos_ref[1] == 0
+    low_is_near = core_ref[0] == 0
+    first_id = part_ref[0] * MINE + RAW
 
     def loads(i):
-        first = start_ref[i]
-        second = jnp.minimum(first + 1, BLK_DEV - 1)
-        pairs = [
-            (half_hbm.at[i], half_s.at[pl.ds(i * WIN, WIN)]),
-            (att_hbm.at[i], att_s.at[pl.ds(i * WIN, WIN)]),
-            (gate_hbm.at[i], gate_s.at[pl.ds(i * WIN, WIN)]),
-            (tokens_ref.at[pl.ds(first * BLOCK, BLOCK)], x_s.at[pl.ds(i * WIN, BLOCK)]),
-            (tokens_ref.at[pl.ds(second * BLOCK, BLOCK)], x_s.at[pl.ds(i * WIN + BLOCK, BLOCK)]),
-        ]
-        return [pltpu.make_async_copy(a, b, sem_in.at[i, j]) for j, (a, b) in enumerate(pairs)]
-
-    weights = w_out_copies(pos_ref[0], w_out_ref, w_out_s, sem_w)
+        rows = pl.ds(i * WIN, WIN)
+        pairs = ((half_hbm, half_s), (att_hbm, att_s), (gate_hbm, gate_s))
+        return [
+            pltpu.make_async_copy(a.at[rows], b.at[rows], sem_in.at[i, MAXB + j])
+            for j, (a, b) in enumerate(pairs)
+        ] + token_copies(tokens_ref, start_ref[0, first_id + i], x_s, i * WIN, sem_in.at[i])
+
+    weights = w_out_copies(part_ref[0], w_out_ref, w_out_s, sem_w)
 
     def sends(i):
         at = (i % HALVES, slice(None), pl.ds((i // HALVES) * N_MP, N_MP))
@@ -281,7 +324,7 @@
         )
         for j in range(GROUP):
             i = first_user + j
-            length = len_ref[i]
+            length = len_ref[0, first_id + i]
             half_id = i % HALVES
             base = (i // HALVES) * N_MP
             mixed = live_rows(both[j * WIN : (j + 1) * WIN], length)
@@ -301,12 +344,12 @@
         sends(i).wait()
 
 
-def layer(tokens, starts, lengths, position, kept, near, far, w_out):
+def layer(tokens, starts, lengths, part, core, kept, near, far, w_out):
     message = (HALVES, GROUPS, MSG, TILE, HEAD)
     return pl.pallas_call(
         layer_kernel,
         grid_spec=pltpu.PrefetchScalarGridSpec(
-            num_scalar_prefetch=3,
+            num_scalar_prefetch=4,
             grid=(1,),
             in_specs=[in_hbm()] * 4 + [in_vmem()] * (2 * HEADS - 2) + [in_hbm()],
             out_specs=[in_hbm(), in_vmem()],
@@ -327,15 +370,16 @@
             jax.ShapeDtypeStruct((DONE, 1, D), BF16),
         ],
         name="layer",
-    )(starts, lengths, position, tokens, *kept, *map(keep, near), *map(keep, far), w_out)
-
-
-def raw_kernel(first_tile, len_ref, pos_ref, src_ref, w_own_ref, *rest):
+    )(starts, lengths, part, core, tokens, *kept, *map(keep, near), *map(keep, far), w_out)
+
+
+def raw_kernel(first_tile, len_ref, part_ref, core_ref, src_ref, w_own_ref, *rest):
     near, far = rest[: HEADS - 1], rest[HEADS - 1 : 2 * HEADS - 2]
     w_out_ref = rest[2 * HEADS - 2]
     pieces = rest[2 * HEADS - 1 : 2 * HEADS - 1 + N_MP]
     state_ref, x_s, w_out_s, mixed_s, sem_x, sem_w = rest[2 * HEADS - 1 + N_MP :]
-    part = pos_ref[0]
+    part = part_ref[0]
+    lengths = [len_ref[0, part * MINE + k] for k in range(RAW)]
     loads = [
         pltpu.make_async_copy(
             src_ref.at[pl.ds(k * GROUPS, GROUPS), pl.ds(first_tile, N_MP)], x_s.at[k], sem_x.at[k]
@@ -351,11 +395,7 @@
     def x_rows():
         return rows_of(x_s[...])
 
-    x = x_rows().astype(F32)
-    mean, inv = norm_stats(
-        jnp.sum(x, axis=1, keepdims=True), jnp.sum(x * x, axis=1, keepdims=True)
-    )
-    half = ((x - mean) * (inv * 0.5)).astype(BF16)
+    half = norm_half(x_rows().astype(F32))
     u, v, q, k = project([half], [w_own_ref[...]])
 
     def w_out_of():
@@ -364,26 +404,26 @@
         return w_out_s[...]
 
     both = mix(
-        pos_ref[1] == 0, half, (attend_users(RAW, q, k, v), u), near, far, w_out_of, x_rows
+        core_ref[0] == 0, half, (attend_users(RAW, q, k, v), u), near, far, w_out_of, x_rows
     )
     for k in range(RAW):
-        mixed = live_rows(both[k * WIN : (k + 1) * WIN], len_ref[k])
+        mixed = live_rows(both[k * WIN : (k + 1) * WIN], lengths[k])
         for q in range(N_MP):
             mixed_s[q, k] = mixed[:, q * HEAD : (q + 1) * HEAD].reshape(GROUPS, TILE, HEAD)
         for q in range(N_MP):
             state_ref[k, :, q * HEAD : (q + 1) * HEAD] = last_row(
-                mixed_s[q, k, (len_ref[k] - 1) // TILE], len_ref[k]
+                mixed_s[q, k, (lengths[k] - 1) // TILE], lengths[k]
             )
     for s in range(N_MP):
         pieces[s][...] = mixed_s[(part + s) % N_MP]
 
 
-def raw_layer(source, first_tile, lengths, position, w_own, near, far, w_out):
+def raw_layer(source, first_tile, lengths, part, core, w_own, near, far, w_out):
     piece = jax.ShapeDtypeStruct((RAW, GROUPS, TILE, HEAD), BF16)
     outs = pl.pallas_call(
         lambda *refs: raw_kernel(first_tile, *refs),
         grid_spec=pltpu.PrefetchScalarGridSpec(
-            num_scalar_prefetch=2,
+            num_scalar_prefetch=3,
             grid=(1,),
             in_specs=[in_hbm()] + [in_vmem()] * (2 * HEADS - 1) + [in_hbm()],
             out_specs=[in_vmem()] * (N_MP + 1),
@@ -396,7 +436,7 @@
             ],
         ),
         out_shape=[piece] * N_MP + [jax.ShapeDtypeStruct((RAW, 1, D), BF16)],
-    )(lengths, position, source, w_own, *near, *far, w_out)
+    )(lengths, part, core, source, w_own, *near, *far, w_out)
     return outs[:N_MP], outs[N_MP]
 
 
@@ -467,9 +507,11 @@
     )(to, keep(spread))
 
 
-def place_kernel(len_ref, off_ref, pos_ref, in_ref, *rest):
-    pieces = rest[:N_MP]
-    out_ref, zero_v, used_s, sem = rest[N_MP:]
+def place_kernel(len_ref, off_ref, part_ref, in_ref, own_ref, *rest):
+    out_ref, zero_v, used_s, own_s, sem, sem_own = rest[N_MP - 1 :]
+    pieces = (own_s, *rest[: N_MP - 1])
+    load = pltpu.make_async_copy(own_ref, own_s, sem_own)
+    load.start()
     per_block = BLOCK // TILE
     zero_v[...] = jnp.zeros_like(zero_v)
 
@@ -495,10 +537,13 @@
         def _():
             block(1)
 
-    for s in range(N_MP):
-        m = (pos_ref[0] + N_MP - s) % N_MP
+    def send_piece(s):
+        m = (part_ref[0] + N_MP - s) % N_MP
         for k in range(RAW):
             send(m * MINE + k, lambda rows: pieces[s].at[k, rows])
+
+    for s in range(1, N_MP):
+        send_piece(s)
 
     def one(n, carry):
         m = n // DONE
@@ -507,6 +552,8 @@
         return carry
 
     lax.fori_loop(0, N_MP * DONE, one, 0)
+    load.wait()
+    send_piece(0)
 
     def fill(b, carry):
         @pl.when(used_s[b] == 0)
@@ -519,25 +566,27 @@
     pltpu.make_async_copy(out_ref, out_ref, sem).wait()
 
 
-def place(arrived, pieces, lengths, offsets, position):
+def place(arrived, pieces, lengths, offsets, part):
     rows = BLK_DEV * BLOCK
     return pl.pallas_call(
         place_kernel,
         grid_spec=pltpu.PrefetchScalarGridSpec(
             num_scalar_prefetch=3,
             grid=(1,),
-            in_specs=[in_vmem()] * (1 + N_MP),
+            in_specs=[in_vmem(), in_hbm()] + [in_vmem()] * (N_MP - 1),
             out_specs=in_hbm(),
             scratch_shapes=[
                 pltpu.VMEM((BLOCK // TILE, TILE, HEAD), BF16),
                 pltpu.SMEM((BLK_DEV,), jnp.int32),
+                pltpu.VMEM((RAW, GROUPS, TILE, HEAD), BF16),
+                pltpu.SemaphoreType.DMA,
                 pltpu.SemaphoreType.DMA,
             ],
         ),
         out_shape=jax.ShapeDtypeStruct((rows // TILE, TILE, HEAD), BF16),
         compiler_params=pltpu.CompilerParams(vmem_limit_bytes=32 * 1024 * 1024),
         name="place",
-    )(lengths, offsets, position, keep(arrived), *map(keep, pieces)).reshape(rows, HEAD)
+    )(lengths, offsets, part, keep(arrived), pieces[0], *map(keep, pieces[1:])).reshape(rows, HEAD)
 
 
 def along_mp(array, s):
@@ -550,11 +599,7 @@
     first = part * MINE
     core = me % 2
     half = me // GROUPS
-    position = jnp.stack([part, core])
-
-    starts = lax.dynamic_slice_in_dim(block_start[0], first, MINE, 0)
-    lengths = lax.dynamic_slice_in_dim(hist_len[0], first, MINE, 0)
-    table = jnp.concatenate([owner, hist_len, recv_offset, jnp.zeros((1, 56), jnp.int32)], axis=1)
+    part_1, core_1 = part[None], core[None]
 
     mine_rows = jnp.where(core == 0, w_uvqk[: D // 2], w_uvqk[D // 2 :])
     near, far = [], []
@@ -563,13 +608,13 @@
     for s in range(1, N_MP):
         far.append(lax.ppermute(near[s - 1], "dp", [(i, i ^ 1) for i in range(N_DP)]))
 
-    raw = pack(tokens, starts[:RAW], table)
+    raw = pack(tokens, block_start, part_1, owner, hist_len, recv_offset)
     raw_in = lax.all_to_all(
         raw.reshape(N_DP, RAW_MSG * TILE, HEAD), "dp", 0, 0, tiled=True
     ).reshape(N_DP, RAW_MSG, TILE, HEAD)
-    kept = own_head(tokens, starts[RAW:], w_uvqk)
+    kept = own_head(tokens, block_start, part_1, w_uvqk)
     message, last = layer(
-        tokens, starts[RAW:], lengths[RAW:], position, kept, near, far, w_out
+        tokens, block_start, hist_len, part_1, core_1, kept, near, far, w_out
     )
     message = merge(
         raw_in, (first + half)[None], message.reshape(N_DP, MSG, TILE, HEAD)
@@ -578,7 +623,7 @@
         message.reshape(N_DP, MSG * TILE, HEAD), "dp", 0, 0, tiled=True
     ).reshape(N_DP, MSG, TILE, HEAD)
     _, raw_last = raw_layer(
-        raw.reshape(N_DP, RAW_MSG, TILE, HEAD), 0, lengths[:RAW], position,
+        raw.reshape(N_DP, RAW_MSG, TILE, HEAD), 0, hist_len, part_1, core_1,
         w_uvqk, near, far, w_out,
     )
 
@@ -595,14 +640,13 @@
         sorted_rows.reshape(N_DP * N_MP, ROUND * TILE, HEAD), ("dp", "mp"), 0, 0, tiled=True
     )
     pieces, _ = raw_layer(
-        spread, ROUND * N_MP,
-        lax.dynamic_slice_in_dim(recv_len, first, RAW, 0), position,
+        spread, ROUND * N_MP, recv_len[None], part_1, core_1,
         w_uvqk, near, far, w_out,
     )
     pieces = [pieces[0]] + [along_mp(pieces[s], s) for s in range(1, N_MP)]
     packed = place(
         arrived.reshape(HALVES, GROUPS, N_MP, ROUND, TILE, HEAD),
-        pieces, recv_len, recv_off, position,
+        pieces, recv_len, recv_off, part_1,
     )
 
     columns = jnp.concatenate([raw_last, last], axis=0).reshape(MINE, N_MP, HEAD)

time: 141 us -> 136 us (0.965)
  local copies, waits for them, and re-layouts: 5.76 us -> 2.48 us
  waiting for transfers between devices: 42.3 us -> 44.9 us
  starting transfers between devices: 44.4 us -> 42 us
  other arithmetic: 4.83 us -> 3.33 us
    slice x4 -> x0, local copies, waits for them, and re-layouts: 2.4 us -> none  [the longest x1 0.67 us: per_device(): starts[RAW:]]
    all_to_all x1, starting transfers between devices: 8.26 us -> 5.94 us  [per_device(): lax.all_to_all(message.reshape(N_DP, MSG * TILE, HEAD), 'dp', 0, 0, tiled...]
    all_to_all x1, waiting for transfers between devices: 1.98 us -> 4.17 us  [per_device(): lax.all_to_all(raw.reshape(N_DP, RAW_MSG * TILE, HEAD), 'dp', 0, 0, tiled...]
  transfers between devices with their start and end apart: 15 -> 15, of which waited for: 6 -> 7; matrix products, arithmetic and copies ran while one was open for 6% -> 3% of each run, Pallas kernels for 25% -> 25%
where the time goes in v7:
time: 136 us; the launch traced here: 134 us
  waiting for transfers between devices  44.9 us (33%)
  starting transfers between devices  42 us (31%)
  Pallas kernels  40 us (29%)
  other arithmetic  3.33 us (2%)
  local copies, waits for them, and re-layouts  2.48 us (2%)
    all_to_all x1, waiting for transfers between devices, per_device(): lax.all_to_all(message.reshape(N_DP, MSG * TILE, HEAD), 'dp', 0, 0, tiled...  36.7 us
    pallas_call x2, Pallas kernels, raw_layer(): pl.pallas_call(lambda *refs: raw_kernel(first_tile, *refs), grid_spec=plt...  15.7 us
    ppermute x9, starting transfers between devices, along_mp(): return lax.ppermute(array, 'mp', [(i, (i + s) % N_MP) for i in range(N_MP)])  15.3 us
    all_to_all x1, starting transfers between devices, per_device(): lax.all_to_all(raw.reshape(N_DP, RAW_MSG * TILE, HEAD), 'dp', 0, 0, tiled...  13.2 us
    pallas_call x1, Pallas kernels, layer(): pl.pallas_call(layer_kernel, grid_spec=pltpu.PrefetchScalarGridSpec(num_s...  9.26 us
    all_to_all x1, starting transfers between devices, per_device(): lax.all_to_all(sorted_rows.reshape(N_DP * N_MP, ROUND * TILE, HEAD), ('dp...  6.54 us
    all_to_all x1, starting transfers between devices, per_device(): lax.all_to_all(message.reshape(N_DP, MSG * TILE, HEAD), 'dp', 0, 0, tiled...  5.94 us
    pallas_call x1, Pallas kernels, own_head(): pl.pallas_call(own_head_kernel, grid_spec=pltpu.PrefetchScalarGridSpec(nu...  5.67 us
  transfers between devices with their start and end apart: 15, of which 7 were waited for; matrix products, arithmetic and copies ran while one was open for 3% of the time, Pallas kernels for 25%

profile of v7, /device:TPU:1, one launch (start us, length us, event | category | flops | bytes accessed | tf_op | source)
XLA Modules:
  0.0 133.9 jit_solution(106404686814237525)
XLA Ops:
  0.6 1.1 slice_select_fusion
  1.7 2.1 %collective-permute-start = (bf16[256,512]{1,0:T(8,128)(2,1)S(1)}, bf16[256,512]{1,0:T(8,128)(2,1)S(1)}, u32[]{:S(2)}, u32[]{:S(2)}) collective-permute-start(bf16[256,512]{1,0:T(8,128)(2,1)S(1)} %slice_select_fusion), channel_id=1, source_target_pairs={{0,1},{1,2},{2,3},{3,0},{4,5},{5,6},{6,7},{7,4},{8,9},{9,10},{10,1... | collective-permute-start | bytes 786440 | tf_op jit(solution)/shard_map/ppermute | solution.py:593
  3.8 2.5 %collective-permute-start.1 = (bf16[256,512]{1,0:T(8,128)(2,1)S(1)}, bf16[256,512]{1,0:T(8,128)(2,1)S(1)}, u32[]{:S(2)}, u32[]{:S(2)}) collective-permute-start(bf16[256,512]{1,0:T(8,128)(2,1)S(1)} %slice_select_fusion), channel_id=1, source_target_pairs={{0,2},{1,3},{2,0},{3,1},{4,6},{5,7},{6,4},{7,5},{8,10},{9,11},{10,... | collective-permute-start | bytes 786440 | tf_op jit(solution)/shard_map/ppermute | solution.py:593
  6.3 1.2 collective-permute-start.2
  7.4 3.4 %pack.1 = bf16[2,32,5,8,128]{4,3,2,1,0:T(8,128)(2,1)} custom-call(s32[1,24]{1,0:T(1,128)} %start_ref.5, s32[1]{0:T(128)} %bitcast.part_ref.refs_1_, bf16[6144,512]{1,0:T(8,128)(2,1)} %tokens_ref.5, s32[1,24]{1,0:T(1,128)} %owner_ref.1, s32[1,24]{1,0:T(1,128)} %refs_0_.1, s32[1,24]{1,0:T(1,128)} %off_ref.1), custom_call_target="tpu_custom_call" | custom-call | tf_op jit(solution)/shard_map/pack/pallas_call | solution.py:201
  10.8 13.2 %all-to-all-start = ((bf16[64,40,128]{2,1,0:T(8,128)(2,1)}), bf16[64,40,128]{2,1,0:T(8,128)(2,1)S(1)}, u32[]{:S(2)}, u32[]{:S(2)}) async-start(bf16[64,40,128]{2,1,0:T(8,128)(2,1)} %bitcast.40), calls=%async_computation | async-start | bytes 1310720 | tf_op jit(solution)/shard_map/all_to_all | solution.py:612
  24.0 0.0 collective-permute-done.rest_0_.refs_5_
  24.0 0.5 collective-permute-start.3
  24.5 0.0 collective-permute-done.1.rest_1_.refs_6_
  24.5 0.1 collective-permute-start.4
  24.7 0.0 collective-permute-done.2.rest_2_.refs_7_
  24.7 0.4 collective-permute-start.5
  25.1 5.7 %own_head.1 = (bf16[1024,512]{1,0:T(8,128)(2,1)}, f32[1024,128]{1,0:T(8,128)}, bf16[1024,128]{1,0:T(8,128)(2,1)}) custom-call(s32[1,24]{1,0:T(1,128)} %start_ref.5, s32[1]{0:T(128)} %bitcast.part_ref.refs_1_, bf16[6144,512]{1,0:T(8,128)(2,1)} %tokens_ref.5, bf16[512,512]{1,0:T(8,128)(2,1)} %refs_4_.3), custom_call_target="tpu_custom_call" | custom-call | flops 17179869184 | bytes 4194304 | tf_op jit(solution)/shard_map/own_head/pallas_call | solution.py:147
  30.8 0.0 collective-permute-done.3.rest_3_.refs_8_
  30.8 0.0 collective-permute-done.4.rest_4_.refs_9_
  30.8 0.0 collective-permute-done.5.rest_5_.refs_10_
  30.9 9.3 %layer.1 = (bf16[2,32,12,8,128]{4,3,2,1,0:T(8,128)(2,1)}, bf16[4,1,512]{2,1,0:T(2,128)(2,1)}) custom-call(s32[1,24]{1,0:T(1,128)} %start_ref.5, s32[1,24]{1,0:T(1,128)} %refs_0_.1, s32[1]{0:T(128)} %bitcast.part_ref.refs_1_, s32[1]{0:T(128)} %bitcast.6.core_ref.refs_2_, bf16[6144,512]{1,0:T(8,128)(2,1)} %tokens_ref.5, ...), custom_call_target="tpu_custom_call" | custom-call | tf_op jit(solution)/shard_map/layer/pallas_call | solution.py:349
  40.2 4.2 %all-to-all-done = bf16[64,40,128]{2,1,0:T(8,128)(2,1)S(1)} async-done(((bf16[64,40,128]{2,1,0:T(8,128)(2,1)}), bf16[64,40,128]{2,1,0:T(8,128)(2,1)S(1)}, u32[]{:S(2)}, u32[]{:S(2)}) %all-to-all-start) | async-done | bytes 655392 | tf_op jit(solution)/shard_map/all_to_all | solution.py:612
  44.3 2.1 %merge.1 = bf16[64,12,8,128]{3,2,1,0:T(8,128)(2,1)} custom-call(s32[1]{0:T(128)} %bitcast.5.first_ref, bf16[64,5,8,128]{3,2,1,0:T(8,128)(2,1)S(1)} %bitcast.35, bf16[64,12,8,128]{3,2,1,0:T(8,128)(2,1)} %bitcast.38), custom_call_target="tpu_custom_call", output_to_operand_aliasing={{}: (2, {})} | custom-call | tf_op jit(solution)/shard_map/merge/pallas_call | solution.py:464
  46.5 5.9 %all-to-all-start.1 = ((bf16[64,96,128]{2,1,0:T(8,128)(2,1)}), bf16[64,96,128]{2,1,0:T(8,128)(2,1)S(1)}, u32[]{:S(2)}, u32[]{:S(2)}) async-start(bf16[64,96,128]{2,1,0:T(8,128)(2,1)} %bitcast.39), calls=%async_computation.1 | async-start | bytes 3145728 | tf_op jit(solution)/shard_map/all_to_all | solution.py:622
  52.4 0.9 slice_convert_fusion
  53.4 0.6 fusion
  54.0 0.1 constant_dynamic-slice_fusion.4
  54.1 0.1 slice.25
  54.1 0.1 copy.11
  54.2 0.6 reshape.44.to_ref
  54.8 36.7 %all-to-all-done.1 = bf16[64,96,128]{2,1,0:T(8,128)(2,1)S(1)} async-done(((bf16[64,96,128]{2,1,0:T(8,128)(2,1)}), bf16[64,96,128]{2,1,0:T(8,128)(2,1)S(1)}, u32[]{:S(2)}, u32[]{:S(2)}) %all-to-all-start.1) | async-done | bytes 1572896 | tf_op jit(solution)/shard_map/all_to_all | solution.py:622
  91.5 1.9 %regroup.1 = bf16[64,4,2,8,128]{4,3,2,1,0:T(8,128)(2,1)} custom-call(s32[128]{0:T(128)} %reshape.44.to_ref, bf16[64,12,8,128]{3,2,1,0:T(8,128)(2,1)S(1)} %bitcast.32), custom_call_target="tpu_custom_call" | custom-call | tf_op jit(solution)/shard_map/regroup/pallas_call | solution.py:497
  93.4 6.5 %all-to-all-start.2 = ((bf16[256,16,128]{2,1,0:T(8,128)(2,1)}), bf16[256,16,128]{2,1,0:T(8,128)(2,1)S(1)}, u32[]{:S(2)}, u32[]{:S(2)}) async-start(bf16[256,16,128]{2,1,0:T(8,128)(2,1)} %bitcast.42), calls=%async_computation.2 | async-start | bytes 2097152 | tf_op jit(solution)/shard_map/all_to_all | solution.py:639
  100.1 7.8 %shard_map.87 = (bf16[2,32,8,128]{3,2,1,0:T(8,128)(2,1)}, bf16[2,32,8,128]{3,2,1,0:T(8,128)(2,1)}, bf16[2,32,8,128]{3,2,1,0:T(8,128)(2,1)}, bf16[2,32,8,128]{3,2,1,0:T(8,128)(2,1)}, bf16[2,1,512]{2,1,0:T(2,128)(2,1)}) custom-call(s32[1,24]{1,0:T(1,128)} %refs_0_.1, s32[1]{0:T(128)} %bitcast.part_ref.refs_1_, s32[1]{0:T(128)} %bitcast.6.core_ref.refs_2_, ...), custom_call_target="tpu_custom_call" | custom-call | tf_op jit(solution)/shard_map/pallas_call | solution.py:423
  107.9 0.7 maximum_reduce_fusion
  108.7 1.4 %collective-permute-start.9 = (bf16[6,128]{1,0:T(8,128)(2,1)S(1)}, bf16[6,128]{1,0:T(8,128)(2,1)S(1)}, u32[]{:S(2)}, u32[]{:S(2)}) collective-permute-start(bf16[6,128]{1,0:T(8,128)(2,1)S(1)} %bitcast.48), channel_id=1, source_target_pairs={{0,1},{1,2},{2,3},{3,0},{4,5},{5,6},{6,7},{7,4},{8,9},{9,10},{10,1... | collective-permute-start | bytes 4616 | tf_op jit(solution)/shard_map/ppermute | solution.py:593
  110.1 2.4 %collective-permute-start.10 = (bf16[6,128]{1,0:T(8,128)(2,1)S(1)}, bf16[6,128]{1,0:T(8,128)(2,1)S(1)}, u32[]{:S(2)}, u32[]{:S(2)}) collective-permute-start(bf16[6,128]{1,0:T(8,128)(2,1)S(1)} %bitcast.47), channel_id=1, source_target_pairs={{0,2},{1,3},{2,0},{3,1},{4,6},{5,7},{6,4},{7,5},{8,10},{9,11},{10,... | collective-permute-start | bytes 4616 | tf_op jit(solution)/shard_map/ppermute | solution.py:593
  112.6 1.2 collective-permute-start.11
  113.7 0.0 collective-permute-done.9
  113.8 0.6 collective-permute-done.10
  114.4 7.9 %shard_map.86 = (bf16[2,32,8,128]{3,2,1,0:T(8,128)(2,1)}, bf16[2,32,8,128]{3,2,1,0:T(8,128)(2,1)}, bf16[2,32,8,128]{3,2,1,0:T(8,128)(2,1)}, bf16[2,32,8,128]{3,2,1,0:T(8,128)(2,1)}, bf16[2,1,512]{2,1,0:T(2,128)(2,1)}) custom-call(s32[1,24]{1,0:T(1,128)} %bitcast.37, s32[1]{0:T(128)} %bitcast.part_ref.refs_1_, s32[1]{0:T(128)} %bitcast.6.core_ref.refs_2_, ...), custom_call_target="tpu_custom_call" | custom-call | tf_op jit(solution)/shard_map/pallas_call | solution.py:423
  122.4 1.3 collective-permute-start.6
  123.7 1.3 collective-permute-start.7
  125.0 1.9 %collective-permute-start.8 = (bf16[2,32,8,128]{3,2,1,0:T(8,128)(2,1)}, bf16[2,32,8,128]{3,2,1,0:T(8,128)(2,1)S(1)}, u32[]{:S(2)}, u32[]{:S(2)}) collective-permute-start(bf16[2,32,8,128]{3,2,1,0:T(8,128)(2,1)} %get-tuple-element.19), channel_id=1, source_target_pairs={{0,3},{1,0},{2,1},{3,2},{4,7},{5,4},{6,5},{7,6},{8,11},{9,8},{10,9... | collective-permute-start | bytes 393224 | tf_op jit(solution)/shard_map/ppermute | solution.py:593
  126.9 0.0 collective-permute-done.11
  126.9 0.6 reshape.53
  127.5 0.9 collective-permute-done.6.rest_0_
  128.5 1.5 %collective-permute-done.7.rest_1_ = bf16[2,32,8,128]{3,2,1,0:T(8,128)(2,1)S(1)} collective-permute-done((bf16[2,32,8,128]{3,2,1,0:T(8,128)(2,1)}, bf16[2,32,8,128]{3,2,1,0:T(8,128)(2,1)S(1)}, u32[]{:S(2)}, u32[]{:S(2)}) %collective-permute-start.7) | collective-permute-done | bytes 131104 | tf_op jit(solution)/shard_map/ppermute | solution.py:593
  130.0 0.1 collective-permute-done.8.rest_2_
  130.1 0.9 all-to-all-done.2
  131.0 0.9 copy-done.8
  131.9 1.9 %place.1 = bf16[768,8,128]{2,1,0:T(8,128)(2,1)} custom-call(s32[24]{0:T(128)S(1)} %copy-done.9, s32[24]{0:T(128)S(1)} %get-tuple-element.22.off_ref, s32[1]{0:T(128)} %bitcast.part_ref.refs_1_, bf16[2,32,4,2,8,128]{5,4,3,2,1,0:T(8,128)(2,1)S(1)} %bitcast.34, bf16[2,32,8,128]{3,2,1,0:T(8,128)(2,1)S(1)} %copy-done.8, ...), custom_call_target="tpu_custom_call" | custom-call | tf_op jit(solution)/shard_map/place/pallas_call | solution.py:571
  (31 shorter events, 0.1 us)
Async XLA Ops:
  1.7 22.3 %collective-permute-start = (bf16[256,512]{1,0:T(8,128)(2,1)S(1)}, bf16[256,512]{1,0:T(8,128)(2,1)S(1)}, u32[]{:S(2)}, u32[]{:S(2)}) collective-permute-start(bf16[256,512]{1,0:T(8,128)(2,1)S(1)} %slice_select_fusion), channel_id=1, source_target_pairs={{0,1},{1,2},{2,3},{3,0},{4,5},{5,6},{6,7},{7,4},{8,9},{9,10},{10,1... | collective-permute-start | bytes 786440 | tf_op jit(solution)/shard_map/ppermute | solution.py:593
  3.8 20.7 %collective-permute-start.1 = (bf16[256,512]{1,0:T(8,128)(2,1)S(1)}, bf16[256,512]{1,0:T(8,128)(2,1)S(1)}, u32[]{:S(2)}, u32[]{:S(2)}) collective-permute-start(bf16[256,512]{1,0:T(8,128)(2,1)S(1)} %slice_select_fusion), channel_id=1, source_target_pairs={{0,2},{1,3},{2,0},{3,1},{4,6},{5,7},{6,4},{7,5},{8,10},{9,11},{10,... | collective-permute-start | bytes 786440 | tf_op jit(solution)/shard_map/ppermute | solution.py:593
  6.3 18.4 %collective-permute-start.2 = (bf16[256,512]{1,0:T(8,128)(2,1)S(1)}, bf16[256,512]{1,0:T(8,128)(2,1)S(1)}, u32[]{:S(2)}, u32[]{:S(2)}) collective-permute-start(bf16[256,512]{1,0:T(8,128)(2,1)S(1)} %slice_select_fusion), channel_id=1, source_target_pairs={{0,3},{1,0},{2,1},{3,2},{4,7},{5,4},{6,5},{7,6},{8,11},{9,8},{10,9... | collective-permute-start | bytes 786440 | tf_op jit(solution)/shard_map/ppermute | solution.py:593
  10.8 33.5 %all-to-all-start = ((bf16[64,40,128]{2,1,0:T(8,128)(2,1)}), bf16[64,40,128]{2,1,0:T(8,128)(2,1)S(1)}, u32[]{:S(2)}, u32[]{:S(2)}) async-start(bf16[64,40,128]{2,1,0:T(8,128)(2,1)} %bitcast.40), calls=%async_computation | async-start | bytes 1310720 | tf_op jit(solution)/shard_map/all_to_all | solution.py:612
  24.0 6.8 %copy-start.2 = (bf16[256,512]{1,0:T(8,128)(2,1)}, bf16[256,512]{1,0:T(8,128)(2,1)S(1)}, u32[]{:S(2)}) copy-start(bf16[256,512]{1,0:T(8,128)(2,1)S(1)} %collective-permute-done.rest_0_.refs_5_) | copy-start | bytes 786436
  24.0 6.8 %collective-permute-start.3 = (bf16[256,512]{1,0:T(8,128)(2,1)S(1)}, bf16[256,512]{1,0:T(8,128)(2,1)S(1)}, u32[]{:S(2)}, u32[]{:S(2)}) collective-permute-start(bf16[256,512]{1,0:T(8,128)(2,1)S(1)} %collective-permute-done.rest_0_.refs_5_), channel_id=1, source_target_pairs={{0,4},{4,0},{8,12},{12,8},{16,20},{20,16},{24,28},{28,24},{32,36},... | collective-permute-start | bytes 786440 | tf_op jit(solution)/shard_map/ppermute | solution.py:609
  24.5 6.3 %copy-start.3 = (bf16[256,512]{1,0:T(8,128)(2,1)}, bf16[256,512]{1,0:T(8,128)(2,1)S(1)}, u32[]{:S(2)}) copy-start(bf16[256,512]{1,0:T(8,128)(2,1)S(1)} %collective-permute-done.1.rest_1_.refs_6_) | copy-start | bytes 786436
  24.5 6.2 %collective-permute-start.4 = (bf16[256,512]{1,0:T(8,128)(2,1)S(1)}, bf16[256,512]{1,0:T(8,128)(2,1)S(1)}, u32[]{:S(2)}, u32[]{:S(2)}) collective-permute-start(bf16[256,512]{1,0:T(8,128)(2,1)S(1)} %collective-permute-done.1.rest_1_.refs_6_), channel_id=1, source_target_pairs={{0,4},{4,0},{8,12},{12,8},{16,20},{20,16},{24,28},{28,24},{32,36},... | collective-permute-start | bytes 786440 | tf_op jit(solution)/shard_map/ppermute | solution.py:609
  24.7 6.2 %copy-start.4 = (bf16[256,512]{1,0:T(8,128)(2,1)}, bf16[256,512]{1,0:T(8,128)(2,1)S(1)}, u32[]{:S(2)}) copy-start(bf16[256,512]{1,0:T(8,128)(2,1)S(1)} %collective-permute-done.2.rest_2_.refs_7_) | copy-start | bytes 786436
  24.7 6.1 %collective-permute-start.5 = (bf16[256,512]{1,0:T(8,128)(2,1)S(1)}, bf16[256,512]{1,0:T(8,128)(2,1)S(1)}, u32[]{:S(2)}, u32[]{:S(2)}) collective-permute-start(bf16[256,512]{1,0:T(8,128)(2,1)S(1)} %collective-permute-done.2.rest_2_.refs_7_), channel_id=1, source_target_pairs={{0,4},{4,0},{8,12},{12,8},{16,20},{20,16},{24,28},{28,24},{32,36},... | collective-permute-start | bytes 786440 | tf_op jit(solution)/shard_map/ppermute | solution.py:609
  30.8 9.3 %copy-start.5 = (bf16[256,512]{1,0:T(8,128)(2,1)}, bf16[256,512]{1,0:T(8,128)(2,1)S(1)}, u32[]{:S(2)}) copy-start(bf16[256,512]{1,0:T(8,128)(2,1)S(1)} %collective-permute-done.3.rest_3_.refs_8_) | copy-start | bytes 786436
  30.8 9.3 %copy-start.6 = (bf16[256,512]{1,0:T(8,128)(2,1)}, bf16[256,512]{1,0:T(8,128)(2,1)S(1)}, u32[]{:S(2)}) copy-start(bf16[256,512]{1,0:T(8,128)(2,1)S(1)} %collective-permute-done.4.rest_4_.refs_9_) | copy-start | bytes 786436
  30.8 9.3 %copy-start.7 = (bf16[256,512]{1,0:T(8,128)(2,1)}, bf16[256,512]{1,0:T(8,128)(2,1)S(1)}, u32[]{:S(2)}) copy-start(bf16[256,512]{1,0:T(8,128)(2,1)S(1)} %collective-permute-done.5.rest_5_.refs_10_) | copy-start | bytes 786436
  44.3 2.1 %copy-start.1 = (bf16[64,40,128]{2,1,0:T(8,128)(2,1)}, bf16[64,40,128]{2,1,0:T(8,128)(2,1)S(1)}, u32[]{:S(2)}) copy-start(bf16[64,40,128]{2,1,0:T(8,128)(2,1)S(1)} %all-to-all-done) | copy-start | bytes 1966084
  46.5 45.0 %all-to-all-start.1 = ((bf16[64,96,128]{2,1,0:T(8,128)(2,1)}), bf16[64,96,128]{2,1,0:T(8,128)(2,1)S(1)}, u32[]{:S(2)}, u32[]{:S(2)}) async-start(bf16[64,96,128]{2,1,0:T(8,128)(2,1)} %bitcast.39), calls=%async_computation.1 | async-start | bytes 3145728 | tf_op jit(solution)/shard_map/all_to_all | solution.py:622
  91.5 1.9 %copy-start = (bf16[64,96,128]{2,1,0:T(8,128)(2,1)}, bf16[64,96,128]{2,1,0:T(8,128)(2,1)S(1)}, u32[]{:S(2)}) copy-start(bf16[64,96,128]{2,1,0:T(8,128)(2,1)S(1)} %all-to-all-done.1) | copy-start | bytes 4718596
  93.4 37.5 %all-to-all-start.2 = ((bf16[256,16,128]{2,1,0:T(8,128)(2,1)}), bf16[256,16,128]{2,1,0:T(8,128)(2,1)S(1)}, u32[]{:S(2)}, u32[]{:S(2)}) async-start(bf16[256,16,128]{2,1,0:T(8,128)(2,1)} %bitcast.42), calls=%async_computation.2 | async-start | bytes 2097152 | tf_op jit(solution)/shard_map/all_to_all | solution.py:639
  100.1 7.8 %copy-start.10 = (bf16[4,1,512]{2,1,0:T(2,128)(2,1)S(1)}, bf16[4,1,512]{2,1,0:T(2,128)(2,1)}, u32[]{:S(2)}) copy-start(bf16[4,1,512]{2,1,0:T(2,128)(2,1)} %get-tuple-element.21) | copy-start | bytes 12292
  108.7 5.1 %collective-permute-start.9 = (bf16[6,128]{1,0:T(8,128)(2,1)S(1)}, bf16[6,128]{1,0:T(8,128)(2,1)S(1)}, u32[]{:S(2)}, u32[]{:S(2)}) collective-permute-start(bf16[6,128]{1,0:T(8,128)(2,1)S(1)} %bitcast.48), channel_id=1, source_target_pairs={{0,1},{1,2},{2,3},{3,0},{4,5},{5,6},{6,7},{7,4},{8,9},{9,10},{10,1... | collective-permute-start | bytes 4616 | tf_op jit(solution)/shard_map/ppermute | solution.py:593
  110.1 4.2 %collective-permute-start.10 = (bf16[6,128]{1,0:T(8,128)(2,1)S(1)}, bf16[6,128]{1,0:T(8,128)(2,1)S(1)}, u32[]{:S(2)}, u32[]{:S(2)}) collective-permute-start(bf16[6,128]{1,0:T(8,128)(2,1)S(1)} %bitcast.47), channel_id=1, source_target_pairs={{0,2},{1,3},{2,0},{3,1},{4,6},{5,7},{6,4},{7,5},{8,10},{9,11},{10,... | collective-permute-start | bytes 4616 | tf_op jit(solution)/shard_map/ppermute | solution.py:593
  112.6 14.4 %collective-permute-start.11 = (bf16[6,128]{1,0:T(8,128)(2,1)S(1)}, bf16[6,128]{1,0:T(8,128)(2,1)S(1)}, u32[]{:S(2)}, u32[]{:S(2)}) collective-permute-start(bf16[6,128]{1,0:T(8,128)(2,1)S(1)} %bitcast.46), channel_id=1, source_target_pairs={{0,3},{1,0},{2,1},{3,2},{4,7},{5,4},{6,5},{7,6},{8,11},{9,8},{10,9... | collective-permute-start | bytes 4616 | tf_op jit(solution)/shard_map/ppermute | solution.py:593
  114.4 16.6 %copy-start.9 = (s32[24]{0:T(128)S(1)}, s32[24]{0:T(128)}, u32[]{:S(2)}) copy-start(s32[24]{0:T(128)} %get-tuple-element.23.len_ref) | copy-start | bytes 292
  122.4 6.1 %collective-permute-start.6 = (bf16[2,32,8,128]{3,2,1,0:T(8,128)(2,1)}, bf16[2,32,8,128]{3,2,1,0:T(8,128)(2,1)S(1)}, u32[]{:S(2)}, u32[]{:S(2)}) collective-permute-start(bf16[2,32,8,128]{3,2,1,0:T(8,128)(2,1)} %get-tuple-element.17), channel_id=1, source_target_pairs={{0,1},{1,2},{2,3},{3,0},{4,5},{5,6},{6,7},{7,4},{8,9},{9,10},{10,1... | collective-permute-start | bytes 393224 | tf_op jit(solution)/shard_map/ppermute | solution.py:593
  123.7 6.3 %collective-permute-start.7 = (bf16[2,32,8,128]{3,2,1,0:T(8,128)(2,1)}, bf16[2,32,8,128]{3,2,1,0:T(8,128)(2,1)S(1)}, u32[]{:S(2)}, u32[]{:S(2)}) collective-permute-start(bf16[2,32,8,128]{3,2,1,0:T(8,128)(2,1)} %get-tuple-element.18), channel_id=1, source_target_pairs={{0,2},{1,3},{2,0},{3,1},{4,6},{5,7},{6,4},{7,5},{8,10},{9,11},{10,... | collective-permute-start | bytes 393224 | tf_op jit(solution)/shard_map/ppermute | solution.py:593
  125.0 5.1 %collective-permute-start.8 = (bf16[2,32,8,128]{3,2,1,0:T(8,128)(2,1)}, bf16[2,32,8,128]{3,2,1,0:T(8,128)(2,1)S(1)}, u32[]{:S(2)}, u32[]{:S(2)}) collective-permute-start(bf16[2,32,8,128]{3,2,1,0:T(8,128)(2,1)} %get-tuple-element.19), channel_id=1, source_target_pairs={{0,3},{1,0},{2,1},{3,2},{4,7},{5,4},{6,5},{7,6},{8,11},{9,8},{10,9... | collective-permute-start | bytes 393224 | tf_op jit(solution)/shard_map/ppermute | solution.py:593
  131.0 0.9 copy-start.8
